TPU v7x, 32 devices: a whole 2x2x4 slice. The times are simulated.
32 devices in a mesh: pipe: 4 (over x, core), mp: 8 (over z, y).
Axes of the slice: x: 2, y: 2, z: 4, core: 2. Of those that a mesh axis runs over, the one named last changes fastest.
Arguments:
- hidden_in: bfloat16 [32, 8192], P(None, 'mp'), may hold values from -24000 to 24000
- lengths: int32 [32], replicated, may hold values from 1 to 256
- assign: int32 [32], replicated, may hold values from 0 to 31, each once
- token_ids: int32 [32], replicated, may hold values from 0 to 12287
- attn_gain: bfloat16 [4, 8192], P('pipe', 'mp'), may hold values from 0.099609375 to 1.8984375
- qkv_weight: bfloat16 [4, 8192, 5120], P('pipe', 'mp'), may hold values from -0.0625 to 0.0625
- qkv_bias: bfloat16 [4, 5120], P('pipe'), may hold values from -3 to 3
- out_weight: bfloat16 [4, 4096, 8192], P('pipe', None, 'mp'), may hold values from -0.375 to 0.375
- kv_cache: bfloat16 [4, 32, 2, 4, 256, 128], P('pipe', 'mp'), may hold values from -120 to 120
- final_gain: bfloat16 [8192], P('mp'), may hold values from 0.099609375 to 1.8984375
- head_weight: bfloat16 [8192, 12288], P(None, ('pipe', 'mp')), may hold values from -0.9923308 to 0.9923308
Outputs:
- logprobs: float32 [32, 12288], P(None, ('pipe', 'mp'))
- chosen: float32 [32], replicated
Inputs may be any that keep to these rules, and one draw needn't show every extreme that they name: `assign`: a permutation of the 32 requests.
All inputs are finite; a program needn't handle non-finite values.
Results may differ from a plain program's by a relative error of at most 0.0017.
Values may be sent and summed in bfloat16 or wider, within the bound.
No kernel may reach another device: no remote copies, remote signals or barrier semaphores. Data moves between devices by JAX's collectives and lax.ppermute only.
A program may use at most 64 MiB of HBM per device.

v0:
```python
import jax
import jax.numpy as jnp
from jax import lax
from jax.sharding import PartitionSpec as P

D = 8192
HEADS = 32
KV_HEADS = 4
HEAD_DIM = 128
MICRO = 4
MB_ROWS = 8


EPS = 1e-06
THETA = 1000000.0


def from_behind(block, axis, distance):
    devices = range(lax.axis_size(axis))
    route = [(i - distance, i) for i in devices if i - distance in devices]
    return lax.ppermute(block, axis, route)


def from_root(value, axis, root):
    mine = lax.axis_index(axis) == root
    return lax.psum(jnp.where(mine, value, jnp.zeros_like(value)), axis)


def rotate(values_in, positions):
    half_dim = values_in.shape[-1] // 2
    frequency = THETA ** (-jnp.arange(half_dim).astype(jnp.float32) * 2.0 / values_in.shape[-1])
    angles = positions.astype(jnp.float32)[:, None, None] * frequency[None, None, :]
    front_half = values_in[..., :half_dim]
    back_half = values_in[..., half_dim:]
    cosine = jnp.cos(angles)
    sine_part = jnp.sin(angles)
    return jnp.concatenate(
        [front_half * cosine - back_half * sine_part, back_half * cosine + front_half * sine_part],
        axis=-1,
    )


def local(
    hidden_in,
    lengths,
    assign,
    token_ids,
    attn_gain,
    qkv_weight,
    qkv_bias,
    out_weight,
    kv_cache,
    final_gain,
    head_weight,
):
    sections = lax.axis_size("pipe")
    section_index = lax.axis_index("pipe")
    local_count = kv_cache.shape[1]
    query_cols = HEADS * HEAD_DIM
    key_cols = KV_HEADS * HEAD_DIM
    group_size = HEADS // KV_HEADS
    scale_factor = HEAD_DIM ** (-0.5)
    own_ids = lax.axis_index("mp") * local_count + jnp.arange(local_count, dtype=jnp.int32)
    slot_ids = jnp.arange(assign.shape[0], dtype=jnp.int32)
    slot_of = jnp.zeros_like(assign).at[assign].set(slot_ids)
    every_row = slot_of % MB_ROWS
    every_batch = slot_of // MB_ROWS
    own_slots = slot_of[own_ids]
    own_lengths = lengths[own_ids]
    own_rows = own_slots % MB_ROWS
    own_batch = own_slots // MB_ROWS
    visible = jnp.arange(kv_cache.shape[4], dtype=jnp.int32)[None, :] < own_lengths[:, None]
    gain_row = attn_gain[0].astype(jnp.float32)
    weight_in = qkv_weight[0]
    bias_row = qkv_bias[0].astype(jnp.float32)
    weight_out = out_weight[0]
    cache_rows = kv_cache[0]
    slot_table = assign.reshape(MICRO, MB_ROWS)
    row_slots = jnp.arange(MB_ROWS, dtype=jnp.int32)

    def attend_one(request_item):
        queries_one, key_one, value_one, cache_one, visible_one, present_one = request_item

        def compute(unused):
            scores = (
                jnp.einsum(
                    "kgd,kjd->kgj", queries_one, cache_one[0], preferred_element_type=jnp.float32
                )
                * scale_factor
            )
            self_score = (
                jnp.einsum("kgd,kd->kg", queries_one, key_one, preferred_element_type=jnp.float32)
                * scale_factor
            )
            key_mask = visible_one[None, None, :]
            row_top = jnp.maximum(jnp.max(jnp.where(key_mask, scores, -1e30), axis=-1), self_score)
            weights = jnp.where(key_mask, jnp.exp(scores - row_top[..., None]), 0.0)
            self_weight = jnp.exp(self_score - row_top)
            row_total = jnp.sum(weights, axis=-1) + self_weight
            summed = jnp.einsum(
                "kgj,kjd->kgd",
                weights.astype(jnp.bfloat16),
                cache_one[1],
                preferred_element_type=jnp.float32,
            )
            summed = summed + jnp.einsum(
                "kg,kd->kgd",
                self_weight.astype(jnp.bfloat16),
                value_one,
                preferred_element_type=jnp.float32,
            )
            return (summed / row_total[..., None]).astype(jnp.bfloat16).reshape(query_cols)

        def nothing(unused):
            return jnp.zeros((query_cols,), jnp.bfloat16)

        return lax.cond(present_one, compute, nothing, 0)

    def apply_layer(rows_in, batch_index):
        current = rows_in.astype(jnp.float32)
        squares = jnp.sum(current * current, axis=1)
        scaled = (current * gain_row).astype(jnp.bfloat16)
        partial_cols = jnp.dot(scaled, weight_in, preferred_element_type=jnp.float32)
        squares_all = lax.psum(squares, "mp")
        share_cols = lax.psum_scatter(partial_cols, "mp", scatter_dimension=1, tiled=True)
        share_width = share_cols.shape[1]
        share_bias = lax.dynamic_slice_in_dim(
            bias_row, lax.axis_index("mp") * share_width, share_width, 0
        )
        share_cols = share_cols * lax.rsqrt(squares_all / D + EPS)[:, None] + share_bias
        wanted = (
            (every_row[:, None] == row_slots[None, :]) & (every_batch[:, None] == batch_index)
        ).astype(jnp.float32)
        routed_rows = jnp.dot(wanted, share_cols, precision=lax.Precision.HIGHEST)
        picked = lax.all_to_all(routed_rows, "mp", split_axis=0, concat_axis=1, tiled=True)
        queries = rotate(
            picked[:, :query_cols].reshape(local_count, HEADS, HEAD_DIM), own_lengths
        ).astype(jnp.bfloat16)
        queries = queries.reshape(local_count, KV_HEADS, group_size, HEAD_DIM)
        key_new = rotate(
            picked[:, query_cols : query_cols + key_cols].reshape(local_count, KV_HEADS, HEAD_DIM),
            own_lengths,
        ).astype(jnp.bfloat16)
        value_new = (
            picked[:, query_cols + key_cols :]
            .reshape(local_count, KV_HEADS, HEAD_DIM)
            .astype(jnp.bfloat16)
        )
        present = own_batch == batch_index
        attended = lax.map(attend_one, (queries, key_new, value_new, cache_rows, visible, present))
        placing = ((own_rows[:, None] == row_slots[None, :]) & present[:, None]).astype(
            jnp.bfloat16
        )
        spread = jnp.dot(placing.T, attended, preferred_element_type=jnp.float32)
        gathered = lax.psum(spread.astype(jnp.bfloat16), "mp")
        update = jnp.dot(gathered, weight_out, preferred_element_type=jnp.float32)
        return (current + update).astype(jnp.bfloat16)

    def advance(turn_index, state_pair):
        outgoing, finished = state_pair
        incoming = from_behind(outgoing, "pipe", 1)
        offset = turn_index - section_index
        batch_index = jnp.clip(offset, 0, MICRO - 1)
        members = lax.dynamic_index_in_dim(slot_table, batch_index, 0, keepdims=False)
        entering = jnp.take(hidden_in, members, axis=0)
        rows_in = jnp.where(section_index == 0, entering, incoming)
        inside = (offset >= 0) & (offset < MICRO)
        rows_out = apply_layer(rows_in, jnp.where(inside, batch_index, -1))
        storing = inside & (section_index == sections - 1)
        placed = lax.dynamic_update_slice_in_dim(finished, rows_out, batch_index * MB_ROWS, 0)
        return (rows_out, jnp.where(storing, placed, finished))

    outgoing = jnp.zeros((MB_ROWS, hidden_in.shape[1]), jnp.bfloat16)
    finished = jnp.zeros(hidden_in.shape, jnp.bfloat16)
    outgoing, finished = lax.fori_loop(0, MICRO + sections - 1, advance, (outgoing, finished))
    final_rows = from_root(finished, "pipe", sections - 1)
    current = final_rows.astype(jnp.float32)
    squares = lax.psum(jnp.sum(current * current, axis=1), "mp")
    normed = (
        current * final_gain.astype(jnp.float32) * lax.rsqrt(squares / D + EPS)[:, None]
    ).astype(jnp.bfloat16)
    logits = jnp.dot(
        lax.all_gather(normed, "mp", axis=1, tiled=True),
        head_weight,
        preferred_element_type=jnp.float32,
    )
    vocab_width = head_weight.shape[1]
    vocab_ids = lax.axis_index(("pipe", "mp")) * vocab_width + jnp.arange(
        vocab_width, dtype=jnp.int32
    )
    targets = token_ids[assign]
    matches = vocab_ids[None, :] == targets[:, None]
    picked_local = jnp.sum(jnp.where(matches, logits, 0.0), axis=1)
    local_top = jnp.max(logits, axis=1)
    row_top = lax.pmax(local_top, ("pipe", "mp"))
    local_total = jnp.sum(jnp.exp(logits - row_top[:, None]), axis=1)
    row_total, picked = lax.psum((local_total, picked_local), ("pipe", "mp"))
    log_total = row_top + jnp.log(row_total)
    return (logits - log_total[:, None], picked - log_total)


def solution(mesh):
    return jax.shard_map(
        local,
        mesh=mesh,
        in_specs=(
            P(None, "mp"),
            P(),
            P(),
            P(),
            P("pipe", "mp"),
            P("pipe", "mp", None),
            P("pipe", None),
            P("pipe", None, "mp"),
            P("pipe", "mp", None, None, None, None),
            P("mp"),
            P(None, ("pipe", "mp")),
        ),
        out_specs=(P(None, ("pipe", "mp")), P()),
        check_vma=False,
    )
```

profile of v0, /device:TPU:0, one launch (start us, length us, event | category | flops | bytes accessed | tf_op | source)
XLA Modules:
  0.0 1333.1 jit_solution(10831050884700243807)
XLA Ops:
  13.6 1140.3 %while.53 = (s32[]{:T(128)}, bf16[8,1024]{1,0:T(8,128)(2,1)S(1)}, bf16[32,1024]{1,0:T(8,128)(2,1)S(1)}, pred[]{:T(512)}, s32[]{:T(128)}, /*index=5*/s32[4,8]{1,0...) while((s32[]{:T(128)}, bf16[8,1024]{1,0:T(8,128)(2,1)S(1)}, ...), condition=%wide.region_12.13_spmd.clone.clone, body=%wide.region_1.12_spmd.clone.clone.sunk | while | flops 157849424 | bytes 22136348 | solution.py:175
  24.2 22.5 %psum.66 = f32[8]{0:T(128)S(1)} all-reduce(f32[8]{0:T(128)S(1)} %get-tuple-element.929), channel_id=1, replica_groups=mesh['pipe'=4,'mp'=8] {'mp'}, use_global_device_ids=true, to_apply=%region_4.4 | all-reduce | flops 8 | bytes 64 | tf_op jit(solution)/shard_map/while/body/eval_jaxpr/psum | solution.py:124
  46.7 36.4 %reduce-scatter.2.cloned.1.call-done = f32[8,640]{1,0:T(8,128)} async-done(((f32[8,5120]{1,0:T(8,128)}), f32[8,640]{1,0:T(8,128)}) %reduce-scatter.2.cloned.1.call-update) | async-done | bytes 20496 | tf_op jit(solution)/shard_map/while/body/eval_jaxpr/reduce_scatter | solution.py:125
  105.8 68.3 %all-reduce.6.cloned.1.call-done = bf16[8,4096]{1,0:T(8,128)(2,1)} async-done(((bf16[8,4096]{1,0:T(8,128)(2,1)}), bf16[8,4096]{1,0:T(8,128)(2,1)}) %all-reduce.6.cloned.1.call-update) | async-done | bytes 65552 | tf_op jit(solution)/shard_map/while/body/eval_jaxpr/psum | solution.py:155
  188.2 20.4 %psum.66 = f32[8]{0:T(128)S(1)} all-reduce(f32[8]{0:T(128)S(1)} %get-tuple-element.929), channel_id=1, replica_groups=mesh['pipe'=4,'mp'=8] {'mp'}, use_global_device_ids=true, to_apply=%region_4.4 | all-reduce | flops 8 | bytes 64 | tf_op jit(solution)/shard_map/while/body/eval_jaxpr/psum | solution.py:124
  208.6 36.8 %reduce-scatter.2.cloned.1.call-done = f32[8,640]{1,0:T(8,128)} async-done(((f32[8,5120]{1,0:T(8,128)}), f32[8,640]{1,0:T(8,128)}) %reduce-scatter.2.cloned.1.call-update) | async-done | bytes 20496 | tf_op jit(solution)/shard_map/while/body/eval_jaxpr/reduce_scatter | solution.py:125
  265.4 71.2 %all-reduce.6.cloned.1.call-done = bf16[8,4096]{1,0:T(8,128)(2,1)} async-done(((bf16[8,4096]{1,0:T(8,128)(2,1)}), bf16[8,4096]{1,0:T(8,128)(2,1)}) %all-reduce.6.cloned.1.call-update) | async-done | bytes 65552 | tf_op jit(solution)/shard_map/while/body/eval_jaxpr/psum | solution.py:155
  350.6 20.4 %psum.66 = f32[8]{0:T(128)S(1)} all-reduce(f32[8]{0:T(128)S(1)} %get-tuple-element.929), channel_id=1, replica_groups=mesh['pipe'=4,'mp'=8] {'mp'}, use_global_device_ids=true, to_apply=%region_4.4 | all-reduce | flops 8 | bytes 64 | tf_op jit(solution)/shard_map/while/body/eval_jaxpr/psum | solution.py:124
  371.0 36.8 %reduce-scatter.2.cloned.1.call-done = f32[8,640]{1,0:T(8,128)} async-done(((f32[8,5120]{1,0:T(8,128)}), f32[8,640]{1,0:T(8,128)}) %reduce-scatter.2.cloned.1.call-update) | async-done | bytes 20496 | tf_op jit(solution)/shard_map/while/body/eval_jaxpr/reduce_scatter | solution.py:125
  430.5 69.3 %all-reduce.6.cloned.1.call-done = bf16[8,4096]{1,0:T(8,128)(2,1)} async-done(((bf16[8,4096]{1,0:T(8,128)(2,1)}), bf16[8,4096]{1,0:T(8,128)(2,1)}) %all-reduce.6.cloned.1.call-update) | async-done | bytes 65552 | tf_op jit(solution)/shard_map/while/body/eval_jaxpr/psum | solution.py:155
  513.9 20.4 %psum.66 = f32[8]{0:T(128)S(1)} all-reduce(f32[8]{0:T(128)S(1)} %get-tuple-element.929), channel_id=1, replica_groups=mesh['pipe'=4,'mp'=8] {'mp'}, use_global_device_ids=true, to_apply=%region_4.4 | all-reduce | flops 8 | bytes 64 | tf_op jit(solution)/shard_map/while/body/eval_jaxpr/psum | solution.py:124
  534.2 36.8 %reduce-scatter.2.cloned.1.call-done = f32[8,640]{1,0:T(8,128)} async-done(((f32[8,5120]{1,0:T(8,128)}), f32[8,640]{1,0:T(8,128)}) %reduce-scatter.2.cloned.1.call-update) | async-done | bytes 20496 | tf_op jit(solution)/shard_map/while/body/eval_jaxpr/reduce_scatter | solution.py:125
  596.5 66.6 %all-reduce.6.cloned.1.call-done = bf16[8,4096]{1,0:T(8,128)(2,1)} async-done(((bf16[8,4096]{1,0:T(8,128)(2,1)}), bf16[8,4096]{1,0:T(8,128)(2,1)}) %all-reduce.6.cloned.1.call-update) | async-done | bytes 65552 | tf_op jit(solution)/shard_map/while/body/eval_jaxpr/psum | solution.py:155
  697.6 36.8 %reduce-scatter.2.cloned.1.call-done = f32[8,640]{1,0:T(8,128)} async-done(((f32[8,5120]{1,0:T(8,128)}), f32[8,640]{1,0:T(8,128)}) %reduce-scatter.2.cloned.1.call-update) | async-done | bytes 20496 | tf_op jit(solution)/shard_map/while/body/eval_jaxpr/reduce_scatter | solution.py:125
  754.4 72.2 %all-reduce.6.cloned.1.call-done = bf16[8,4096]{1,0:T(8,128)(2,1)} async-done(((bf16[8,4096]{1,0:T(8,128)(2,1)}), bf16[8,4096]{1,0:T(8,128)(2,1)}) %all-reduce.6.cloned.1.call-update) | async-done | bytes 65552 | tf_op jit(solution)/shard_map/while/body/eval_jaxpr/psum | solution.py:155
  861.0 36.8 %reduce-scatter.2.cloned.1.call-done = f32[8,640]{1,0:T(8,128)} async-done(((f32[8,5120]{1,0:T(8,128)}), f32[8,640]{1,0:T(8,128)}) %reduce-scatter.2.cloned.1.call-update) | async-done | bytes 20496 | tf_op jit(solution)/shard_map/while/body/eval_jaxpr/reduce_scatter | solution.py:125
  917.8 72.1 %all-reduce.6.cloned.1.call-done = bf16[8,4096]{1,0:T(8,128)(2,1)} async-done(((bf16[8,4096]{1,0:T(8,128)(2,1)}), bf16[8,4096]{1,0:T(8,128)(2,1)}) %all-reduce.6.cloned.1.call-update) | async-done | bytes 65552 | tf_op jit(solution)/shard_map/while/body/eval_jaxpr/psum | solution.py:155
  1024.4 36.8 %reduce-scatter.2.cloned.1.call-done = f32[8,640]{1,0:T(8,128)} async-done(((f32[8,5120]{1,0:T(8,128)}), f32[8,640]{1,0:T(8,128)}) %reduce-scatter.2.cloned.1.call-update) | async-done | bytes 20496 | tf_op jit(solution)/shard_map/while/body/eval_jaxpr/reduce_scatter | solution.py:125
  1081.2 68.1 %all-reduce.6.cloned.1.call-done = bf16[8,4096]{1,0:T(8,128)(2,1)} async-done(((bf16[8,4096]{1,0:T(8,128)(2,1)}), bf16[8,4096]{1,0:T(8,128)(2,1)}) %all-reduce.6.cloned.1.call-update) | async-done | bytes 65552 | tf_op jit(solution)/shard_map/while/body/eval_jaxpr/psum | solution.py:155
  1155.3 32.6 %all-reduce.4.cloned.1.call-done = bf16[32,1024]{1,0:T(8,128)(2,1)} async-done(((bf16[32,1024]{1,0:T(8,128)(2,1)}), bf16[32,1024]{1,0:T(8,128)(2,1)}) %all-reduce.4.cloned.1.call-update) | async-done | bytes 65552 | tf_op jit(solution)/shard_map/psum | solution.py:26
  1188.9 21.4 %psum.57 = f32[32]{0:T(128)S(1)} all-reduce(f32[32]{0:T(128)S(1)} %fusion.50), channel_id=1, replica_groups=mesh['pipe'=4,'mp'=8] {'mp'}, use_global_device_ids=true, to_apply=%region_15.16 | all-reduce | flops 32 | bytes 256 | tf_op jit(solution)/shard_map/psum | solution.py:178
  1211.2 31.4 %all_gather.3 = bf16[32,8192]{1,0:T(8,128)(2,1)S(1)} all-gather(bf16[32,1024]{1,0:T(8,128)(2,1)S(1)} %fusion.49), channel_id=1, replica_groups=mesh['pipe'=4,'mp'=8] {'mp'}, dimensions={1}, use_global_device_ids=true | all-gather | bytes 589824 | tf_op jit(solution)/shard_map/all_gather | solution.py:183
  1246.5 36.8 %pmax.7 = f32[32]{0:T(128)S(1)} all-reduce(f32[32]{0:T(128)S(1)} %get-tuple-element.743), channel_id=1, replica_groups=mesh['pipe'=4,'mp'=8] {'pipe','mp'}, use_global_device_ids=true, to_apply=%region_17.18 | all-reduce | flops 32 | bytes 256 | tf_op jit(solution)/shard_map/pmax | solution.py:195
  1283.5 41.2 %all-reduce = (f32[32]{0:T(128)S(1)}, f32[32]{0:T(128)S(1)}) all-reduce(f32[32]{0:T(128)S(1)} %get-tuple-element.666, f32[32]{0:T(128)S(1)} %get-tuple-element.665), channel_id=1, replica_groups=mesh['pipe'=4,'mp'=8] {'pipe','mp'}, use_global_device_ids=true, to_apply=%region_19.20 | all-reduce | flops 64 | bytes 512 | tf_op jit(solution)/shard_map/psum | solution.py:197
  (450 shorter events, 370.7 us)
Async XLA Ops:
  13.6 69.5 %reduce-scatter.2.cloned.1.call-start = ((), (), s32[]{:S(2)}) async-start(), calls=%async_computation.3 | async-start | bytes 184320 | tf_op jit(solution)/shard_map/while/body/eval_jaxpr/reduce_scatter | solution.py:125
  13.7 4.1 collective-permute-start
  84.7 10.6 all-to-all-start
  88.3 85.8 %all-reduce.6.cloned.1.call-start = ((), (), s32[]{:S(2)}) async-start(), calls=%async_computation.4 | async-start | bytes 131072 | tf_op jit(solution)/shard_map/while/body/eval_jaxpr/psum | solution.py:155
  178.7 66.7 %reduce-scatter.2.cloned.1.call-start = ((), (), s32[]{:S(2)}) async-start(), calls=%async_computation.3 | async-start | bytes 184320 | tf_op jit(solution)/shard_map/while/body/eval_jaxpr/reduce_scatter | solution.py:125
  247.0 10.6 all-to-all-start
  250.6 85.9 %all-reduce.6.cloned.1.call-start = ((), (), s32[]{:S(2)}) async-start(), calls=%async_computation.4 | async-start | bytes 131072 | tf_op jit(solution)/shard_map/while/body/eval_jaxpr/psum | solution.py:155
  341.1 66.7 %reduce-scatter.2.cloned.1.call-start = ((), (), s32[]{:S(2)}) async-start(), calls=%async_computation.3 | async-start | bytes 184320 | tf_op jit(solution)/shard_map/while/body/eval_jaxpr/reduce_scatter | solution.py:125
  341.2 3.0 collective-permute-start
  409.4 10.6 all-to-all-start
  413.1 86.7 %all-reduce.6.cloned.1.call-start = ((), (), s32[]{:S(2)}) async-start(), calls=%async_computation.4 | async-start | bytes 131072 | tf_op jit(solution)/shard_map/while/body/eval_jaxpr/psum | solution.py:155
  504.4 66.7 %reduce-scatter.2.cloned.1.call-start = ((), (), s32[]{:S(2)}) async-start(), calls=%async_computation.3 | async-start | bytes 184320 | tf_op jit(solution)/shard_map/while/body/eval_jaxpr/reduce_scatter | solution.py:125
  572.7 10.6 all-to-all-start
  576.3 86.8 %all-reduce.6.cloned.1.call-start = ((), (), s32[]{:S(2)}) async-start(), calls=%async_computation.4 | async-start | bytes 131072 | tf_op jit(solution)/shard_map/while/body/eval_jaxpr/psum | solution.py:155
  667.7 66.7 %reduce-scatter.2.cloned.1.call-start = ((), (), s32[]{:S(2)}) async-start(), calls=%async_computation.3 | async-start | bytes 184320 | tf_op jit(solution)/shard_map/while/body/eval_jaxpr/reduce_scatter | solution.py:125
  736.0 10.6 all-to-all-start
  739.6 86.9 %all-reduce.6.cloned.1.call-start = ((), (), s32[]{:S(2)}) async-start(), calls=%async_computation.4 | async-start | bytes 131072 | tf_op jit(solution)/shard_map/while/body/eval_jaxpr/psum | solution.py:155
  831.2 66.7 %reduce-scatter.2.cloned.1.call-start = ((), (), s32[]{:S(2)}) async-start(), calls=%async_computation.3 | async-start | bytes 184320 | tf_op jit(solution)/shard_map/while/body/eval_jaxpr/reduce_scatter | solution.py:125
  899.5 10.6 all-to-all-start
  903.1 86.8 %all-reduce.6.cloned.1.call-start = ((), (), s32[]{:S(2)}) async-start(), calls=%async_computation.4 | async-start | bytes 131072 | tf_op jit(solution)/shard_map/while/body/eval_jaxpr/psum | solution.py:155
  994.5 66.7 %reduce-scatter.2.cloned.1.call-start = ((), (), s32[]{:S(2)}) async-start(), calls=%async_computation.3 | async-start | bytes 184320 | tf_op jit(solution)/shard_map/while/body/eval_jaxpr/reduce_scatter | solution.py:125
  1062.8 10.6 all-to-all-start
  1066.4 82.8 %all-reduce.6.cloned.1.call-start = ((), (), s32[]{:S(2)}) async-start(), calls=%async_computation.4 | async-start | bytes 131072 | tf_op jit(solution)/shard_map/while/body/eval_jaxpr/psum | solution.py:155
  1153.9 34.1 %all-reduce.4.cloned.1.call-start = ((), (), s32[]{:S(2)}) async-start(), calls=%async_computation.2 | async-start | bytes 131072 | tf_op jit(solution)/shard_map/psum | solution.py:26
  (7 other events, 2302.6 us)
Sparse Core Ops, SparseCore 0:
  24.2 58.8 reduce-scatter.1
  105.9 68.1 all-reduce.5
  188.2 57.1 reduce-scatter.1
  265.5 71.0 all-reduce.5
  350.6 57.1 reduce-scatter.1
  430.6 69.1 all-reduce.5
  513.9 57.1 reduce-scatter.1
  596.6 66.4 all-reduce.5
  677.2 57.1 reduce-scatter.1
  754.5 72.0 all-reduce.5
  840.7 57.1 reduce-scatter.1
  917.9 71.9 all-reduce.5
  1004.0 57.1 reduce-scatter.1
  1081.3 67.9 all-reduce.5
Sparse Core Ops, SparseCore 1:
  1156.7 31.2 all-reduce.3
where the time goes:
time: 1340 us; the launch traced here: 1330 us
  waiting for transfers between devices  827 us (62%)
  blocking collectives  276 us (21%)
  matrix products  102 us (8%)
  local copies, waits for them, and re-layouts  43.2 us (3%)
  starting transfers between devices  35.9 us (3%)
  loops' own time  22.4 us (2%)
  between operations  15.3 us (1%)
    psum x7, waiting for transfers between devices, apply_layer(): gathered = lax.psum(spread.astype(jnp.bfloat16), 'mp')  488 us
    reduce_scatter x7, waiting for transfers between devices, apply_layer(): lax.psum_scatter(partial_cols, 'mp', scatter_dimension=1, tiled=True)  257 us
    psum x7, blocking collectives, apply_layer(): squares_all = lax.psum(squares, 'mp')  145 us
    all_to_all x7, waiting for transfers between devices, apply_layer(): lax.all_to_all(routed_rows, 'mp', split_axis=0, concat_axis=1, tiled=True)  48.7 us
    dot_general x7, matrix products, apply_layer(): jnp.dot(scaled, weight_in, preferred_element_type=jnp.float32)  42.7 us
    psum x1, blocking collectives, local(): row_total, picked = lax.psum((local_total, picked_local), ('pipe', 'mp'))  41.2 us
    pmax x1, blocking collectives, local(): row_top = lax.pmax(local_top, ('pipe', 'mp'))  36.8 us
    psum x1, waiting for transfers between devices, from_root(): return lax.psum(jnp.where(mine, value, jnp.zeros_like(value)), axis)  32.6 us
  transfers between devices with their start and end apart: 29, of which 22 were waited for; matrix products, arithmetic and copies ran while one was open for 1% of the time, Pallas kernels for 0%

commit v1 on v0

v1 whole, which is shorter than its diff:
```python
import functools

import jax
import jax.numpy as jnp
from jax import lax
from jax.experimental import pallas as pl
from jax.experimental.pallas import tpu as pltpu
from jax.sharding import PartitionSpec as P

HEADS = 32
KV_HEADS = 4
HEAD_DIM = 128
GROUP = HEADS // KV_HEADS
EPS = 1e-06
THETA = 1000000.0
LANES = 128


def split_three(value):
    high = lax.reduce_precision(value, 8, 7)
    rest = value - high
    middle = lax.reduce_precision(rest, 8, 7)
    low = lax.reduce_precision(rest - middle, 8, 7)
    return high, middle, low


def attend_kernel(
    part_q, part_k, part_v, part_s, bias_q, bias_k, bias_v, cos_ref, sin_ref, upper_ref, cache_ref,
    out_ref, *, width,
):
    count = out_ref.shape[0]
    length = cache_ref.shape[3]
    squares = jnp.sum(jnp.sum(part_s[...].astype(jnp.float32), axis=0), axis=1, keepdims=True)
    inverse = lax.rsqrt(squares / width + EPS)
    cosine = cos_ref[...]
    sine = sin_ref[...]

    def project(part, bias):
        summed = jnp.sum(part[...].astype(jnp.float32), axis=0)
        return summed * inverse + bias[...].astype(jnp.float32)

    def rotate(head):
        return head * cosine + pltpu.roll(head, HEAD_DIM // 2, 1) * sine

    flat = project(part_q, bias_q)
    heads = [rotate(flat[:, g * HEAD_DIM : (g + 1) * HEAD_DIM]) for g in range(GROUP)]
    queries = jnp.concatenate(heads, axis=0).astype(jnp.bfloat16)
    key_new = rotate(project(part_k, bias_k)).astype(jnp.bfloat16).astype(jnp.float32)
    value_new = project(part_v, bias_v).astype(jnp.bfloat16).astype(jnp.float32)
    keys = cache_ref[:, 0, 0].reshape(count * length, HEAD_DIM)
    values = cache_ref[:, 1, 0].reshape(count * length, HEAD_DIM)
    scale = HEAD_DIM ** (-0.5)
    scores = (
        lax.dot_general(
            queries, keys, (((1,), (1,)), ((), ())), preferred_element_type=jnp.float32
        )
        * scale
    )
    tiled_key = jnp.concatenate([key_new] * GROUP, axis=0)
    tiled_value = jnp.concatenate([value_new] * GROUP, axis=0)
    self_score = (
        jnp.sum(queries.astype(jnp.float32) * tiled_key, axis=1, keepdims=True) * scale
    )
    rows = lax.broadcasted_iota(jnp.int32, scores.shape, 0) % count
    columns = lax.broadcasted_iota(jnp.int32, scores.shape, 1)
    visible = (columns >= rows * length) & (columns < upper_ref[...])
    top = jnp.maximum(jnp.max(jnp.where(visible, scores, -1e30), axis=1, keepdims=True), self_score)
    weights = jnp.where(visible, jnp.exp(scores - top), 0.0)
    self_weight = jnp.exp(self_score - top)
    total = jnp.sum(weights, axis=1, keepdims=True) + self_weight
    summed = jnp.dot(weights.astype(jnp.bfloat16), values, preferred_element_type=jnp.float32)
    summed = summed + self_weight.astype(jnp.bfloat16).astype(jnp.float32) * tiled_value
    attended = summed / total
    for g in range(GROUP):
        out_ref[:, g * HEAD_DIM : (g + 1) * HEAD_DIM] = attended[
            g * count : (g + 1) * count
        ].astype(jnp.bfloat16)


def attend(parts, bias, cosine, sine, upper, cache, width):
    peers, count, _ = parts.shape
    length = cache.shape[3]
    group_cols = GROUP * HEAD_DIM
    first_key = HEADS
    first_value = HEADS + KV_HEADS
    squares_at = HEADS + 2 * KV_HEADS
    head_part = lambda place: pl.BlockSpec((peers, count, HEAD_DIM), lambda k: (0, 0, place(k)))
    head_bias = lambda place: pl.BlockSpec((1, HEAD_DIM), lambda k: (0, place(k)))
    whole = lambda array: pl.BlockSpec(array.shape, lambda k: (0, 0))
    return pl.pallas_call(
        functools.partial(attend_kernel, width=width),
        grid=(KV_HEADS,),
        in_specs=[
            pl.BlockSpec((peers, count, group_cols), lambda k: (0, 0, k)),
            head_part(lambda k: first_key + k),
            head_part(lambda k: first_value + k),
            head_part(lambda k: squares_at),
            pl.BlockSpec((1, group_cols), lambda k: (0, k)),
            head_bias(lambda k: first_key + k),
            head_bias(lambda k: first_value + k),
            whole(cosine),
            whole(sine),
            whole(upper),
            pl.BlockSpec((count, 2, 1, length, HEAD_DIM), lambda k: (0, 0, k, 0, 0)),
        ],
        out_specs=pl.BlockSpec((count, group_cols), lambda k: (0, k)),
        out_shape=jax.ShapeDtypeStruct((count, HEADS * HEAD_DIM), jnp.bfloat16),
        name="attend",
    )(parts, parts, parts, parts, bias, bias, bias, cosine, sine, upper, cache)


def exchange(blocks, axis):
    return lax.all_to_all(blocks, axis, 0, 0, tiled=True)


def spread(value, axis):
    blocks = jnp.broadcast_to(value[None], (lax.axis_size(axis),) + value.shape)
    return exchange(blocks, axis)


def local(
    hidden_in,
    lengths,
    assign,
    token_ids,
    attn_gain,
    qkv_weight,
    qkv_bias,
    out_weight,
    kv_cache,
    final_gain,
    head_weight,
):
    sections = lax.axis_size("pipe")
    section = lax.axis_index("pipe")
    peers = lax.axis_size("mp")
    count = kv_cache.shape[1]
    length = kv_cache.shape[4]
    requests, share = hidden_in.shape
    width = share * peers
    first = lax.axis_index("mp") * count
    own_lengths = lax.dynamic_slice_in_dim(lengths, first, count, 0)
    half = HEAD_DIM // 2
    frequency = THETA ** (-jnp.arange(half).astype(jnp.float32) * 2.0 / HEAD_DIM)
    angles = own_lengths.astype(jnp.float32)[:, None] * frequency[None, :]
    cosine = jnp.cos(angles)
    sine = jnp.sin(angles)
    cosine = jnp.concatenate([cosine, cosine], axis=1)
    sine = jnp.concatenate([-sine, sine], axis=1)
    upper = jnp.arange(count, dtype=jnp.int32) * length + own_lengths
    upper = jnp.tile(upper, GROUP)[:, None]
    gain = attn_gain[0].astype(jnp.float32)
    weight_in = qkv_weight[0]
    weight_out = out_weight[0]
    cache = kv_cache[0]

    gain_blocks = jnp.broadcast_to(final_gain[None, None], (peers, 1, share))
    gain_full = lax.cond(section != 0, lambda b: exchange(b, "mp"), lambda b: b, gain_blocks)

    stream = hidden_in
    for layer in range(sections):
        active = section == layer
        current = stream.astype(jnp.float32)
        squares = jnp.sum(current * current, axis=1, keepdims=True)
        scaled = (current * gain).astype(jnp.bfloat16)
        partial_cols = jnp.dot(scaled, weight_in, preferred_element_type=jnp.float32)
        lane = lax.broadcasted_iota(jnp.int32, (requests, LANES), 1)
        high, middle, low = split_three(squares)
        tail = jnp.where(
            lane == 0, high, jnp.where(lane == 1, middle, jnp.where(lane == 2, low, 0.0))
        )
        payload = jnp.concatenate([partial_cols, tail], axis=1).astype(jnp.bfloat16)
        payload = payload.reshape(peers, count, -1)
        parts = lax.cond(active, lambda b: exchange(b, "mp"), lambda b: b, payload)
        attended = attend(parts, qkv_bias, cosine, sine, upper, cache, width)
        gathered = lax.cond(
            active,
            lambda b: spread(b, "mp"),
            lambda b: jnp.broadcast_to(b[None], (peers,) + b.shape),
            attended,
        )
        gathered = gathered.reshape(requests, -1)
        update = jnp.dot(gathered, weight_out, preferred_element_type=jnp.float32)
        stream = (current + update).astype(jnp.bfloat16)
        if layer + 1 < sections:
            stream = lax.ppermute(stream, "pipe", [(layer, layer + 1)])
        if layer == 0:
            gain_full, stream = lax.optimization_barrier((gain_full, stream))
            gain_full = lax.cond(section == 0, lambda b: exchange(b, "mp"), lambda b: b, gain_full)

    last = sections - 1
    odd = section % 2 == 1
    arrived = stream
    for target in range(1, last, 2):
        copied = lax.ppermute(stream, "pipe", [(last, target)])
        arrived = jnp.where(section == target, copied, arrived)
    rows = lax.cond(
        odd,
        lambda b: spread(b, "mp"),
        lambda b: jnp.broadcast_to(b[None], (peers,) + b.shape),
        arrived,
    )
    over = lax.ppermute(rows, "pipe", [(i, i - 1) for i in range(1, sections, 2)])
    rows = jnp.where(odd, rows, over)

    current = rows.astype(jnp.float32)
    squares = jnp.sum(current * current, axis=(0, 2))
    inverse = lax.rsqrt(squares / width + EPS)
    normed = (current * gain_full.astype(jnp.float32) * inverse[None, :, None]).astype(jnp.bfloat16)
    normed = jnp.transpose(normed, (1, 0, 2)).reshape(requests, width)
    placing = (assign[:, None] == jnp.arange(requests, dtype=jnp.int32)[None, :]).astype(
        jnp.bfloat16
    )
    normed = jnp.dot(placing, normed, preferred_element_type=jnp.float32).astype(jnp.bfloat16)
    logits = jnp.dot(normed, head_weight, preferred_element_type=jnp.float32)
    vocab = head_weight.shape[1]
    vocab_ids = lax.axis_index(("pipe", "mp")) * vocab + jnp.arange(vocab, dtype=jnp.int32)
    matches = vocab_ids[None, :] == token_ids[assign][:, None]
    picked = jnp.sum(jnp.where(matches, logits, 0.0), axis=1)
    local_top = jnp.max(logits, axis=1)
    local_total = jnp.sum(jnp.exp(logits - local_top[:, None]), axis=1)
    stats = spread(jnp.stack([local_top, local_total, picked]), ("pipe", "mp"))
    stats = stats.reshape(-1, 3, requests)
    row_top = jnp.max(stats[:, 0], axis=0)
    row_total = jnp.sum(stats[:, 1] * jnp.exp(stats[:, 0] - row_top[None, :]), axis=0)
    log_total = row_top + jnp.log(row_total)
    chosen = jnp.sum(stats[:, 2], axis=0) - log_total
    return (logits - log_total[:, None], chosen)


def solution(mesh):
    return jax.shard_map(
        local,
        mesh=mesh,
        in_specs=(
            P(None, "mp"),
            P(),
            P(),
            P(),
            P("pipe", "mp"),
            P("pipe", "mp", None),
            P("pipe", None),
            P("pipe", None, "mp"),
            P("pipe", "mp", None, None, None, None),
            P("mp"),
            P(None, ("pipe", "mp")),
        ),
        out_specs=(P(None, ("pipe", "mp")), P()),
        check_vma=False,
    )
```

time: 1340 us -> 201 us (0.15)
  waiting for transfers between devices: 827 us -> 73.2 us
  blocking collectives: 276 us -> 46 us
  matrix products: 102 us -> 47.3 us
  local copies, waits for them, and re-layouts: 43.2 us -> 3.23 us
  starting transfers between devices: 35.9 us -> 4.58 us
  loops' own time: 22.4 us -> 0.41 us
  Pallas kernels: 0 us -> 17.1 us
  between operations: 15.3 us -> 1.17 us
    psum x8 -> x0, waiting for transfers between devices: 520 us -> none  [the longest x7 488 us: apply_layer(): gathered = lax.psum(spread.astype(jnp.bfloat16), 'mp')]
    reduce_scatter x7 -> x0, waiting for transfers between devices: 257 us -> none  [apply_layer(): lax.psum_scatter(partial_cols, 'mp', scatter_dimension=1, tiled=True)]
    psum x9 -> x0, blocking collectives: 207 us -> none  [the longest x7 145 us: apply_layer(): squares_all = lax.psum(squares, 'mp')]
    ppermute x7 -> x5, waiting for transfers between devices: 0.02 us -> 73.2 us  [the longest x1 72.3 us: local(): lax.ppermute(rows, 'pipe', [(i, i - 1) for i in range(1, sections, 2)])]
    dot_general x41 -> x9, matrix products: 102 us -> 47.3 us  [the longest x4 23.3 us: local(): jnp.dot(scaled, weight_in, preferred_element_type=jnp.float32)]
    all_to_all x7 -> x0, waiting for transfers between devices: 48.7 us -> none  [apply_layer(): lax.all_to_all(routed_rows, 'mp', split_axis=0, concat_axis=1, tiled=True)]
    all_to_all x0 -> x4, blocking collectives: none -> 46 us  [exchange(): return lax.all_to_all(blocks, axis, 0, 0, tiled=True)]
    pmax x1 -> x0, blocking collectives: 36.8 us -> none  [local(): row_top = lax.pmax(local_top, ('pipe', 'mp'))]
  transfers between devices with their start and end apart: 29 -> 5, of which waited for: 22 -> 2; matrix products, arithmetic and copies ran while one was open for 1% -> 1% of each run, Pallas kernels for 0% -> 0%
where the time goes in v1:
time: 201 us; the launch traced here: 200 us
  waiting for transfers between devices  73.2 us (36%)
  matrix products  47.3 us (24%)
  blocking collectives  46 us (23%)
  Pallas kernels  17.1 us (9%)
  other arithmetic  7.41 us (4%)
  starting transfers between devices  4.58 us (2%)
  local copies, waits for them, and re-layouts  3.23 us (2%)
    ppermute x1, waiting for transfers between devices, local(): lax.ppermute(rows, 'pipe', [(i, i - 1) for i in range(1, sections, 2)])  72.3 us
    all_to_all x4, blocking collectives, exchange(): return lax.all_to_all(blocks, axis, 0, 0, tiled=True)  46 us
    dot_general x4, matrix products, local(): jnp.dot(scaled, weight_in, preferred_element_type=jnp.float32)  23.3 us
    dot_general x4, matrix products, local(): update = jnp.dot(gathered, weight_out, preferred_element_type=jnp.float32)  19.8 us
    pallas_call x4, Pallas kernels, attend(): pl.pallas_call(functools.partial(attend_kernel, width=width), grid=(KV_HE...  17.1 us
    dot_general x1, matrix products, local(): logits = jnp.dot(normed, head_weight, preferred_element_type=jnp.float32)  4.15 us
  transfers between devices with their start and end apart: 5, of which 2 were waited for; matrix products, arithmetic and copies ran while one was open for 1% of the time, Pallas kernels for 0%

profile of v1, /device:TPU:0, one launch (start us, length us, event | category | flops | bytes accessed | tf_op | source)
XLA Modules:
  0.0 200.3 jit_solution(17131965408600349013)
XLA Ops:
  1.4 1.0 fusion.57
  4.0 5.9 %fusion.16 = bf16[8,4,5120]{2,1,0:T(4,128)(2,1)S(1)} fusion(bf16[8,4,1024]{2,1,0:T(4,128)(2,1)S(1)} %dot_general.38, bf16[1,1024,5120]{2,1,0:T(8,128)(2,1)} %param.38), kind=kOutput, calls=%fused_computation.18 | convolution fusion | flops 335708160 | bytes 10878976 | tf_op jit(solution)/shard_map/dot_general | solution.py:166
  10.2 16.3 %conditional.12 = (bf16[8,4,5248]{2,1,0:T(4,128)(2,1)S(1)}) conditional(s32[]{:T(128)} %convert_element_type.93, bf16[8,4,5248]{2,1,0:T(4,128)(2,1)S(1)} %pad_maximum_fusion, bf16[8,4,5248]{2,1,0:T(4,128)(2,1)S(1)} %pad_maximum_fusion), branch_computations={%region_3.4_spmd, %region_4.5_spmd} | conditional | bytes 1343496 | solution.py:174
  10.3 16.2 %all_to_all.50 = bf16[8,4,5248]{2,1,0:T(4,128)(2,1)S(1)} all-to-all(bf16[8,4,5248]{2,1,0:T(4,128)(2,1)S(1)} %copy.63), channel_id=1, replica_groups=mesh['pipe'=4,'mp'=8] {'mp'}, dimensions={0} | all-to-all | bytes 671744 | tf_op jit(solution)/shard_map/cond/branch_1_fun/all_to_all | solution.py:113
  27.1 4.2 %attend.4 = bf16[4,4096]{1,0:T(4,128)(2,1)S(1)} custom-call(bf16[8,4,5248]{2,1,0:T(4,128)(2,1)S(1)} %get-tuple-element.104.part_q.part_k.part_v.part_s, bf16[8,4,5248]{2,1,0:T(4,128)(2,1)S(1)} %get-tuple-element.104.part_q.part_k.part_v.part_s, bf16[8,4,5248]{2,1,0:T(4,128)(2,1)S(1)} %get-tuple-element.104.part_q.part_k.part_v.part_s, ...), custom_call_target="tpu_custom_call" | custom-call | tf_op jit(solution)/shard_map/attend/pallas_call | solution.py:90
  31.4 11.0 %conditional.13 = (bf16[32,4096]{1,0:T(8,128)(2,1)S(1)}) conditional(s32[]{:T(128)} %convert_element_type.93, bf16[4,4096]{1,0:T(4,128)(2,1)S(1)} %attend.4, bf16[4,4096]{1,0:T(4,128)(2,1)S(1)} %attend.4), branch_computations={%region_5.6_spmd, %region_6.7_spmd} | conditional | bytes 1343496 | solution.py:176
  31.5 10.9 %all_to_all.51 = bf16[8,4,4096]{2,1,0:T(4,128)(2,1)S(1)} all-to-all(bf16[8,4,4096]{2,1,0:T(4,128)(2,1)S(1)} %broadcast_in_dim.123), channel_id=1, replica_groups=mesh['pipe'=4,'mp'=8] {'mp'}, dimensions={0} | all-to-all | bytes 524288 | tf_op jit(solution)/shard_map/cond/branch_1_fun/all_to_all | solution.py:113
  42.4 4.9 %fusion.50 = bf16[32,1024]{1,0:T(8,128)(2,1)S(1)} fusion(bf16[32,4096]{1,0:T(8,128)(2,1)S(1)} %get-tuple-element.105, bf16[1,4096,1024]{2,1,0:T(8,128)(2,1)} %param.40, bf16[32,1024]{1,0:T(8,128)(2,1)S(1)} %copy-done.1), kind=kOutput, calls=%fused_computation.32 | convolution fusion | flops 268533760 | bytes 8781824 | tf_op jit(solution)/shard_map/dot_general | solution.py:183
  47.4 1.3 collective-permute-start
  49.8 5.8 %fusion.19 = bf16[8,4,5120]{2,1,0:T(4,128)(2,1)S(1)} fusion(bf16[8,4,1024]{2,1,0:T(4,128)(2,1)S(1)} %dot_general.41, bf16[1,1024,5120]{2,1,0:T(8,128)(2,1)} %param.38), kind=kOutput, calls=%fused_computation.19 | convolution fusion | flops 335708160 | bytes 10878976 | tf_op jit(solution)/shard_map/dot_general | solution.py:166
  55.9 4.3 %attend.5 = bf16[4,4096]{1,0:T(4,128)(2,1)S(1)} custom-call(bf16[8,4,5248]{2,1,0:T(4,128)(2,1)S(1)} %get-tuple-element.106.part_q.part_k.part_v.part_s, bf16[8,4,5248]{2,1,0:T(4,128)(2,1)S(1)} %get-tuple-element.106.part_q.part_k.part_v.part_s, bf16[8,4,5248]{2,1,0:T(4,128)(2,1)S(1)} %get-tuple-element.106.part_q.part_k.part_v.part_s, ...), custom_call_target="tpu_custom_call" | custom-call | tf_op jit(solution)/shard_map/attend/pallas_call | solution.py:90
  60.4 4.9 %fusion.47 = bf16[32,1024]{1,0:T(8,128)(2,1)S(1)} fusion(bf16[32,4096]{1,0:T(8,128)(2,1)S(1)} %get-tuple-element.107, bf16[1,4096,1024]{2,1,0:T(8,128)(2,1)} %param.40, bf16[32,1024]{1,0:T(8,128)(2,1)S(1)} %collective-permute-done), kind=kOutput, calls=%fused_computation.31 | convolution fusion | flops 268533760 | bytes 8781824 | tf_op jit(solution)/shard_map/dot_general | solution.py:183
  66.2 5.8 %fusion.22 = bf16[8,4,5120]{2,1,0:T(4,128)(2,1)S(1)} fusion(bf16[8,4,1024]{2,1,0:T(4,128)(2,1)S(1)} %dot_general.44, bf16[1,1024,5120]{2,1,0:T(8,128)(2,1)} %param.38), kind=kOutput, calls=%fused_computation.20 | convolution fusion | flops 335708160 | bytes 10878976 | tf_op jit(solution)/shard_map/dot_general | solution.py:166
  72.4 4.3 %attend.6 = bf16[4,4096]{1,0:T(4,128)(2,1)S(1)} custom-call(bf16[8,4,5248]{2,1,0:T(4,128)(2,1)S(1)} %get-tuple-element.108.part_q.part_k.part_v.part_s, bf16[8,4,5248]{2,1,0:T(4,128)(2,1)S(1)} %get-tuple-element.108.part_q.part_k.part_v.part_s, bf16[8,4,5248]{2,1,0:T(4,128)(2,1)S(1)} %get-tuple-element.108.part_q.part_k.part_v.part_s, ...), custom_call_target="tpu_custom_call" | custom-call | tf_op jit(solution)/shard_map/attend/pallas_call | solution.py:90
  77.0 4.9 %fusion.44 = bf16[32,1024]{1,0:T(8,128)(2,1)S(1)} fusion(bf16[32,4096]{1,0:T(8,128)(2,1)S(1)} %get-tuple-element.109, bf16[1,4096,1024]{2,1,0:T(8,128)(2,1)} %param.40, bf16[32,1024]{1,0:T(8,128)(2,1)S(1)} %collective-permute-done.1), kind=kOutput, calls=%fused_computation.30 | convolution fusion | flops 268533760 | bytes 8781824 | tf_op jit(solution)/shard_map/dot_general | solution.py:183
  82.8 5.8 %fusion.25 = bf16[8,4,5120]{2,1,0:T(4,128)(2,1)S(1)} fusion(bf16[8,4,1024]{2,1,0:T(4,128)(2,1)S(1)} %dot_general.47, bf16[1,1024,5120]{2,1,0:T(8,128)(2,1)} %param.38), kind=kOutput, calls=%fused_computation.21 | convolution fusion | flops 335708160 | bytes 10878976 | tf_op jit(solution)/shard_map/dot_general | solution.py:166
  89.0 4.3 %attend.7 = bf16[4,4096]{1,0:T(4,128)(2,1)S(1)} custom-call(bf16[8,4,5248]{2,1,0:T(4,128)(2,1)S(1)} %get-tuple-element.110.part_q.part_k.part_v.part_s, bf16[8,4,5248]{2,1,0:T(4,128)(2,1)S(1)} %get-tuple-element.110.part_q.part_k.part_v.part_s, bf16[8,4,5248]{2,1,0:T(4,128)(2,1)S(1)} %get-tuple-element.110.part_q.part_k.part_v.part_s, ...), custom_call_target="tpu_custom_call" | custom-call | tf_op jit(solution)/shard_map/attend/pallas_call | solution.py:90
  93.5 4.9 %fusion.41 = bf16[32,1024]{1,0:T(8,128)(2,1)S(1)} fusion(bf16[32,4096]{1,0:T(8,128)(2,1)S(1)} %get-tuple-element.111, bf16[1,4096,1024]{2,1,0:T(8,128)(2,1)} %param.40, bf16[32,1024]{1,0:T(8,128)(2,1)S(1)} %collective-permute-done.2), kind=kOutput, calls=%fused_computation.29 | convolution fusion | flops 268533760 | bytes 8781824 | tf_op jit(solution)/shard_map/dot_general | solution.py:183
  99.3 1.3 collective-permute-start.4
  101.3 10.6 %conditional.21 = (bf16[8,1,1024]{2,1,0:T(2,128)(2,1)S(1)}) conditional(s32[]{:T(128)} %convert_element_type.93, bf16[8,1,1024]{2,1,0:T(2,128)(2,1)S(1)} %get-tuple-element.103, bf16[8,1,1024]{2,1,0:T(2,128)(2,1)S(1)} %get-tuple-element.103), branch_computations={%region_24.25_spmd, %region_25.26_spmd} | conditional | bytes 131086 | solution.py:189
  102.6 9.3 %all_to_all.59 = bf16[8,2,512]{2,1,0:T(2,128)(2,1)S(1)} all-to-all(bf16[8,2,512]{2,1,0:T(2,128)(2,1)S(1)} %reshape.296), channel_id=1, replica_groups=mesh['pipe'=4,'mp'=8] {'mp'}, dimensions={0} | all-to-all | bytes 32768 | tf_op jit(solution)/shard_map/cond/branch_1_fun/all_to_all | solution.py:113
  111.9 72.3 %collective-permute-done.4 = bf16[8,32,1024]{2,1,0:T(8,128)(2,1)S(1)} collective-permute-done((bf16[8,32,1024]{2,1,0:T(8,128)(2,1)S(1)}, bf16[8,32,1024]{2,1,0:T(8,128)(2,1)S(1)}, u32[]{:S(2)}, u32[]{:S(2)}) %collective-permute-start.4) | collective-permute-done | bytes 524320 | tf_op jit(solution)/shard_map/ppermute | solution.py:203
  184.9 4.1 %fusion.74 = (f32[32]{0:T(128)S(1)}, f32[32,384]{1,0:T(8,128)S(1)}) fusion(bf16[8192,384]{1,0:T(8,128)(2,1)} %param.43, bf16[32,8192]{1,0:T(8,128)(2,1)S(1)} %bitcast.74, s32[32]{0:T(128)S(1)} %copy-done.3), kind=kOutput, calls=%fused_computation.101 | convolution fusion | flops 218379232 | bytes 6865152 | tf_op jit(solution)/shard_map/dot_general | solution.py:215
  189.2 9.7 %all_to_all.60 = f32[32,3,32]{2,1,0:T(4,128)S(1)} all-to-all(f32[32,3,32]{2,1,0:T(4,128)S(1)} %broadcast_in_dim.192), channel_id=1, replica_groups=mesh['pipe'=4,'mp'=8] {'pipe','mp'}, dimensions={0} | all-to-all | bytes 24576 | tf_op jit(solution)/shard_map/all_to_all | solution.py:113
  (89 shorter events, 13.3 us)
Async XLA Ops:
  0.6 100.0 %copy-start = (s32[32]{0:T(128)S(1)}, s32[32]{0:T(128)}, u32[]{:S(2)}) copy-start(s32[32]{0:T(128)} %param.36) | copy-start | bytes 388
  4.0 38.4 %copy-start.1 = (bf16[32,1024]{1,0:T(8,128)(2,1)S(1)}, bf16[32,1024]{1,0:T(8,128)(2,1)}, u32[]{:S(2)}) copy-start(bf16[32,1024]{1,0:T(8,128)(2,1)} %param.33) | copy-start | bytes 196612
  42.4 6.3 %copy-start.2 = (bf16[1024]{0:T(1024)(128)(2,1)S(1)}, bf16[1024]{0:T(1024)(128)(2,1)}, u32[]{:S(2)}) copy-start(bf16[1024]{0:T(1024)(128)(2,1)} %param.42) | copy-start | bytes 6148
  47.4 2.2 %collective-permute-start = (bf16[32,1024]{1,0:T(8,128)(2,1)S(1)}, bf16[32,1024]{1,0:T(8,128)(2,1)S(1)}, u32[]{:S(2)}, u32[]{:S(2)}) collective-permute-start(bf16[32,1024]{1,0:T(8,128)(2,1)S(1)} %fusion.50), channel_id=1, source_target_pairs={{0,8},{1,9},{2,10},{3,11},{4,12},{5,13},{6,14},{7,15}} | collective-permute-start | bytes 196616 | tf_op jit(solution)/shard_map/ppermute | solution.py:186
  65.3 0.7 collective-permute-start.1
  82.0 0.7 collective-permute-start.2
  93.5 7.1 %copy-start.3 = (s32[32]{0:T(128)S(1)}, s32[32]{0:T(128)}, u32[]{:S(2)}) copy-start(s32[32]{0:T(128)} %param.35) | copy-start | bytes 388
  98.5 0.7 collective-permute-start.3
  99.3 85.0 %collective-permute-start.4 = (bf16[8,32,1024]{2,1,0:T(8,128)(2,1)S(1)}, bf16[8,32,1024]{2,1,0:T(8,128)(2,1)S(1)}, u32[]{:S(2)}, u32[]{:S(2)}) collective-permute-start(bf16[8,32,1024]{2,1,0:T(8,128)(2,1)S(1)} %get-tuple-element.112), channel_id=1, source_target_pairs={{8,0},{24,16},{9,1},{25,17},{10,2},{26,18},{11,3},{27,19},{12,4},{... | collective-permute-start | bytes 1572872 | tf_op jit(solution)/shard_map/ppermute | solution.py:203

commit v2 on v1

v2 whole, which is shorter than its diff:
```python
import functools

import jax
import jax.numpy as jnp
import numpy as np
from jax import lax
from jax.experimental import pallas as pl
from jax.experimental.pallas import tpu as pltpu
from jax.sharding import PartitionSpec as P

HEADS = 32
KV_HEADS = 4
HEAD_DIM = 128
GROUP = HEADS // KV_HEADS
EPS = 1e-06
THETA = 1000000.0
LANES = 128
CHUNK = 512
GRANT = 16 * 1024 * 1024

VMEM = pl.BlockSpec(memory_space=pltpu.VMEM)
SMEM = pl.BlockSpec(memory_space=pltpu.SMEM)
HBM = pl.BlockSpec(memory_space=pltpu.HBM)
PARAMS = pltpu.CompilerParams(vmem_limit_bytes=GRANT)


def in_hbm(array):
    return pltpu.with_memory_space_constraint(array, pltpu.HBM)


def in_vmem(array):
    return pltpu.with_memory_space_constraint(array, pltpu.VMEM)


def column_copies(source, target, sem):
    return [
        pltpu.make_async_copy(
            source.at[:, pl.ds(i * CHUNK, CHUNK)], target.at[:, pl.ds(i * CHUNK, CHUNK)], sem.at[i]
        )
        for i in range(target.shape[1] // CHUNK)
    ]


def project_body(stream_ref, gain_ref, weight, out_ref, copies):
    peers, count, _ = out_ref.shape
    current = stream_ref[...].astype(jnp.float32)
    squares = jnp.sum(current * current, axis=1, keepdims=True)
    scaled = (current * gain_ref[...].astype(jnp.float32)).astype(jnp.bfloat16)
    high = squares.astype(jnp.bfloat16).astype(jnp.float32)
    middle = (squares - high).astype(jnp.bfloat16).astype(jnp.float32)
    low = squares - high - middle
    lane = lax.broadcasted_iota(jnp.int32, (current.shape[0], LANES), 1)
    tail = jnp.where(lane == 0, high, jnp.where(lane == 1, middle, jnp.where(lane == 2, low, 0.0)))

    def store(block, at):
        for j in range(peers):
            out_ref[j, :, at : at + block.shape[1]] = block[j * count : (j + 1) * count].astype(
                jnp.bfloat16
            )

    store(tail, weight.shape[1])
    for i in range(weight.shape[1] // CHUNK):
        if copies is not None:
            copies[i].wait()
        block = jnp.dot(
            scaled,
            weight[:, i * CHUNK : (i + 1) * CHUNK],
            preferred_element_type=jnp.float32,
        )
        store(block, i * CHUNK)


def project_first_kernel(stream_ref, gain_ref, source_ref, out_ref, weight_ref, sem):
    copies = column_copies(source_ref, weight_ref, sem)
    for copy in copies:
        copy.start()
    project_body(stream_ref, gain_ref, weight_ref, out_ref, copies)


def project_kernel(stream_ref, gain_ref, weight_ref, out_ref):
    project_body(stream_ref, gain_ref, weight_ref, out_ref, None)


def project_first(stream, gain, weight, peers):
    columns = weight.shape[1]
    count = stream.shape[0] // peers
    return pl.pallas_call(
        project_first_kernel,
        in_specs=[VMEM, VMEM, HBM],
        out_specs=[VMEM, VMEM],
        out_shape=[
            jax.ShapeDtypeStruct((peers, count, columns + LANES), jnp.bfloat16),
            pltpu.VMEM(weight.shape, weight.dtype),
        ],
        scratch_shapes=[pltpu.SemaphoreType.DMA((columns // CHUNK,))],
        compiler_params=PARAMS,
        name="project_first",
    )(stream, gain, in_hbm(weight))


def project(stream, gain, weight, peers):
    columns = weight.shape[1]
    count = stream.shape[0] // peers
    return pl.pallas_call(
        project_kernel,
        in_specs=[VMEM, VMEM, VMEM],
        out_specs=VMEM,
        out_shape=jax.ShapeDtypeStruct((peers, count, columns + LANES), jnp.bfloat16),
        compiler_params=PARAMS,
        name="project",
    )(stream, gain, in_vmem(weight))


def attend_body(lengths_ref, place_ref, parts_ref, bias_ref, frequency_ref, cache, out_ref, width, ready):
    count = out_ref.shape[0]
    length = cache.shape[3]
    query_cols = HEADS * HEAD_DIM
    key_cols = KV_HEADS * HEAD_DIM
    first = place_ref[0] * count
    at_row = lax.broadcasted_iota(jnp.int32, (count, HEAD_DIM), 0)
    positions = jnp.zeros((count, HEAD_DIM), jnp.int32)
    wide = (GROUP * count, count * length)
    rows = lax.broadcasted_iota(jnp.int32, wide, 0) % count
    columns = lax.broadcasted_iota(jnp.int32, wide, 1)
    visible = columns < 0
    for r in range(count):
        position = lengths_ref[first + r]
        positions = jnp.where(at_row == r, position, positions)
        mine = (rows == r) & (columns >= r * length) & (columns < r * length + position)
        visible = visible | mine
    angles = positions.astype(jnp.float32) * frequency_ref[...]
    lane = lax.broadcasted_iota(jnp.int32, (count, HEAD_DIM), 1)
    cosine = jnp.cos(angles)
    sine = jnp.sin(angles)
    sine = jnp.where(lane < HEAD_DIM // 2, -sine, sine)

    def total_of(at, size):
        acc = parts_ref[0, :, at : at + size].astype(jnp.float32)
        for j in range(1, parts_ref.shape[0]):
            acc = acc + parts_ref[j, :, at : at + size].astype(jnp.float32)
        return acc

    squares = jnp.sum(total_of(query_cols + 2 * key_cols, LANES), axis=1, keepdims=True)
    inverse = lax.rsqrt(squares / width + EPS)

    def columns_of(at):
        bias = bias_ref[:, at : at + HEAD_DIM].astype(jnp.float32)
        return total_of(at, HEAD_DIM) * inverse + bias

    def rotate(head):
        return head * cosine + pltpu.roll(head, HEAD_DIM // 2, 1) * sine

    scale = HEAD_DIM ** (-0.5)
    heads = []
    for k in range(KV_HEADS):
        stack = [rotate(columns_of((k * GROUP + g) * HEAD_DIM)) for g in range(GROUP)]
        queries = jnp.concatenate(stack, axis=0).astype(jnp.bfloat16)
        key_new = rotate(columns_of(query_cols + k * HEAD_DIM))
        key_new = key_new.astype(jnp.bfloat16).astype(jnp.float32)
        value_new = columns_of(query_cols + key_cols + k * HEAD_DIM)
        value_new = value_new.astype(jnp.bfloat16).astype(jnp.float32)
        heads.append((queries, key_new, value_new))
    ready()
    for k in range(KV_HEADS):
        queries, key_new, value_new = heads[k]
        keys = cache[:, 0, k].reshape(count * length, HEAD_DIM)
        values = cache[:, 1, k].reshape(count * length, HEAD_DIM)
        scores = (
            lax.dot_general(
                queries, keys, (((1,), (1,)), ((), ())), preferred_element_type=jnp.float32
            )
            * scale
        )
        tiled_key = jnp.concatenate([key_new] * GROUP, axis=0)
        tiled_value = jnp.concatenate([value_new] * GROUP, axis=0)
        self_score = (
            jnp.sum(queries.astype(jnp.float32) * tiled_key, axis=1, keepdims=True) * scale
        )
        top = jnp.max(jnp.where(visible, scores, -1e30), axis=1, keepdims=True)
        top = jnp.maximum(top, self_score)
        weights = jnp.where(visible, jnp.exp(scores - top), 0.0)
        self_weight = jnp.exp(self_score - top)
        total = jnp.sum(weights, axis=1, keepdims=True) + self_weight
        summed = jnp.dot(weights.astype(jnp.bfloat16), values, preferred_element_type=jnp.float32)
        summed = summed + self_weight.astype(jnp.bfloat16).astype(jnp.float32) * tiled_value
        attended = summed / total
        for g in range(GROUP):
            at = (k * GROUP + g) * HEAD_DIM
            out_ref[:, at : at + HEAD_DIM] = attended[g * count : (g + 1) * count].astype(
                jnp.bfloat16
            )


def attend_first_kernel(
    lengths_ref, place_ref, parts_ref, bias_ref, frequency_ref, cache_hbm, weight_hbm,
    out_ref, cache_ref, weight_ref, sem, *, width,
):
    copy_cache = pltpu.make_async_copy(cache_hbm, cache_ref, sem.at[0])
    copy_weight = pltpu.make_async_copy(weight_hbm, weight_ref, sem.at[1])
    copy_cache.start()
    copy_weight.start()
    attend_body(
        lengths_ref, place_ref, parts_ref, bias_ref, frequency_ref, cache_ref, out_ref, width,
        copy_cache.wait,
    )
    copy_weight.wait()


def attend_kernel(
    lengths_ref, place_ref, parts_ref, bias_ref, frequency_ref, cache_ref, out_ref, *, width
):
    attend_body(
        lengths_ref, place_ref, parts_ref, bias_ref, frequency_ref, cache_ref, out_ref, width,
        lambda: None,
    )


def attend_first(lengths, place, parts, bias, frequency, cache, weight, width):
    count = parts.shape[1]
    return pl.pallas_call(
        functools.partial(attend_first_kernel, width=width),
        in_specs=[SMEM, SMEM, VMEM, VMEM, VMEM, HBM, HBM],
        out_specs=[VMEM, VMEM, VMEM],
        out_shape=[
            jax.ShapeDtypeStruct((count, HEADS * HEAD_DIM), jnp.bfloat16),
            pltpu.VMEM(cache.shape, cache.dtype),
            pltpu.VMEM(weight.shape, weight.dtype),
        ],
        scratch_shapes=[pltpu.SemaphoreType.DMA((2,))],
        compiler_params=PARAMS,
        name="attend_first",
    )(lengths, place, parts, bias, frequency, in_hbm(cache), in_hbm(weight))


def attend(lengths, place, parts, bias, frequency, cache, width):
    count = parts.shape[1]
    return pl.pallas_call(
        functools.partial(attend_kernel, width=width),
        in_specs=[SMEM, SMEM, VMEM, VMEM, VMEM, VMEM],
        out_specs=VMEM,
        out_shape=jax.ShapeDtypeStruct((count, HEADS * HEAD_DIM), jnp.bfloat16),
        compiler_params=PARAMS,
        name="attend",
    )(lengths, place, parts, bias, frequency, in_vmem(cache))


def combine_kernel(gathered_ref, weight_ref, stream_ref, out_ref):
    peers = gathered_ref.shape[0]
    blocks = [gathered_ref[j].astype(jnp.float32) for j in range(peers)]
    gathered = jnp.concatenate(blocks, axis=0).astype(jnp.bfloat16)
    for at in range(0, out_ref.shape[1], 256):
        update = jnp.dot(
            gathered, weight_ref[:, at : at + 256], preferred_element_type=jnp.float32
        )
        current = stream_ref[:, at : at + 256].astype(jnp.float32)
        out_ref[:, at : at + 256] = (current + update).astype(jnp.bfloat16)


def combine(gathered, weight, stream):
    return pl.pallas_call(
        combine_kernel,
        in_specs=[VMEM, VMEM, VMEM],
        out_specs=VMEM,
        out_shape=jax.ShapeDtypeStruct(stream.shape, jnp.bfloat16),
        compiler_params=PARAMS,
        name="combine",
    )(gathered, in_vmem(weight), stream)


def load_kernel(idle_ref, source_ref, out_ref, sem):
    @pl.when(idle_ref[0] == 1)
    def _():
        copy = pltpu.make_async_copy(source_ref, out_ref, sem.at[0])
        copy.start()
        copy.wait()


def load_rest_kernel(idle_ref, source_ref, before_ref, out_ref, sem):
    del before_ref
    load_kernel(idle_ref, source_ref, out_ref, sem)


def load(idle, weight, before=None):
    first = before is None
    return pl.pallas_call(
        load_kernel if first else load_rest_kernel,
        in_specs=[SMEM, HBM] + ([] if first else [VMEM]),
        out_specs=VMEM,
        out_shape=pltpu.VMEM(weight.shape, weight.dtype),
        scratch_shapes=[pltpu.SemaphoreType.DMA((1,))],
        compiler_params=PARAMS,
        input_output_aliases={} if first else {2: 0},
        name="load" if first else "load_rest",
    )(idle, in_hbm(weight), *([] if first else [in_vmem(before)]))


def logits_kernel(
    assign_ref, tokens_ref, place_ref, rows_ref, over_ref, gain_ref, weight_ref,
    logits_ref, stats_ref, scratch_ref, *, width,
):
    pieces, requests, share = rows_ref.shape
    vocab = weight_ref.shape[1]
    own = place_ref[1] == 1
    squares = jnp.zeros((requests, 1), jnp.float32)
    for m in range(pieces):
        current = jnp.where(own, rows_ref[m], over_ref[m]).astype(jnp.float32)
        squares = squares + jnp.sum(current * current, axis=1, keepdims=True)
    inverse = lax.rsqrt(squares / width + EPS)
    logits = jnp.zeros((requests, vocab), jnp.float32)
    for m in range(pieces):
        current = jnp.where(own, rows_ref[m], over_ref[m]).astype(jnp.float32)
        normed = (current * gain_ref[m].astype(jnp.float32) * inverse).astype(jnp.bfloat16)
        logits = logits + jnp.dot(
            normed, weight_ref[m * share : (m + 1) * share], preferred_element_type=jnp.float32
        )
    scratch_ref[...] = logits
    row = lax.broadcasted_iota(jnp.int32, (requests, vocab), 0)
    targets = jnp.zeros((requests, vocab), jnp.int32)
    for s in range(requests):
        request = assign_ref[s]
        logits_ref[pl.ds(s, 1), :] = scratch_ref[pl.ds(request, 1), :]
        targets = jnp.where(row == s, tokens_ref[request] - place_ref[0], targets)
    ordered = logits_ref[...]
    column = lax.broadcasted_iota(jnp.int32, (requests, vocab), 1)
    picked = jnp.sum(jnp.where(column == targets, ordered, 0.0), axis=1, keepdims=True)
    top = jnp.max(ordered, axis=1, keepdims=True)
    total = jnp.sum(jnp.exp(ordered - top), axis=1, keepdims=True)
    wide = (requests, stats_ref.shape[1])
    lane = lax.broadcasted_iota(jnp.int32, wide, 1) - lax.broadcasted_iota(jnp.int32, wide, 0)
    spread_out = jnp.where(lane == 0, top, 0.0)
    spread_out = jnp.where(lane == requests, total, spread_out)
    spread_out = jnp.where(lane == 2 * requests, picked, spread_out)
    stats_ref[...] = jnp.sum(spread_out, axis=0, keepdims=True)


def final_logits(assign, tokens, place, rows, over, gain, weight, width):
    requests = rows.shape[1]
    vocab = weight.shape[1]
    lanes = -(-3 * requests // LANES) * LANES
    return pl.pallas_call(
        functools.partial(logits_kernel, width=width),
        in_specs=[SMEM, SMEM, SMEM, VMEM, VMEM, VMEM, VMEM],
        out_specs=[VMEM, VMEM],
        out_shape=[
            jax.ShapeDtypeStruct((requests, vocab), jnp.float32),
            jax.ShapeDtypeStruct((1, lanes), jnp.float32),
        ],
        scratch_shapes=[pltpu.VMEM((requests, vocab), jnp.float32)],
        compiler_params=PARAMS,
        name="final_logits",
    )(assign, tokens, place, rows, over, gain, in_vmem(weight))


def finish_kernel(logits_ref, stats_ref, out_ref, chosen_ref):
    requests = logits_ref.shape[0]
    stats = stats_ref[...]
    lanes = stats.shape[1]
    top = jnp.max(stats, axis=0, keepdims=True)
    sums = pltpu.roll(stats, lanes - requests, 1)
    picks = pltpu.roll(stats, lanes - 2 * requests, 1)
    total = jnp.sum(sums * jnp.exp(jnp.minimum(stats - top, 0.0)), axis=0, keepdims=True)
    lane = lax.broadcasted_iota(jnp.int32, (1, lanes), 1)
    total = jnp.where(lane < requests, total, 1.0)
    log_total = jnp.where(lane < requests, top, 0.0) + jnp.log(total)
    chosen_ref[...] = (jnp.sum(picks, axis=0, keepdims=True) - log_total)[:, :requests]
    wide = (requests, lanes)
    here = lax.broadcasted_iota(jnp.int32, wide, 1) == lax.broadcasted_iota(jnp.int32, wide, 0)
    column = jnp.sum(jnp.where(here, log_total, 0.0), axis=1, keepdims=True)
    out_ref[...] = logits_ref[...] - column


def finish(logits, stats):
    requests = logits.shape[0]
    return pl.pallas_call(
        finish_kernel,
        in_specs=[VMEM, VMEM],
        out_specs=[VMEM, VMEM],
        out_shape=[
            jax.ShapeDtypeStruct(logits.shape, jnp.float32),
            jax.ShapeDtypeStruct((1, requests), jnp.float32),
        ],
        compiler_params=PARAMS,
        name="finish",
    )(logits, stats)


def exchange(blocks, axis):
    return lax.all_to_all(blocks, axis, 0, 0, tiled=True)


def spread(value, axis):
    blocks = jnp.broadcast_to(value[None], (lax.axis_size(axis),) + value.shape)
    return exchange(blocks, axis)


def local(
    hidden_in,
    lengths,
    assign,
    token_ids,
    attn_gain,
    qkv_weight,
    qkv_bias,
    out_weight,
    kv_cache,
    final_gain,
    head_weight,
):
    sections = lax.axis_size("pipe")
    section = lax.axis_index("pipe")
    peers = lax.axis_size("mp")
    share = hidden_in.shape[1]
    width = share * peers
    place = lax.axis_index("mp").astype(jnp.int32).reshape(1)
    exponents = np.arange(HEAD_DIM // 2, dtype=np.float64) * 2.0 / HEAD_DIM
    frequency = np.tile(THETA ** (-exponents), 2)[None, :].astype(np.float32)
    weight_in = qkv_weight[0]
    weight_out = out_weight[0]
    cache = kv_cache[0]

    gain_blocks = jnp.broadcast_to(final_gain[None, None], (peers, 1, share))
    gain_full = lax.cond(section != 0, lambda b: exchange(b, "mp"), lambda b: b, gain_blocks)

    def only_active(active, fn, other, value):
        return lax.cond(active, fn, other, value)

    stream = hidden_in
    for layer in range(sections):
        active = section == layer
        if layer == 0:
            payload, weight_in = project_first(stream, attn_gain, weight_in, peers)
        else:
            payload = project(stream, attn_gain, weight_in, peers)
        parts = lax.cond(active, lambda b: exchange(b, "mp"), lambda b: b, payload)
        if layer == 0:
            attended, cache, weight_out = attend_first(
                lengths, place, parts, qkv_bias, frequency, cache, weight_out, width
            )
        else:
            attended = attend(lengths, place, parts, qkv_bias, frequency, cache, width)
        gathered = lax.cond(
            active,
            lambda b: spread(b, "mp"),
            lambda b: jnp.broadcast_to(b[None], (peers,) + b.shape),
            attended,
        )
        stream = combine(gathered, weight_out, stream)
        if layer + 1 < sections:
            stream = lax.ppermute(stream, "pipe", [(layer, layer + 1)])
        if layer == 0:
            gain_full, stream = lax.optimization_barrier((gain_full, stream))
            gain_full = lax.cond(section == 0, lambda b: exchange(b, "mp"), lambda b: b, gain_full)
            weight_head = load((section != 0).astype(jnp.int32).reshape(1), head_weight)
        if layer == 1:
            weight_head = load((section == 0).astype(jnp.int32).reshape(1), head_weight, weight_head)

    last = sections - 1
    odd = section % 2 == 1
    arrived = stream
    for target in range(1, last, 2):
        copied = lax.ppermute(stream, "pipe", [(last, target)])
        arrived = jnp.where(section == target, copied, arrived)
    rows = lax.cond(
        odd,
        lambda b: spread(b, "mp"),
        lambda b: jnp.broadcast_to(b[None], (peers,) + b.shape),
        arrived,
    )
    over = lax.ppermute(rows, "pipe", [(i, i - 1) for i in range(1, sections, 2)])

    vocab_first = lax.axis_index(("pipe", "mp")) * head_weight.shape[1]
    head_place = jnp.stack([vocab_first, odd.astype(vocab_first.dtype)]).astype(jnp.int32)
    logits, stats = final_logits(
        assign, token_ids, head_place, rows, over, gain_full, weight_head, width
    )
    stats = spread(stats, ("pipe", "mp"))
    logprobs, chosen = finish(logits, stats.reshape(stats.shape[0], stats.shape[2]))
    return logprobs, chosen[0]


def solution(mesh):
    return jax.shard_map(
        local,
        mesh=mesh,
        in_specs=(
            P(None, "mp"),
            P(),
            P(),
            P(),
            P("pipe", "mp"),
            P("pipe", "mp", None),
            P("pipe", None),
            P("pipe", None, "mp"),
            P("pipe", "mp", None, None, None, None),
            P("mp"),
            P(None, ("pipe", "mp")),
        ),
        out_specs=(P(None, ("pipe", "mp")), P()),
        check_vma=False,
    )
```

time: 201 us -> 199 us (0.990)
  matrix products: 47.3 us -> 0 us
  local copies, waits for them, and re-layouts: 3.23 us -> 40.7 us
  Pallas kernels: 17.1 us -> 32.8 us
  other arithmetic: 7.41 us -> 0.82 us
  waiting for transfers between devices: 73.2 us -> 68.4 us
  blocking collectives: 46 us -> 49.7 us
    dot_general x9 -> x0, matrix products: 47.3 us -> none  [the longest x4 23.3 us: local(): jnp.dot(scaled, weight_in, preferred_element_type=jnp.float32)]
    unnamed x9 -> x42, local copies, waits for them, and re-layouts: 0.04 us -> 39.7 us
    pallas_call x4 -> x16, Pallas kernels: 17.1 us -> 32.8 us  [the longest x3 6.26 us: attend(): pl.pallas_call(functools.partial(attend_kernel, width=width), in_specs=[S...]
    ppermute x1, waiting for transfers between devices: 72.3 us -> 67.6 us  [local(): lax.ppermute(rows, 'pipe', [(i, i - 1) for i in range(1, sections, 2)])]
    all_to_all x4, blocking collectives: 46 us -> 49.7 us  [exchange(): return lax.all_to_all(blocks, axis, 0, 0, tiled=True)]
  transfers between devices with their start and end apart: 5 -> 5, of which waited for: 2 -> 2; matrix products, arithmetic and copies ran while one was open for 1% -> 1% of each run, Pallas kernels for 0% -> 1%
where the time goes in v2:
time: 199 us; the launch traced here: 198 us
  waiting for transfers between devices  68.4 us (34%)
  blocking collectives  49.7 us (25%)
  local copies, waits for them, and re-layouts  40.7 us (20%)
  Pallas kernels  32.8 us (16%)
  starting transfers between devices  4.77 us (2%)
    ppermute x1, waiting for transfers between devices, local(): lax.ppermute(rows, 'pipe', [(i, i - 1) for i in range(1, sections, 2)])  67.6 us
    all_to_all x4, blocking collectives, exchange(): return lax.all_to_all(blocks, axis, 0, 0, tiled=True)  49.7 us
    unnamed x42, local copies, waits for them, and re-layouts  39.7 us
    pallas_call x3, Pallas kernels, attend(): pl.pallas_call(functools.partial(attend_kernel, width=width), in_specs=[S...  6.26 us
    pallas_call x4, Pallas kernels, combine(): pl.pallas_call(combine_kernel, in_specs=[VMEM, VMEM, VMEM], out_specs=VME...  6.15 us
    pallas_call x3, Pallas kernels, project(): pl.pallas_call(project_kernel, in_specs=[VMEM, VMEM, VMEM], out_specs=VME...  5.72 us
    pallas_call x1, Pallas kernels, attend_first(): pl.pallas_call(functools.partial(attend_first_kernel, width=width), in_sp...  4.59 us
    pallas_call x1, Pallas kernels, project_first(): pl.pallas_call(project_first_kernel, in_specs=[VMEM, VMEM, HBM], out_spec...  4.47 us
  transfers between devices with their start and end apart: 5, of which 2 were waited for; matrix products, arithmetic and copies ran while one was open for 1% of the time, Pallas kernels for 1%

profile of v2, /device:TPU:0, one launch (start us, length us, event | category | flops | bytes accessed | tf_op | source)
XLA Modules:
  0.0 198.4 jit_solution(589279818643033001)
XLA Ops:
  2.2 4.5 %project_first.1 = (bf16[8,4,5248]{2,1,0:T(4,128)(2,1)S(1)}, bf16[1024,5120]{1,0:T(8,128)(2,1)S(1)}) custom-call(bf16[32,1024]{1,0:T(8,128)(2,1)S(1)} %copy-done.12, bf16[1,1024]{1,0:T(2,128)(2,1)S(1)} %copy-done.14, bf16[1024,5120]{1,0:T(8,128)(2,1)} %bitcast.13), custom_call_target="tpu_custom_call" | custom-call | tf_op jit(solution)/shard_map/project_first/pallas_call | solution.py:87
  6.7 4.0 %copy-done.5 = bf16[1024,5120]{1,0:T(8,128)(2,1)} copy-done((bf16[1024,5120]{1,0:T(8,128)(2,1)}, bf16[1024,5120]{1,0:T(8,128)(2,1)S(1)}, u32[]{:S(2)}) %copy-start.5) | copy-done | bytes 10485784
  10.7 16.3 %conditional.12 = (bf16[8,4,5248]{2,1,0:T(4,128)(2,1)S(1)}) conditional(s32[]{:T(128)} %convert_element_type.31, bf16[8,4,5248]{2,1,0:T(4,128)(2,1)S(1)} %get-tuple-element.68, bf16[8,4,5248]{2,1,0:T(4,128)(2,1)S(1)} %get-tuple-element.68), branch_computations={%region_2.0_spmd, %region_3.0_spmd} | conditional | bytes 1343496 | solution.py:434
  10.8 16.2 %all_to_all.50 = bf16[8,4,5248]{2,1,0:T(4,128)(2,1)S(1)} all-to-all(bf16[8,4,5248]{2,1,0:T(4,128)(2,1)S(1)} %copy.38), channel_id=1, replica_groups=mesh['pipe'=4,'mp'=8] {'mp'}, dimensions={0} | all-to-all | bytes 671744 | tf_op jit(solution)/shard_map/cond/branch_1_fun/all_to_all | solution.py:388
  27.0 4.6 %attend_first.1 = (bf16[4,4096]{1,0:T(4,128)(2,1)S(1)}, bf16[4,2,4,256,128]{4,3,2,1,0:T(8,128)(2,1)S(1)}, bf16[4096,1024]{1,0:T(8,128)(2,1)S(1)}) custom-call(s32[32]{0:T(128)S(1)} %copy-done.16, s32[1]{0:T(128)} %bitcast.2.place_ref, bf16[8,4,5248]{2,1,0:T(4,128)(2,1)S(1)} %get-tuple-element.80.parts_ref, bf16[1,5120]{1,0:T(2,128)(2,1)S(1)} %copy-done.11, ...), custom_call_target="tpu_custom_call" | custom-call | tf_op jit(solution)/shard_map/attend_first/pallas_call | solution.py:220
  31.6 3.3 %copy-done = bf16[4096,1024]{1,0:T(8,128)(2,1)} copy-done((bf16[4096,1024]{1,0:T(8,128)(2,1)}, bf16[4096,1024]{1,0:T(8,128)(2,1)S(1)}, u32[]{:S(2)}) %copy-start) | copy-done | bytes 8388632
  34.9 10.9 %conditional.13 = (bf16[8,4,4096]{2,1,0:T(4,128)(2,1)S(1)}) conditional(s32[]{:T(128)} %convert_element_type.31, bf16[4,4096]{1,0:T(4,128)(2,1)S(1)} %get-tuple-element.69, bf16[4,4096]{1,0:T(4,128)(2,1)S(1)} %get-tuple-element.69), branch_computations={%region_4.0_spmd, %region_5.0_spmd} | conditional | bytes 819208 | solution.py:441
  35.0 10.9 %all_to_all.51 = bf16[8,4,4096]{2,1,0:T(4,128)(2,1)S(1)} all-to-all(bf16[8,4,4096]{2,1,0:T(4,128)(2,1)S(1)} %broadcast_in_dim.32), channel_id=1, replica_groups=mesh['pipe'=4,'mp'=8] {'mp'}, dimensions={0} | all-to-all | bytes 524288 | tf_op jit(solution)/shard_map/cond/branch_1_fun/all_to_all | solution.py:388
  45.8 3.4 %copy-done.1 = bf16[4096,1024]{1,0:T(8,128)(2,1)S(1)} copy-done((bf16[4096,1024]{1,0:T(8,128)(2,1)S(1)}, bf16[4096,1024]{1,0:T(8,128)(2,1)}, u32[]{:S(2)}) %copy-start.1) | copy-done | bytes 8388632
  52.9 4.0 %copy-done.6 = bf16[1024,5120]{1,0:T(8,128)(2,1)S(1)} copy-done((bf16[1024,5120]{1,0:T(8,128)(2,1)S(1)}, bf16[1024,5120]{1,0:T(8,128)(2,1)}, u32[]{:S(2)}) %copy-start.6) | copy-done | bytes 10485784
  58.8 2.1 %attend.3 = bf16[4,4096]{1,0:T(4,128)(2,1)S(1)} custom-call(s32[32]{0:T(128)S(1)} %copy-done.16, s32[1]{0:T(128)} %bitcast.2.place_ref, bf16[8,4,5248]{2,1,0:T(4,128)(2,1)S(1)} %get-tuple-element.82.parts_ref, bf16[1,5120]{1,0:T(2,128)(2,1)S(1)} %copy-done.11, f32[1,128]{1,0:T(1,128)S(1)} %copy-done.17, ...), custom_call_target="tpu_custom_call" | custom-call | tf_op jit(solution)/shard_map/attend/pallas_call | solution.py:237
  61.0 3.4 %copy-done.2 = bf16[4096,1024]{1,0:T(8,128)(2,1)S(1)} copy-done((bf16[4096,1024]{1,0:T(8,128)(2,1)S(1)}, bf16[4096,1024]{1,0:T(8,128)(2,1)}, u32[]{:S(2)}) %copy-start.2) | copy-done | bytes 8388632
  66.7 4.0 %copy-done.7 = bf16[1024,5120]{1,0:T(8,128)(2,1)S(1)} copy-done((bf16[1024,5120]{1,0:T(8,128)(2,1)S(1)}, bf16[1024,5120]{1,0:T(8,128)(2,1)}, u32[]{:S(2)}) %copy-start.7) | copy-done | bytes 10485784
  74.8 3.4 %copy-done.3 = bf16[4096,1024]{1,0:T(8,128)(2,1)S(1)} copy-done((bf16[4096,1024]{1,0:T(8,128)(2,1)S(1)}, bf16[4096,1024]{1,0:T(8,128)(2,1)}, u32[]{:S(2)}) %copy-start.3) | copy-done | bytes 8388632
  80.5 4.0 %copy-done.8 = bf16[1024,5120]{1,0:T(8,128)(2,1)S(1)} copy-done((bf16[1024,5120]{1,0:T(8,128)(2,1)S(1)}, bf16[1024,5120]{1,0:T(8,128)(2,1)}, u32[]{:S(2)}) %copy-start.8) | copy-done | bytes 10485784
  86.4 2.1 %attend.5 = bf16[4,4096]{1,0:T(4,128)(2,1)S(1)} custom-call(s32[32]{0:T(128)S(1)} %copy-done.16, s32[1]{0:T(128)} %bitcast.2.place_ref, bf16[8,4,5248]{2,1,0:T(4,128)(2,1)S(1)} %get-tuple-element.86.parts_ref, bf16[1,5120]{1,0:T(2,128)(2,1)S(1)} %copy-done.11, f32[1,128]{1,0:T(1,128)S(1)} %copy-done.17, ...), custom_call_target="tpu_custom_call" | custom-call | tf_op jit(solution)/shard_map/attend/pallas_call | solution.py:237
  88.6 3.4 %copy-done.4 = bf16[4096,1024]{1,0:T(8,128)(2,1)S(1)} copy-done((bf16[4096,1024]{1,0:T(8,128)(2,1)S(1)}, bf16[4096,1024]{1,0:T(8,128)(2,1)}, u32[]{:S(2)}) %copy-start.4) | copy-done | bytes 8388632
  95.7 2.8 %load_rest.1.weight_ref = bf16[8192,384]{1,0:T(8,128)(2,1)S(1)} custom-call(s32[1]{0:T(128)} %bitcast.6.idle_ref, bf16[8192,384]{1,0:T(8,128)(2,1)} %source_ref.3, bf16[8192,384]{1,0:T(8,128)(2,1)S(1)} %load.1.before_ref), custom_call_target="tpu_custom_call", output_to_operand_aliasing={{}: (2, {})} | custom-call | tf_op jit(solution)/shard_map/load_rest/pallas_call | solution.py:285
  98.5 2.6 %copy-done.9 = bf16[8192,384]{1,0:T(8,128)(2,1)} copy-done((bf16[8192,384]{1,0:T(8,128)(2,1)}, bf16[8192,384]{1,0:T(8,128)(2,1)S(1)}, u32[]{:S(2)}) %copy-start.9) | copy-done | bytes 6291480
  101.2 10.6 %conditional.21 = (bf16[8,1,1024]{2,1,0:T(2,128)(2,1)S(1)}) conditional(s32[]{:T(128)} %convert_element_type.31, bf16[8,1,1024]{2,1,0:T(2,128)(2,1)S(1)} %get-tuple-element.79, bf16[8,1,1024]{2,1,0:T(2,128)(2,1)S(1)} %get-tuple-element.79), branch_computations={%region_20.21_spmd, %region_21.22_spmd} | conditional | bytes 131086 | solution.py:452
  102.5 9.3 %all_to_all.59 = bf16[8,2,512]{2,1,0:T(2,128)(2,1)S(1)} all-to-all(bf16[8,2,512]{2,1,0:T(2,128)(2,1)S(1)} %reshape.38), channel_id=1, replica_groups=mesh['pipe'=4,'mp'=8] {'mp'}, dimensions={0} | all-to-all | bytes 32768 | tf_op jit(solution)/shard_map/cond/branch_1_fun/all_to_all | solution.py:388
  111.8 67.6 %collective-permute-done.4.over_ref = bf16[8,32,1024]{2,1,0:T(8,128)(2,1)S(1)} collective-permute-done((bf16[8,32,1024]{2,1,0:T(8,128)(2,1)S(1)}, bf16[8,32,1024]{2,1,0:T(8,128)(2,1)S(1)}, u32[]{:S(2)}, u32[]{:S(2)}) %collective-permute-start.4) | collective-permute-done | bytes 524320 | tf_op jit(solution)/shard_map/ppermute | solution.py:469
  179.3 2.8 %copy-done.10 = bf16[8192,384]{1,0:T(8,128)(2,1)S(1)} copy-done((bf16[8192,384]{1,0:T(8,128)(2,1)S(1)}, bf16[8192,384]{1,0:T(8,128)(2,1)}, u32[]{:S(2)}) %copy-start.10) | copy-done | bytes 6291480
  184.1 13.4 %all_to_all.60 = f32[32,1,128]{2,1,0:T(1,128)S(1)} all-to-all(f32[32,1,128]{2,1,0:T(1,128)S(1)} %broadcast_in_dim.58), channel_id=1, replica_groups=mesh['pipe'=4,'mp'=8] {'pipe','mp'}, dimensions={0} | all-to-all | bytes 32768 | tf_op jit(solution)/shard_map/all_to_all | solution.py:388
  (73 shorter events, 26.1 us)
Async XLA Ops:
  0.6 26.4 %copy-start.17 = (f32[1,128]{1,0:T(1,128)S(1)}, f32[1,128]{1,0:T(1,128)}, u32[]{:S(2)}) copy-start(f32[1,128]{1,0:T(1,128)} %constant.31.clone.frequency_ref) | copy-start | bytes 1540
  0.6 26.3 %copy-start.11 = (bf16[1,5120]{1,0:T(2,128)(2,1)S(1)}, bf16[1,5120]{1,0:T(2,128)(2,1)}, u32[]{:S(2)}) copy-start(bf16[1,5120]{1,0:T(2,128)(2,1)} %bias_ref.7) | copy-start | bytes 30724
  2.2 24.8 %copy-start.16 = (s32[32]{0:T(128)S(1)}, s32[32]{0:T(128)}, u32[]{:S(2)}) copy-start(s32[32]{0:T(128)} %lengths_ref.7) | copy-start | bytes 388
  6.7 4.0 %copy-start.5 = (bf16[1024,5120]{1,0:T(8,128)(2,1)}, bf16[1024,5120]{1,0:T(8,128)(2,1)S(1)}, u32[]{:S(2)}) copy-start(bf16[1024,5120]{1,0:T(8,128)(2,1)S(1)} %get-tuple-element.72.weight_ref) | copy-start | bytes 31457284
  27.0 18.8 %copy-start.13 = (bf16[32,1024]{1,0:T(8,128)(2,1)S(1)}, bf16[32,1024]{1,0:T(8,128)(2,1)}, u32[]{:S(2)}) copy-start(bf16[32,1024]{1,0:T(8,128)(2,1)} %stream_ref.3) | copy-start | bytes 196612
  31.6 3.3 %copy-start = (bf16[4096,1024]{1,0:T(8,128)(2,1)}, bf16[4096,1024]{1,0:T(8,128)(2,1)S(1)}, u32[]{:S(2)}) copy-start(bf16[4096,1024]{1,0:T(8,128)(2,1)S(1)} %get-tuple-element.70.weight_ref) | copy-start | bytes 25165828
  34.9 17.2 %copy-start.20 = (bf16[1024]{0:T(1024)(128)(2,1)S(1)}, bf16[1024]{0:T(1024)(128)(2,1)}, u32[]{:S(2)}) copy-start(bf16[1024]{0:T(1024)(128)(2,1)} %param.43) | copy-start | bytes 6148
  34.9 18.0 %copy-start.15 = (bf16[1,1024]{1,0:T(2,128)(2,1)S(1)}, bf16[1,1024]{1,0:T(2,128)(2,1)}, u32[]{:S(2)}) copy-start(bf16[1,1024]{1,0:T(2,128)(2,1)} %gain_ref.7) | copy-start | bytes 6148
  45.8 3.4 %copy-start.1 = (bf16[4096,1024]{1,0:T(8,128)(2,1)S(1)}, bf16[4096,1024]{1,0:T(8,128)(2,1)}, u32[]{:S(2)}) copy-start(bf16[4096,1024]{1,0:T(8,128)(2,1)} %copy-done) | copy-start | bytes 25165828
  50.7 2.2 %collective-permute-start = (bf16[32,1024]{1,0:T(8,128)(2,1)S(1)}, bf16[32,1024]{1,0:T(8,128)(2,1)S(1)}, u32[]{:S(2)}, u32[]{:S(2)}) collective-permute-start(bf16[32,1024]{1,0:T(8,128)(2,1)S(1)} %combine.4), channel_id=1, source_target_pairs={{0,8},{1,9},{2,10},{3,11},{4,12},{5,13},{6,14},{7,15}} | collective-permute-start | bytes 196616 | tf_op jit(solution)/shard_map/ppermute | solution.py:449
  52.9 4.0 %copy-start.6 = (bf16[1024,5120]{1,0:T(8,128)(2,1)S(1)}, bf16[1024,5120]{1,0:T(8,128)(2,1)}, u32[]{:S(2)}) copy-start(bf16[1024,5120]{1,0:T(8,128)(2,1)} %copy-done.5) | copy-start | bytes 31457284
  61.0 3.4 %copy-start.2 = (bf16[4096,1024]{1,0:T(8,128)(2,1)S(1)}, bf16[4096,1024]{1,0:T(8,128)(2,1)}, u32[]{:S(2)}) copy-start(bf16[4096,1024]{1,0:T(8,128)(2,1)} %copy-done) | copy-start | bytes 25165828
  66.0 0.7 collective-permute-start.1
  66.6 4.0 %copy-start.7 = (bf16[1024,5120]{1,0:T(8,128)(2,1)S(1)}, bf16[1024,5120]{1,0:T(8,128)(2,1)}, u32[]{:S(2)}) copy-start(bf16[1024,5120]{1,0:T(8,128)(2,1)} %copy-done.5) | copy-start | bytes 31457284
  74.7 3.4 %copy-start.3 = (bf16[4096,1024]{1,0:T(8,128)(2,1)S(1)}, bf16[4096,1024]{1,0:T(8,128)(2,1)}, u32[]{:S(2)}) copy-start(bf16[4096,1024]{1,0:T(8,128)(2,1)} %copy-done) | copy-start | bytes 25165828
  79.7 0.9 collective-permute-start.2
  80.5 4.0 %copy-start.8 = (bf16[1024,5120]{1,0:T(8,128)(2,1)S(1)}, bf16[1024,5120]{1,0:T(8,128)(2,1)}, u32[]{:S(2)}) copy-start(bf16[1024,5120]{1,0:T(8,128)(2,1)} %copy-done.5) | copy-start | bytes 31457284
  88.6 3.4 %copy-start.4 = (bf16[4096,1024]{1,0:T(8,128)(2,1)S(1)}, bf16[4096,1024]{1,0:T(8,128)(2,1)}, u32[]{:S(2)}) copy-start(bf16[4096,1024]{1,0:T(8,128)(2,1)} %copy-done) | copy-start | bytes 25165828
  93.6 0.7 collective-permute-start.3
  94.4 85.0 %collective-permute-start.4 = (bf16[8,32,1024]{2,1,0:T(8,128)(2,1)S(1)}, bf16[8,32,1024]{2,1,0:T(8,128)(2,1)S(1)}, u32[]{:S(2)}, u32[]{:S(2)}) collective-permute-start(bf16[8,32,1024]{2,1,0:T(8,128)(2,1)S(1)} %get-tuple-element.88.rows_ref), channel_id=1, source_target_pairs={{8,0},{24,16},{9,1},{25,17},{10,2},{26,18},{11,3},{27,19},{12,4},{... | collective-permute-start | bytes 1572872 | tf_op jit(solution)/shard_map/ppermute | solution.py:469
  95.7 83.7 %copy-start.18 = (s32[32]{0:T(128)S(1)}, s32[32]{0:T(128)}, u32[]{:S(2)}) copy-start(s32[32]{0:T(128)} %assign_ref.1) | copy-start | bytes 388
  95.7 83.7 %copy-start.19 = (s32[32]{0:T(128)S(1)}, s32[32]{0:T(128)}, u32[]{:S(2)}) copy-start(s32[32]{0:T(128)} %tokens_ref.1) | copy-start | bytes 388
  98.5 2.6 %copy-start.9 = (bf16[8192,384]{1,0:T(8,128)(2,1)}, bf16[8192,384]{1,0:T(8,128)(2,1)S(1)}, u32[]{:S(2)}) copy-start(bf16[8192,384]{1,0:T(8,128)(2,1)S(1)} %load_rest.1.weight_ref) | copy-start | bytes 18874372
  179.3 2.8 %copy-start.10 = (bf16[8192,384]{1,0:T(8,128)(2,1)S(1)}, bf16[8192,384]{1,0:T(8,128)(2,1)}, u32[]{:S(2)}) copy-start(bf16[8192,384]{1,0:T(8,128)(2,1)} %copy-done.9) | copy-start | bytes 18874372
  (2 other events, 1.5 us)

commit v3 on v2

--- a/solution.py
+++ b/solution.py
@@ -16,6 +16,7 @@
 THETA = 1000000.0
 LANES = 128
 CHUNK = 512
+OUT_CHUNK = 512
 GRANT = 16 * 1024 * 1024
 
 VMEM = pl.BlockSpec(memory_space=pltpu.VMEM)
@@ -38,6 +39,17 @@
             source.at[:, pl.ds(i * CHUNK, CHUNK)], target.at[:, pl.ds(i * CHUNK, CHUNK)], sem.at[i]
         )
         for i in range(target.shape[1] // CHUNK)
+    ]
+
+
+def row_copies(source, target, sem, first):
+    return [
+        pltpu.make_async_copy(
+            source.at[pl.ds(first + i * OUT_CHUNK, OUT_CHUNK)],
+            target.at[pl.ds(i * OUT_CHUNK, OUT_CHUNK)],
+            sem.at[i],
+        )
+        for i in range(target.shape[0] // OUT_CHUNK)
     ]
 
 
@@ -70,10 +82,20 @@
         store(block, i * CHUNK)
 
 
-def project_first_kernel(stream_ref, gain_ref, source_ref, out_ref, weight_ref, sem):
+def project_first_kernel(
+    place_ref, stream_hbm, gain_hbm, source_ref, out_ref, stream_ref, gain_ref, weight_ref, sem
+):
+    del place_ref
+    columns = weight_ref.shape[1] // CHUNK
+    copy_stream = pltpu.make_async_copy(stream_hbm, stream_ref, sem.at[columns])
+    copy_gain = pltpu.make_async_copy(gain_hbm, gain_ref, sem.at[columns + 1])
     copies = column_copies(source_ref, weight_ref, sem)
+    copy_stream.start()
+    copy_gain.start()
     for copy in copies:
         copy.start()
+    copy_stream.wait()
+    copy_gain.wait()
     project_body(stream_ref, gain_ref, weight_ref, out_ref, copies)
 
 
@@ -81,21 +103,56 @@
     project_body(stream_ref, gain_ref, weight_ref, out_ref, None)
 
 
-def project_first(stream, gain, weight, peers):
+def project_first(place, stream, gain, weight, peers):
     columns = weight.shape[1]
     count = stream.shape[0] // peers
     return pl.pallas_call(
         project_first_kernel,
-        in_specs=[VMEM, VMEM, HBM],
+        in_specs=[SMEM, HBM, HBM, HBM],
         out_specs=[VMEM, VMEM],
         out_shape=[
             jax.ShapeDtypeStruct((peers, count, columns + LANES), jnp.bfloat16),
+            pltpu.VMEM(stream.shape, stream.dtype),
+        ],
+        scratch_shapes=[
+            pltpu.VMEM(gain.shape, gain.dtype),
             pltpu.VMEM(weight.shape, weight.dtype),
-        ],
-        scratch_shapes=[pltpu.SemaphoreType.DMA((columns // CHUNK,))],
+            pltpu.SemaphoreType.DMA((columns // CHUNK + 2,)),
+        ],
         compiler_params=PARAMS,
         name="project_first",
-    )(stream, gain, in_hbm(weight))
+    )(place, in_hbm(stream), in_hbm(gain), in_hbm(weight))
+
+
+def load_kernel(order_ref, after_ref, *refs):
+    del order_ref, after_ref
+    count = len(refs) // 2
+    sem = refs[-1]
+    copies = [
+        pltpu.make_async_copy(
+            refs[i].at[pl.ds(0, refs[count + i].shape[0])], refs[count + i], sem.at[i]
+        )
+        for i in range(count)
+    ]
+    for copy in copies:
+        copy.start()
+    for copy in copies:
+        copy.wait()
+
+
+def load(order, after, arrays, rows=None):
+    shapes = [array.shape if rows is None else (rows,) + array.shape[1:] for array in arrays]
+    size = sum(array.size for array in arrays)
+    return pl.pallas_call(
+        load_kernel,
+        in_specs=[SMEM, VMEM] + [HBM] * len(arrays),
+        out_specs=[VMEM] * len(arrays),
+        out_shape=[pltpu.VMEM(shape, array.dtype) for shape, array in zip(shapes, arrays)],
+        scratch_shapes=[pltpu.SemaphoreType.DMA((len(arrays),))],
+        compiler_params=PARAMS,
+        cost_estimate=pl.CostEstimate(flops=4 * size, bytes_accessed=4 * size, transcendentals=0),
+        name="load",
+    )(jnp.full((1,), order, jnp.int32), after, *[in_hbm(array) for array in arrays])
 
 
 def project(stream, gain, weight, peers):
@@ -111,7 +168,7 @@
     )(stream, gain, in_vmem(weight))
 
 
-def attend_body(lengths_ref, place_ref, parts_ref, bias_ref, frequency_ref, cache, out_ref, width, ready):
+def attend_body(lengths_ref, place_ref, parts_ref, bias_ref, frequency_ref, cache, out_ref, width):
     count = out_ref.shape[0]
     length = cache.shape[3]
     query_cols = HEADS * HEAD_DIM
@@ -160,7 +217,6 @@
         value_new = columns_of(query_cols + key_cols + k * HEAD_DIM)
         value_new = value_new.astype(jnp.bfloat16).astype(jnp.float32)
         heads.append((queries, key_new, value_new))
-    ready()
     for k in range(KV_HEADS):
         queries, key_new, value_new = heads[k]
         keys = cache[:, 0, k].reshape(count * length, HEAD_DIM)
@@ -191,116 +247,92 @@
             )
 
 
-def attend_first_kernel(
-    lengths_ref, place_ref, parts_ref, bias_ref, frequency_ref, cache_hbm, weight_hbm,
-    out_ref, cache_ref, weight_ref, sem, *, width,
+def attend_kernel(
+    lengths_ref, place_ref, parts_ref, bias_ref, frequency_ref, cache_ref, stream_ref, source_ref,
+    out_ref, same_ref, weight_ref, sem, *, width,
 ):
-    copy_cache = pltpu.make_async_copy(cache_hbm, cache_ref, sem.at[0])
-    copy_weight = pltpu.make_async_copy(weight_hbm, weight_ref, sem.at[1])
-    copy_cache.start()
-    copy_weight.start()
+    copies = row_copies(source_ref, weight_ref, sem, 0)
+    for copy in copies:
+        copy.start()
+    same_ref[...] = stream_ref[...]
     attend_body(
-        lengths_ref, place_ref, parts_ref, bias_ref, frequency_ref, cache_ref, out_ref, width,
-        copy_cache.wait,
+        lengths_ref, place_ref, parts_ref, bias_ref, frequency_ref, cache_ref, out_ref, width
     )
-    copy_weight.wait()
-
-
-def attend_kernel(
-    lengths_ref, place_ref, parts_ref, bias_ref, frequency_ref, cache_ref, out_ref, *, width
-):
-    attend_body(
-        lengths_ref, place_ref, parts_ref, bias_ref, frequency_ref, cache_ref, out_ref, width,
-        lambda: None,
-    )
-
-
-def attend_first(lengths, place, parts, bias, frequency, cache, weight, width):
+    for copy in copies:
+        copy.wait()
+
+
+def attend(lengths, place, parts, bias, frequency, cache, stream, weight, early, width):
     count = parts.shape[1]
     return pl.pallas_call(
-        functools.partial(attend_first_kernel, width=width),
-        in_specs=[SMEM, SMEM, VMEM, VMEM, VMEM, HBM, HBM],
-        out_specs=[VMEM, VMEM, VMEM],
+        functools.partial(attend_kernel, width=width),
+        in_specs=[SMEM, SMEM] + [VMEM] * 5 + [HBM],
+        out_specs=[VMEM] * 3,
         out_shape=[
             jax.ShapeDtypeStruct((count, HEADS * HEAD_DIM), jnp.bfloat16),
-            pltpu.VMEM(cache.shape, cache.dtype),
-            pltpu.VMEM(weight.shape, weight.dtype),
-        ],
-        scratch_shapes=[pltpu.SemaphoreType.DMA((2,))],
-        compiler_params=PARAMS,
-        name="attend_first",
-    )(lengths, place, parts, bias, frequency, in_hbm(cache), in_hbm(weight))
-
-
-def attend(lengths, place, parts, bias, frequency, cache, width):
-    count = parts.shape[1]
-    return pl.pallas_call(
-        functools.partial(attend_kernel, width=width),
-        in_specs=[SMEM, SMEM, VMEM, VMEM, VMEM, VMEM],
-        out_specs=VMEM,
-        out_shape=jax.ShapeDtypeStruct((count, HEADS * HEAD_DIM), jnp.bfloat16),
+            jax.ShapeDtypeStruct(stream.shape, stream.dtype),
+            pltpu.VMEM((early, weight.shape[1]), weight.dtype),
+        ],
+        scratch_shapes=[pltpu.SemaphoreType.DMA((early // OUT_CHUNK,))],
         compiler_params=PARAMS,
         name="attend",
-    )(lengths, place, parts, bias, frequency, in_vmem(cache))
-
-
-def combine_kernel(gathered_ref, weight_ref, stream_ref, out_ref):
+    )(lengths, place, parts, bias, frequency, in_vmem(cache), stream, in_hbm(weight))
+
+
+def combine_kernel(gathered_ref, early_ref, stream_ref, source_ref, out_ref, late_ref, sem):
+    early = early_ref.shape[0]
+    copies = row_copies(source_ref, late_ref, sem, early)
+    for copy in copies:
+        copy.start()
     peers = gathered_ref.shape[0]
     blocks = [gathered_ref[j].astype(jnp.float32) for j in range(peers)]
     gathered = jnp.concatenate(blocks, axis=0).astype(jnp.bfloat16)
-    for at in range(0, out_ref.shape[1], 256):
-        update = jnp.dot(
-            gathered, weight_ref[:, at : at + 256], preferred_element_type=jnp.float32
-        )
-        current = stream_ref[:, at : at + 256].astype(jnp.float32)
-        out_ref[:, at : at + 256] = (current + update).astype(jnp.bfloat16)
-
-
-def combine(gathered, weight, stream):
+    update = jnp.dot(gathered[:, :early], early_ref[...], preferred_element_type=jnp.float32)
+    for i, copy in enumerate(copies):
+        copy.wait()
+        at = i * OUT_CHUNK
+        update = update + jnp.dot(
+            gathered[:, early + at : early + at + OUT_CHUNK],
+            late_ref[at : at + OUT_CHUNK],
+            preferred_element_type=jnp.float32,
+        )
+    out_ref[...] = (stream_ref[...].astype(jnp.float32) + update).astype(jnp.bfloat16)
+
+
+def combine(gathered, early, stream, weight):
+    late = weight.shape[0] - early.shape[0]
     return pl.pallas_call(
         combine_kernel,
-        in_specs=[VMEM, VMEM, VMEM],
+        in_specs=[VMEM, VMEM, VMEM, HBM],
         out_specs=VMEM,
         out_shape=jax.ShapeDtypeStruct(stream.shape, jnp.bfloat16),
+        scratch_shapes=[
+            pltpu.VMEM((late, weight.shape[1]), weight.dtype),
+            pltpu.SemaphoreType.DMA((late // OUT_CHUNK,)),
+        ],
         compiler_params=PARAMS,
         name="combine",
-    )(gathered, in_vmem(weight), stream)
-
-
-def load_kernel(idle_ref, source_ref, out_ref, sem):
-    @pl.when(idle_ref[0] == 1)
-    def _():
-        copy = pltpu.make_async_copy(source_ref, out_ref, sem.at[0])
-        copy.start()
-        copy.wait()
-
-
-def load_rest_kernel(idle_ref, source_ref, before_ref, out_ref, sem):
-    del before_ref
-    load_kernel(idle_ref, source_ref, out_ref, sem)
-
-
-def load(idle, weight, before=None):
-    first = before is None
-    return pl.pallas_call(
-        load_kernel if first else load_rest_kernel,
-        in_specs=[SMEM, HBM] + ([] if first else [VMEM]),
-        out_specs=VMEM,
-        out_shape=pltpu.VMEM(weight.shape, weight.dtype),
-        scratch_shapes=[pltpu.SemaphoreType.DMA((1,))],
-        compiler_params=PARAMS,
-        input_output_aliases={} if first else {2: 0},
-        name="load" if first else "load_rest",
-    )(idle, in_hbm(weight), *([] if first else [in_vmem(before)]))
+    )(gathered, in_vmem(early), stream, in_hbm(weight))
 
 
 def logits_kernel(
-    assign_ref, tokens_ref, place_ref, rows_ref, over_ref, gain_ref, weight_ref,
-    logits_ref, stats_ref, scratch_ref, *, width,
+    assign_ref, tokens_ref, place_ref, rows_ref, over_ref, gain_ref, early_ref, source_ref,
+    logits_ref, stats_ref, scratch_ref, late_ref, sem, *, width,
 ):
     pieces, requests, share = rows_ref.shape
-    vocab = weight_ref.shape[1]
-    own = place_ref[1] == 1
+    vocab = early_ref.shape[1]
+    early = early_ref.shape[0] // share
+    copies = []
+    for i in range(pieces - early):
+        copies.append(
+            pltpu.make_async_copy(
+                source_ref.at[pl.ds((early + i) * share, share)],
+                late_ref.at[pl.ds(i * share, share)],
+                sem.at[i],
+            )
+        )
+        copies[i].start()
+    own = place_ref[2] == 1
     squares = jnp.zeros((requests, 1), jnp.float32)
     for m in range(pieces):
         current = jnp.where(own, rows_ref[m], over_ref[m]).astype(jnp.float32)
@@ -310,16 +342,19 @@
     for m in range(pieces):
         current = jnp.where(own, rows_ref[m], over_ref[m]).astype(jnp.float32)
         normed = (current * gain_ref[m].astype(jnp.float32) * inverse).astype(jnp.bfloat16)
-        logits = logits + jnp.dot(
-            normed, weight_ref[m * share : (m + 1) * share], preferred_element_type=jnp.float32
-        )
+        if m < early:
+            weight = early_ref[m * share : (m + 1) * share]
+        else:
+            copies[m - early].wait()
+            weight = late_ref[(m - early) * share : (m - early + 1) * share]
+        logits = logits + jnp.dot(normed, weight, preferred_element_type=jnp.float32)
     scratch_ref[...] = logits
     row = lax.broadcasted_iota(jnp.int32, (requests, vocab), 0)
     targets = jnp.zeros((requests, vocab), jnp.int32)
     for s in range(requests):
         request = assign_ref[s]
         logits_ref[pl.ds(s, 1), :] = scratch_ref[pl.ds(request, 1), :]
-        targets = jnp.where(row == s, tokens_ref[request] - place_ref[0], targets)
+        targets = jnp.where(row == s, tokens_ref[request] - place_ref[1], targets)
     ordered = logits_ref[...]
     column = lax.broadcasted_iota(jnp.int32, (requests, vocab), 1)
     picked = jnp.sum(jnp.where(column == targets, ordered, 0.0), axis=1, keepdims=True)
@@ -333,22 +368,27 @@
     stats_ref[...] = jnp.sum(spread_out, axis=0, keepdims=True)
 
 
-def final_logits(assign, tokens, place, rows, over, gain, weight, width):
-    requests = rows.shape[1]
+def final_logits(assign, tokens, place, rows, over, gain, early, weight, width):
+    pieces, requests, share = rows.shape
     vocab = weight.shape[1]
+    late = weight.shape[0] - early.shape[0]
     lanes = -(-3 * requests // LANES) * LANES
     return pl.pallas_call(
         functools.partial(logits_kernel, width=width),
-        in_specs=[SMEM, SMEM, SMEM, VMEM, VMEM, VMEM, VMEM],
+        in_specs=[SMEM, SMEM, SMEM, VMEM, VMEM, VMEM, VMEM, HBM],
         out_specs=[VMEM, VMEM],
         out_shape=[
             jax.ShapeDtypeStruct((requests, vocab), jnp.float32),
             jax.ShapeDtypeStruct((1, lanes), jnp.float32),
         ],
-        scratch_shapes=[pltpu.VMEM((requests, vocab), jnp.float32)],
+        scratch_shapes=[
+            pltpu.VMEM((requests, vocab), jnp.float32),
+            pltpu.VMEM((late, vocab), weight.dtype),
+            pltpu.SemaphoreType.DMA((late // share,)),
+        ],
         compiler_params=PARAMS,
         name="final_logits",
-    )(assign, tokens, place, rows, over, gain, in_vmem(weight))
+    )(assign, tokens, place, rows, over, gain, in_vmem(early), in_hbm(weight))
 
 
 def finish_kernel(logits_ref, stats_ref, out_ref, chosen_ref):
@@ -411,51 +451,51 @@
     peers = lax.axis_size("mp")
     share = hidden_in.shape[1]
     width = share * peers
-    place = lax.axis_index("mp").astype(jnp.int32).reshape(1)
+    vocab_first = lax.axis_index(("pipe", "mp")) * head_weight.shape[1]
+    odd = section % 2 == 1
+    place = jnp.stack([lax.axis_index("mp"), vocab_first, odd.astype(vocab_first.dtype)])
+    place = place.astype(jnp.int32)
     exponents = np.arange(HEAD_DIM // 2, dtype=np.float64) * 2.0 / HEAD_DIM
     frequency = np.tile(THETA ** (-exponents), 2)[None, :].astype(np.float32)
     weight_in = qkv_weight[0]
     weight_out = out_weight[0]
     cache = kv_cache[0]
-
-    gain_blocks = jnp.broadcast_to(final_gain[None, None], (peers, 1, share))
-    gain_full = lax.cond(section != 0, lambda b: exchange(b, "mp"), lambda b: b, gain_blocks)
-
-    def only_active(active, fn, other, value):
-        return lax.cond(active, fn, other, value)
-
-    stream = hidden_in
+    final_row = final_gain[None]
+
+    early = out_weight.shape[1] * 5 // 8 // OUT_CHUNK * OUT_CHUNK
+
+    def run_layer(payload, current, gains, cache_ready):
+        parts = exchange(payload, "mp")
+        attended, current, early_weight = attend(
+            lengths, place, parts, qkv_bias, frequency, cache_ready, current, weight_out, early,
+            width,
+        )
+        return combine(spread(attended, "mp"), early_weight, current, weight_out), gains
+
+    def share_gains(payload, current, gains, *ready):
+        return current, spread(final_row, "mp")
+
+    def skip(payload, current, gains, *ready):
+        return current, gains
+
+    gain_full = jnp.zeros((peers, 1, share), final_gain.dtype)
     for layer in range(sections):
         active = section == layer
         if layer == 0:
-            payload, weight_in = project_first(stream, attn_gain, weight_in, peers)
+            payload, stream = project_first(place, hidden_in, attn_gain, weight_in, peers)
+            branch = jnp.where(active, 0, 1)
+            branches = (run_layer, share_gains)
+            ready = [cache]
         else:
-            payload = project(stream, attn_gain, weight_in, peers)
-        parts = lax.cond(active, lambda b: exchange(b, "mp"), lambda b: b, payload)
-        if layer == 0:
-            attended, cache, weight_out = attend_first(
-                lengths, place, parts, qkv_bias, frequency, cache, weight_out, width
-            )
-        else:
-            attended = attend(lengths, place, parts, qkv_bias, frequency, cache, width)
-        gathered = lax.cond(
-            active,
-            lambda b: spread(b, "mp"),
-            lambda b: jnp.broadcast_to(b[None], (peers,) + b.shape),
-            attended,
-        )
-        stream = combine(gathered, weight_out, stream)
+            payload = project(stream, attn_gain, in_ready, peers)
+            branch = jnp.where(active, 1, jnp.where(section == 0, 2, 0) if layer == 1 else 0)
+            branches = (skip, run_layer, share_gains) if layer == 1 else (skip, run_layer)
+        stream, gain_full = lax.switch(branch, branches, payload, stream, gain_full, *ready)
         if layer + 1 < sections:
+            in_ready, *ready = load(layer, stream, [weight_in, cache])
             stream = lax.ppermute(stream, "pipe", [(layer, layer + 1)])
-        if layer == 0:
-            gain_full, stream = lax.optimization_barrier((gain_full, stream))
-            gain_full = lax.cond(section == 0, lambda b: exchange(b, "mp"), lambda b: b, gain_full)
-            weight_head = load((section != 0).astype(jnp.int32).reshape(1), head_weight)
-        if layer == 1:
-            weight_head = load((section == 0).astype(jnp.int32).reshape(1), head_weight, weight_head)
 
     last = sections - 1
-    odd = section % 2 == 1
     arrived = stream
     for target in range(1, last, 2):
         copied = lax.ppermute(stream, "pipe", [(last, target)])
@@ -466,12 +506,11 @@
         lambda b: jnp.broadcast_to(b[None], (peers,) + b.shape),
         arrived,
     )
+    (head_ready,) = load(sections, rows, [head_weight], width * 3 // 4)
     over = lax.ppermute(rows, "pipe", [(i, i - 1) for i in range(1, sections, 2)])
 
-    vocab_first = lax.axis_index(("pipe", "mp")) * head_weight.shape[1]
-    head_place = jnp.stack([vocab_first, odd.astype(vocab_first.dtype)]).astype(jnp.int32)
     logits, stats = final_logits(
-        assign, token_ids, head_place, rows, over, gain_full, weight_head, width
+        assign, token_ids, place, rows, over, gain_full, head_ready, head_weight, width
     )
     stats = spread(stats, ("pipe", "mp"))
     logprobs, chosen = finish(logits, stats.reshape(stats.shape[0], stats.shape[2]))

time: 199 us -> 167 us (0.84)
  local copies, waits for them, and re-layouts: 40.7 us -> 0.84 us
  waiting for transfers between devices: 68.4 us -> 75.7 us
  Pallas kernels: 32.8 us -> 36.2 us
  blocking collectives: 49.7 us -> 46.7 us
    unnamed x42 -> x16, local copies, waits for them, and re-layouts: 39.7 us -> 0.04 us
    ppermute x1, waiting for transfers between devices: 67.6 us -> 75.7 us  [local(): lax.ppermute(rows, 'pipe', [(i, i - 1) for i in range(1, sections, 2)])]
    pallas_call x8 -> x6, Pallas kernels: 18 us -> 24.1 us  [the longest x4 16.1 us: load(): pl.pallas_call(load_kernel, in_specs=[SMEM, VMEM] + [HBM] * len(arrays),...]
    pallas_call x3 -> x1, Pallas kernels: 6.26 us -> 3.12 us  [attend(): pl.pallas_call(functools.partial(attend_kernel, width=width), in_specs=[S...]
    all_to_all x4, blocking collectives: 49.7 us -> 46.7 us  [exchange(): return lax.all_to_all(blocks, axis, 0, 0, tiled=True)]
  transfers between devices with their start and end apart: 5 -> 5, of which waited for: 2 -> 1; matrix products, arithmetic and copies ran while one was open for 1% -> 0% of each run, Pallas kernels for 1% -> 10%
where the time goes in v3:
time: 167 us; the launch traced here: 166 us
  waiting for transfers between devices  75.7 us (45%)
  blocking collectives  46.7 us (28%)
  Pallas kernels  36.2 us (22%)
  starting transfers between devices  4.58 us (3%)
    ppermute x1, waiting for transfers between devices, local(): lax.ppermute(rows, 'pipe', [(i, i - 1) for i in range(1, sections, 2)])  75.7 us
    all_to_all x4, blocking collectives, exchange(): return lax.all_to_all(blocks, axis, 0, 0, tiled=True)  46.7 us
    pallas_call x4, Pallas kernels, load(): pl.pallas_call(load_kernel, in_specs=[SMEM, VMEM] + [HBM] * len(arrays),...  16.1 us
    pallas_call x3, Pallas kernels, project(): pl.pallas_call(project_kernel, in_specs=[VMEM, VMEM, VMEM], out_specs=VME...  5.73 us
    pallas_call x1, Pallas kernels, project_first(): pl.pallas_call(project_first_kernel, in_specs=[SMEM, HBM, HBM, HBM], out_...  5.18 us
  transfers between devices with their start and end apart: 5, of which 1 were waited for; matrix products, arithmetic and copies ran while one was open for 0% of the time, Pallas kernels for 10%

profile of v3, /device:TPU:0, one launch (start us, length us, event | category | flops | bytes accessed | tf_op | source)
XLA Modules:
  0.0 166.2 jit_solution(13121102433158223543)
XLA Ops:
  0.8 5.2 %project_first.1 = (bf16[8,4,5248]{2,1,0:T(4,128)(2,1)S(1)}, bf16[32,1024]{1,0:T(8,128)(2,1)S(1)}) custom-call(s32[3]{0:T(128)S(1)} %pad_add_fusion.place_ref, bf16[32,1024]{1,0:T(8,128)(2,1)} %stream_hbm.1, bf16[1,1024]{1,0:T(2,128)(2,1)} %gain_ref.5, bf16[1024,5120]{1,0:T(8,128)(2,1)} %bitcast.19), custom_call_target="tpu_custom_call" | custom-call | tf_op jit(solution)/shard_map/project_first/pallas_call | solution.py:109
  6.0 33.3 %conditional.5 = (bf16[32,1024]{1,0:T(8,128)(2,1)S(1)}, bf16[8,1,1024]{2,1,0:T(2,128)(2,1)S(1)}) conditional(s32[]{:T(128)} %clamp.15, (bf16[8,4,5248]{2,1,0:T(4,128)(2,1)S(1)}, s32[32]{0:T(128)S(1)}, s32[3]{0:T(128)S(1)}, bf16[1,5120]{1,0:T(2,128)(2,1)S(1)}, f32[1,128]{1,0:T(1,128)S(1)}, /*index=5*/bf16[4,2,4,256,128]{4,3,2,1,0:T(8,128)(2,1)S(1)}, ...), branch_computations={%region_0.1_spmd, %region_1.2_spmd} | conditional | bytes 1507346 | solution.py:493
  6.0 16.3 %all_to_all.49.parts_ref = bf16[8,4,5248]{2,1,0:T(4,128)(2,1)S(1)} all-to-all(bf16[8,4,5248]{2,1,0:T(4,128)(2,1)S(1)} %get-tuple-element.93), channel_id=1, replica_groups=mesh['pipe'=4,'mp'=8] {'mp'}, dimensions={0} | all-to-all | bytes 671744 | tf_op jit(solution)/shard_map/cond/branch_0_fun/all_to_all | solution.py:428
  22.3 3.1 %attend.4 = (bf16[4,4096]{1,0:T(4,128)(2,1)S(1)}, bf16[32,1024]{1,0:T(8,128)(2,1)S(1)}, bf16[2560,1024]{1,0:T(8,128)(2,1)S(1)}) custom-call(s32[32]{0:T(128)S(1)} %get-tuple-element.91.lengths_ref, s32[3]{0:T(128)S(1)} %get-tuple-element.92.place_ref, bf16[8,4,5248]{2,1,0:T(4,128)(2,1)S(1)} %all_to_all.49.parts_ref, ...), custom_call_target="tpu_custom_call" | custom-call | tf_op jit(solution)/shard_map/cond/branch_0_fun/attend/pallas_call | solution.py:267
  25.5 10.9 %all_to_all.50.gathered_ref = bf16[8,4,4096]{2,1,0:T(4,128)(2,1)S(1)} all-to-all(bf16[8,4,4096]{2,1,0:T(4,128)(2,1)S(1)} %broadcast_in_dim.19), channel_id=1, replica_groups=mesh['pipe'=4,'mp'=8] {'mp'}, dimensions={0} | all-to-all | bytes 524288 | tf_op jit(solution)/shard_map/cond/branch_0_fun/all_to_all | solution.py:428
  36.4 2.8 %combine.4 = bf16[32,1024]{1,0:T(8,128)(2,1)S(1)} custom-call(bf16[8,4,4096]{2,1,0:T(4,128)(2,1)S(1)} %all_to_all.50.gathered_ref, bf16[2560,1024]{1,0:T(8,128)(2,1)S(1)} %get-tuple-element.100.early_ref, bf16[32,1024]{1,0:T(8,128)(2,1)S(1)} %get-tuple-element.101.stream_ref, bf16[4096,1024]{1,0:T(8,128)(2,1)} %get-tuple-element.98.source_ref), custom_call_target="tpu_custom_call" | custom-call | tf_op jit(solution)/shard_map/cond/branch_0_fun/combine/pallas_call | solution.py:304
  39.3 1.3 collective-permute-start
  40.6 4.6 %load.4 = (bf16[1024,5120]{1,0:T(8,128)(2,1)S(1)}, bf16[4,2,4,256,128]{4,3,2,1,0:T(8,128)(2,1)S(1)}) custom-call(s32[1]{0:T(128)} %constant.37.clone.1.order_ref, bf16[32,1024]{1,0:T(8,128)(2,1)S(1)} %get-tuple-element.160.after_ref, bf16[1024,5120]{1,0:T(8,128)(2,1)} %bitcast.20, bf16[4,2,4,256,128]{4,3,2,1,0:T(8,128)(2,1)} %bitcast.9), custom_call_target="tpu_custom_call" | custom-call | flops 25165824 | bytes 25165824 | tf_op jit(solution)/shard_map/load/pallas_call | solution.py:146
  45.2 1.9 %project.3 = bf16[8,4,5248]{2,1,0:T(4,128)(2,1)S(1)} custom-call(bf16[32,1024]{1,0:T(8,128)(2,1)S(1)} %collective-permute-done.stream_ref, bf16[1,1024]{1,0:T(2,128)(2,1)S(1)} %copy-done.1, bf16[1024,5120]{1,0:T(8,128)(2,1)S(1)} %get-tuple-element.162.weight_ref), custom_call_target="tpu_custom_call" | custom-call | tf_op jit(solution)/shard_map/project/pallas_call | solution.py:161
  47.2 10.7 %conditional.6 = ((bf16[32,1024]{1,0:T(8,128)(2,1)S(1)}, bf16[8,1,1024]{2,1,0:T(2,128)(2,1)S(1)})) conditional(s32[]{:T(128)} %clamp.14, (bf16[32,1024]{1,0:T(8,128)(2,1)S(1)}, bf16[8,1,1024]{2,1,0:T(2,128)(2,1)S(1)}) %tuple.47, (bf16[8,4,5248]{2,1,0:T(4,128)(2,1)S(1)}, s32[32]{0:T(128)S(1)}, s32[3]{0:T(128)S(1)}, ...), branch_computations={%region_2.3_spmd, %region_3.4_spmd, %region_4.5_spmd} | conditional | bytes 1490968 | solution.py:493
  47.8 0.8 reduce.1
  48.6 9.3 %all_to_all.53 = bf16[8,2,512]{2,1,0:T(2,128)(2,1)S(1)} all-to-all(bf16[8,2,512]{2,1,0:T(2,128)(2,1)S(1)} %reshape.25), channel_id=1, replica_groups=mesh['pipe'=4,'mp'=8] {'mp'}, dimensions={0} | all-to-all | bytes 32768 | tf_op jit(solution)/shard_map/cond/branch_2_fun/all_to_all | solution.py:428
  57.9 0.7 collective-permute-start.1
  58.6 4.6 %load.5 = (bf16[1024,5120]{1,0:T(8,128)(2,1)S(1)}, bf16[4,2,4,256,128]{4,3,2,1,0:T(8,128)(2,1)S(1)}) custom-call(s32[1]{0:T(128)} %constant.38.clone.1.order_ref, bf16[32,1024]{1,0:T(8,128)(2,1)S(1)} %get-tuple-element.164.after_ref, bf16[1024,5120]{1,0:T(8,128)(2,1)} %bitcast.21, bf16[4,2,4,256,128]{4,3,2,1,0:T(8,128)(2,1)} %bitcast.10), custom_call_target="tpu_custom_call" | custom-call | flops 25165824 | bytes 25165824 | tf_op jit(solution)/shard_map/load/pallas_call | solution.py:146
  63.2 1.9 %project.4 = bf16[8,4,5248]{2,1,0:T(4,128)(2,1)S(1)} custom-call(bf16[32,1024]{1,0:T(8,128)(2,1)S(1)} %collective-permute-done.1.stream_ref, bf16[1,1024]{1,0:T(2,128)(2,1)S(1)} %copy-done.1, bf16[1024,5120]{1,0:T(8,128)(2,1)S(1)} %get-tuple-element.165.weight_ref), custom_call_target="tpu_custom_call" | custom-call | tf_op jit(solution)/shard_map/project/pallas_call | solution.py:161
  65.3 0.7 collective-permute-start.2
  66.0 4.6 %load.6 = (bf16[1024,5120]{1,0:T(8,128)(2,1)S(1)}, bf16[4,2,4,256,128]{4,3,2,1,0:T(8,128)(2,1)S(1)}) custom-call(s32[1]{0:T(128)} %constant.39.clone.1.order_ref, bf16[32,1024]{1,0:T(8,128)(2,1)S(1)} %get-tuple-element.185.after_ref, bf16[1024,5120]{1,0:T(8,128)(2,1)} %bitcast.22, bf16[4,2,4,256,128]{4,3,2,1,0:T(8,128)(2,1)} %bitcast.11), custom_call_target="tpu_custom_call" | custom-call | flops 25165824 | bytes 25165824 | tf_op jit(solution)/shard_map/load/pallas_call | solution.py:146
  70.6 1.9 %project.5 = bf16[8,4,5248]{2,1,0:T(4,128)(2,1)S(1)} custom-call(bf16[32,1024]{1,0:T(8,128)(2,1)S(1)} %collective-permute-done.2.stream_ref, bf16[1,1024]{1,0:T(2,128)(2,1)S(1)} %copy-done.1, bf16[1024,5120]{1,0:T(8,128)(2,1)S(1)} %get-tuple-element.167.weight_ref), custom_call_target="tpu_custom_call" | custom-call | tf_op jit(solution)/shard_map/project/pallas_call | solution.py:161
  73.3 1.3 collective-permute-start.4
  74.6 2.3 %load.7.early_ref = bf16[6144,384]{1,0:T(8,128)(2,1)S(1)} custom-call(s32[1]{0:T(128)} %constant.40.clone.1.order_ref, bf16[8,32,1024]{2,1,0:T(8,128)(2,1)S(1)} %get-tuple-element.187.after_ref.rows_ref, bf16[8192,384]{1,0:T(8,128)(2,1)} %source_ref.1), custom_call_target="tpu_custom_call" | custom-call | flops 12582912 | bytes 12582912 | tf_op jit(solution)/shard_map/load/pallas_call | solution.py:146
  77.0 75.7 %collective-permute-done.4.over_ref = bf16[8,32,1024]{2,1,0:T(8,128)(2,1)S(1)} collective-permute-done((bf16[8,32,1024]{2,1,0:T(8,128)(2,1)S(1)}, bf16[8,32,1024]{2,1,0:T(8,128)(2,1)S(1)}, u32[]{:S(2)}, u32[]{:S(2)}) %collective-permute-start.4) | collective-permute-done | bytes 524320 | tf_op jit(solution)/shard_map/ppermute | solution.py:510
  152.7 2.4 %final_logits.1 = (f32[32,384]{1,0:T(8,128)S(1)}, f32[1,128]{1,0:T(1,128)S(1)}) custom-call(s32[32]{0:T(128)S(1)} %copy-done.2, s32[32]{0:T(128)S(1)} %copy-done.3, s32[3]{0:T(128)S(1)} %pad_add_fusion.place_ref, bf16[8,32,1024]{2,1,0:T(8,128)(2,1)S(1)} %get-tuple-element.187.after_ref.rows_ref, bf16[8,32,1024]{2,1,0:T(8,128)(2,1)S(1)} %collective-permute-done.4.over_ref, ...), custom_call_target="tpu_custom_call" | custom-call | tf_op jit(solution)/shard_map/final_logits/pallas_call | solution.py:376
  155.1 10.3 %all_to_all.59 = f32[32,1,128]{2,1,0:T(1,128)S(1)} all-to-all(f32[32,1,128]{2,1,0:T(1,128)S(1)} %broadcast_in_dim.46), channel_id=1, replica_groups=mesh['pipe'=4,'mp'=8] {'pipe','mp'}, dimensions={0} | all-to-all | bytes 32768 | tf_op jit(solution)/shard_map/all_to_all | solution.py:428
  165.4 0.8 finish.1
  (34 shorter events, 1.9 us)
Async XLA Ops:
  0.7 5.2 %copy-start = (bf16[1,4,2,4,256,128]{5,4,3,2,1,0:T(8,128)(2,1)S(1)}, bf16[1,4,2,4,256,128]{5,4,3,2,1,0:T(8,128)(2,1)}, u32[]{:S(2)}) copy-start(bf16[1,4,2,4,256,128]{5,4,3,2,1,0:T(8,128)(2,1)} %param.31) | copy-start | bytes 6291460
  0.7 5.2 %copy-start.4 = (bf16[1,5120]{1,0:T(2,128)(2,1)S(1)}, bf16[1,5120]{1,0:T(2,128)(2,1)}, u32[]{:S(2)}) copy-start(bf16[1,5120]{1,0:T(2,128)(2,1)} %param.29) | copy-start | bytes 30724
  0.7 5.2 %copy-start.5 = (s32[32]{0:T(128)S(1)}, s32[32]{0:T(128)}, u32[]{:S(2)}) copy-start(s32[32]{0:T(128)} %param.24) | copy-start | bytes 388
  0.7 5.2 %copy-start.6 = (f32[1,128]{1,0:T(1,128)S(1)}, f32[1,128]{1,0:T(1,128)}, u32[]{:S(2)}) copy-start(f32[1,128]{1,0:T(1,128)} %constant.41.clone) | copy-start | bytes 1540
  0.7 5.2 %copy-start.7 = (bf16[1024]{0:T(1024)(128)(2,1)S(1)}, bf16[1024]{0:T(1024)(128)(2,1)}, u32[]{:S(2)}) copy-start(bf16[1024]{0:T(1024)(128)(2,1)} %param.32) | copy-start | bytes 6148
  39.3 5.9 %collective-permute-start = (bf16[32,1024]{1,0:T(8,128)(2,1)S(1)}, bf16[32,1024]{1,0:T(8,128)(2,1)S(1)}, u32[]{:S(2)}, u32[]{:S(2)}) collective-permute-start(bf16[32,1024]{1,0:T(8,128)(2,1)S(1)} %get-tuple-element.160.after_ref), channel_id=1, source_target_pairs={{0,8},{1,9},{2,10},{3,11},{4,12},{5,13},{6,14},{7,15}} | collective-permute-start | bytes 196616 | tf_op jit(solution)/shard_map/ppermute | solution.py:496
  40.6 4.6 %copy-start.1 = (bf16[1,1024]{1,0:T(2,128)(2,1)S(1)}, bf16[1,1024]{1,0:T(2,128)(2,1)}, u32[]{:S(2)}) copy-start(bf16[1,1024]{1,0:T(2,128)(2,1)} %gain_ref.5) | copy-start | bytes 6148
  57.9 5.3 %collective-permute-start.1 = (bf16[32,1024]{1,0:T(8,128)(2,1)S(1)}, bf16[32,1024]{1,0:T(8,128)(2,1)S(1)}, u32[]{:S(2)}, u32[]{:S(2)}) collective-permute-start(bf16[32,1024]{1,0:T(8,128)(2,1)S(1)} %get-tuple-element.164.after_ref), channel_id=1, source_target_pairs={{8,16},{9,17},{10,18},{11,19},{12,20},{13,21},{14,22},{15,23}} | collective-permute-start | bytes 196616 | tf_op jit(solution)/shard_map/ppermute | solution.py:496
  65.3 5.3 %collective-permute-start.2 = (bf16[32,1024]{1,0:T(8,128)(2,1)S(1)}, bf16[32,1024]{1,0:T(8,128)(2,1)S(1)}, u32[]{:S(2)}, u32[]{:S(2)}) collective-permute-start(bf16[32,1024]{1,0:T(8,128)(2,1)S(1)} %get-tuple-element.185.after_ref), channel_id=1, source_target_pairs={{16,24},{17,25},{18,26},{19,27},{20,28},{21,29},{22,30},{23,31}} | collective-permute-start | bytes 196616 | tf_op jit(solution)/shard_map/ppermute | solution.py:496
  72.5 0.7 collective-permute-start.3
  73.3 79.4 %copy-start.2 = (s32[32]{0:T(128)S(1)}, s32[32]{0:T(128)}, u32[]{:S(2)}) copy-start(s32[32]{0:T(128)} %assign_ref.1) | copy-start | bytes 388
  73.3 79.4 %copy-start.3 = (s32[32]{0:T(128)S(1)}, s32[32]{0:T(128)}, u32[]{:S(2)}) copy-start(s32[32]{0:T(128)} %tokens_ref.1) | copy-start | bytes 388
  73.3 79.3 %collective-permute-start.4 = (bf16[8,32,1024]{2,1,0:T(8,128)(2,1)S(1)}, bf16[8,32,1024]{2,1,0:T(8,128)(2,1)S(1)}, u32[]{:S(2)}, u32[]{:S(2)}) collective-permute-start(bf16[8,32,1024]{2,1,0:T(8,128)(2,1)S(1)} %get-tuple-element.187.after_ref.rows_ref), channel_id=1, source_target_pairs={{8,0},{24,16},{9,1},{25,17},{10,2},{26,18},{11,3},{27,19},{12,4},{... | collective-permute-start | bytes 1572872 | tf_op jit(solution)/shard_map/ppermute | solution.py:510

commit v4 on v3

--- a/solution.py
+++ b/solution.py
@@ -16,8 +16,10 @@
 THETA = 1000000.0
 LANES = 128
 CHUNK = 512
-OUT_CHUNK = 512
+OUT_CHUNK = 256
+COVER = 32
 GRANT = 16 * 1024 * 1024
+FULL_GRANT = 60 * 1024 * 1024
 
 VMEM = pl.BlockSpec(memory_space=pltpu.VMEM)
 SMEM = pl.BlockSpec(memory_space=pltpu.SMEM)
@@ -39,17 +41,6 @@
             source.at[:, pl.ds(i * CHUNK, CHUNK)], target.at[:, pl.ds(i * CHUNK, CHUNK)], sem.at[i]
         )
         for i in range(target.shape[1] // CHUNK)
-    ]
-
-
-def row_copies(source, target, sem, first):
-    return [
-        pltpu.make_async_copy(
-            source.at[pl.ds(first + i * OUT_CHUNK, OUT_CHUNK)],
-            target.at[pl.ds(i * OUT_CHUNK, OUT_CHUNK)],
-            sem.at[i],
-        )
-        for i in range(target.shape[0] // OUT_CHUNK)
     ]
 
 
@@ -119,7 +110,7 @@
             pltpu.VMEM(weight.shape, weight.dtype),
             pltpu.SemaphoreType.DMA((columns // CHUNK + 2,)),
         ],
-        compiler_params=PARAMS,
+        compiler_params=pltpu.CompilerParams(vmem_limit_bytes=FULL_GRANT),
         name="project_first",
     )(place, in_hbm(stream), in_hbm(gain), in_hbm(weight))
 
@@ -248,71 +239,54 @@
 
 
 def attend_kernel(
-    lengths_ref, place_ref, parts_ref, bias_ref, frequency_ref, cache_ref, stream_ref, source_ref,
-    out_ref, same_ref, weight_ref, sem, *, width,
+    lengths_ref, place_ref, parts_ref, bias_ref, frequency_ref, cache_ref, stream_ref,
+    out_ref, same_ref, *, width,
 ):
-    copies = row_copies(source_ref, weight_ref, sem, 0)
-    for copy in copies:
-        copy.start()
     same_ref[...] = stream_ref[...]
     attend_body(
         lengths_ref, place_ref, parts_ref, bias_ref, frequency_ref, cache_ref, out_ref, width
     )
-    for copy in copies:
-        copy.wait()
-
-
-def attend(lengths, place, parts, bias, frequency, cache, stream, weight, early, width):
+
+
+def attend(lengths, place, parts, bias, frequency, cache, stream, width):
     count = parts.shape[1]
     return pl.pallas_call(
         functools.partial(attend_kernel, width=width),
-        in_specs=[SMEM, SMEM] + [VMEM] * 5 + [HBM],
-        out_specs=[VMEM] * 3,
+        in_specs=[SMEM, SMEM] + [VMEM] * 5,
+        out_specs=[VMEM] * 2,
         out_shape=[
             jax.ShapeDtypeStruct((count, HEADS * HEAD_DIM), jnp.bfloat16),
             jax.ShapeDtypeStruct(stream.shape, stream.dtype),
-            pltpu.VMEM((early, weight.shape[1]), weight.dtype),
         ],
-        scratch_shapes=[pltpu.SemaphoreType.DMA((early // OUT_CHUNK,))],
         compiler_params=PARAMS,
+        cost_estimate=pl.CostEstimate(
+            flops=COVER * stream.size * HEADS * HEAD_DIM, bytes_accessed=cache.size * 2, transcendentals=0
+        ),
         name="attend",
-    )(lengths, place, parts, bias, frequency, in_vmem(cache), stream, in_hbm(weight))
-
-
-def combine_kernel(gathered_ref, early_ref, stream_ref, source_ref, out_ref, late_ref, sem):
-    early = early_ref.shape[0]
-    copies = row_copies(source_ref, late_ref, sem, early)
-    for copy in copies:
-        copy.start()
+    )(lengths, place, parts, bias, frequency, in_vmem(cache), stream)
+
+
+def combine_kernel(gathered_ref, weight_ref, stream_ref, out_ref):
     peers = gathered_ref.shape[0]
     blocks = [gathered_ref[j].astype(jnp.float32) for j in range(peers)]
     gathered = jnp.concatenate(blocks, axis=0).astype(jnp.bfloat16)
-    update = jnp.dot(gathered[:, :early], early_ref[...], preferred_element_type=jnp.float32)
-    for i, copy in enumerate(copies):
-        copy.wait()
-        at = i * OUT_CHUNK
-        update = update + jnp.dot(
-            gathered[:, early + at : early + at + OUT_CHUNK],
-            late_ref[at : at + OUT_CHUNK],
-            preferred_element_type=jnp.float32,
-        )
-    out_ref[...] = (stream_ref[...].astype(jnp.float32) + update).astype(jnp.bfloat16)
-
-
-def combine(gathered, early, stream, weight):
-    late = weight.shape[0] - early.shape[0]
+    for at in range(0, out_ref.shape[1], OUT_CHUNK):
+        update = jnp.dot(
+            gathered, weight_ref[:, at : at + OUT_CHUNK], preferred_element_type=jnp.float32
+        )
+        current = stream_ref[:, at : at + OUT_CHUNK].astype(jnp.float32)
+        out_ref[:, at : at + OUT_CHUNK] = (current + update).astype(jnp.bfloat16)
+
+
+def combine(gathered, weight, stream):
     return pl.pallas_call(
         combine_kernel,
-        in_specs=[VMEM, VMEM, VMEM, HBM],
+        in_specs=[VMEM, VMEM, VMEM],
         out_specs=VMEM,
         out_shape=jax.ShapeDtypeStruct(stream.shape, jnp.bfloat16),
-        scratch_shapes=[
-            pltpu.VMEM((late, weight.shape[1]), weight.dtype),
-            pltpu.SemaphoreType.DMA((late // OUT_CHUNK,)),
-        ],
         compiler_params=PARAMS,
         name="combine",
-    )(gathered, in_vmem(early), stream, in_hbm(weight))
+    )(gathered, in_vmem(weight), stream)
 
 
 def logits_kernel(
@@ -462,15 +436,12 @@
     cache = kv_cache[0]
     final_row = final_gain[None]
 
-    early = out_weight.shape[1] * 5 // 8 // OUT_CHUNK * OUT_CHUNK
-
     def run_layer(payload, current, gains, cache_ready):
         parts = exchange(payload, "mp")
-        attended, current, early_weight = attend(
-            lengths, place, parts, qkv_bias, frequency, cache_ready, current, weight_out, early,
-            width,
-        )
-        return combine(spread(attended, "mp"), early_weight, current, weight_out), gains
+        attended, current = attend(
+            lengths, place, parts, qkv_bias, frequency, cache_ready, current, width
+        )
+        return combine(spread(attended, "mp"), weight_out, current), gains
 
     def share_gains(payload, current, gains, *ready):
         return current, spread(final_row, "mp")

time: 167 us -> 158 us (0.946)
  waiting for transfers between devices: 75.7 us -> 69.1 us
  Pallas kernels: 36.2 us -> 33.8 us
    ppermute x1, waiting for transfers between devices: 75.7 us -> 69.1 us  [local(): lax.ppermute(rows, 'pipe', [(i, i - 1) for i in range(1, sections, 2)])]
where the time goes in v4:
time: 158 us; the launch traced here: 157 us
  waiting for transfers between devices  69.1 us (44%)
  blocking collectives  46.8 us (30%)
  Pallas kernels  33.8 us (21%)
  starting transfers between devices  4.76 us (3%)
    ppermute x1, waiting for transfers between devices, local(): lax.ppermute(rows, 'pipe', [(i, i - 1) for i in range(1, sections, 2)])  69.1 us
    all_to_all x4, blocking collectives, exchange(): return lax.all_to_all(blocks, axis, 0, 0, tiled=True)  46.8 us
    pallas_call x4, Pallas kernels, load(): pl.pallas_call(load_kernel, in_specs=[SMEM, VMEM] + [HBM] * len(arrays),...  16.1 us
    pallas_call x3, Pallas kernels, project(): pl.pallas_call(project_kernel, in_specs=[VMEM, VMEM, VMEM], out_specs=VME...  5.73 us
    pallas_call x1, Pallas kernels, project_first(): pl.pallas_call(project_first_kernel, in_specs=[SMEM, HBM, HBM, HBM], out_...  5.06 us
  transfers between devices with their start and end apart: 5, of which 1 were waited for; matrix products, arithmetic and copies ran while one was open for 0% of the time, Pallas kernels for 10%

profile of v4, /device:TPU:0, one launch (start us, length us, event | category | flops | bytes accessed | tf_op | source)
XLA Modules:
  0.0 157.2 jit_solution(16238095636954582155)
XLA Ops:
  0.8 5.1 %project_first.1 = (bf16[8,4,5248]{2,1,0:T(4,128)(2,1)S(1)}, bf16[32,1024]{1,0:T(8,128)(2,1)S(1)}) custom-call(s32[3]{0:T(128)S(1)} %pad_add_fusion.place_ref, bf16[32,1024]{1,0:T(8,128)(2,1)} %stream_hbm.1, bf16[1,1024]{1,0:T(2,128)(2,1)} %gain_ref.5, bf16[1024,5120]{1,0:T(8,128)(2,1)} %bitcast.27), custom_call_target="tpu_custom_call" | custom-call | tf_op jit(solution)/shard_map/project_first/pallas_call | solution.py:100
  5.9 31.1 %conditional.5 = (bf16[32,1024]{1,0:T(8,128)(2,1)S(1)}, bf16[8,1,1024]{2,1,0:T(2,128)(2,1)S(1)}) conditional(s32[]{:T(128)} %clamp.15, (bf16[8,4,5248]{2,1,0:T(4,128)(2,1)S(1)}, s32[32]{0:T(128)S(1)}, s32[3]{0:T(128)S(1)}, bf16[1,5120]{1,0:T(2,128)(2,1)S(1)}, f32[1,128]{1,0:T(1,128)S(1)}, /*index=5*/bf16[4,2,4,256,128]{4,3,2,1,0:T(8,128)(2,1)S(1)}, ...), branch_computations={%region_0.1_spmd, %region_1.2_spmd} | conditional | flops 4294967296 | bytes 28770370 | solution.py:464
  5.9 16.3 %all_to_all.49.parts_ref = bf16[8,4,5248]{2,1,0:T(4,128)(2,1)S(1)} all-to-all(bf16[8,4,5248]{2,1,0:T(4,128)(2,1)S(1)} %get-tuple-element.93), channel_id=1, replica_groups=mesh['pipe'=4,'mp'=8] {'mp'}, dimensions={0} | all-to-all | bytes 671744 | tf_op jit(solution)/shard_map/cond/branch_0_fun/all_to_all | solution.py:402
  22.2 2.1 %attend.4 = (bf16[4,4096]{1,0:T(4,128)(2,1)S(1)}, bf16[32,1024]{1,0:T(8,128)(2,1)S(1)}) custom-call(s32[32]{0:T(128)S(1)} %get-tuple-element.91.lengths_ref, s32[3]{0:T(128)S(1)} %get-tuple-element.92.place_ref, bf16[8,4,5248]{2,1,0:T(4,128)(2,1)S(1)} %all_to_all.49.parts_ref, bf16[1,5120]{1,0:T(2,128)(2,1)S(1)} %get-tuple-element.94.bias_ref, ...), custom_call_target="tpu_custom_call" | custom-call | flops 4294967296 | bytes 2097152 | tf_op jit(solution)/shard_map/cond/branch_0_fun/attend/pallas_call | solution.py:253
  24.4 11.0 %all_to_all.50.gathered_ref = bf16[8,4,4096]{2,1,0:T(4,128)(2,1)S(1)} all-to-all(bf16[8,4,4096]{2,1,0:T(4,128)(2,1)S(1)} %broadcast_in_dim.19), channel_id=1, replica_groups=mesh['pipe'=4,'mp'=8] {'mp'}, dimensions={0} | all-to-all | bytes 524288 | tf_op jit(solution)/shard_map/cond/branch_0_fun/all_to_all | solution.py:402
  35.4 1.5 combine.4
  37.0 1.3 collective-permute-start
  38.4 4.6 %load.4 = (bf16[1024,5120]{1,0:T(8,128)(2,1)S(1)}, bf16[4,2,4,256,128]{4,3,2,1,0:T(8,128)(2,1)S(1)}) custom-call(s32[1]{0:T(128)} %constant.37.clone.1.order_ref, bf16[32,1024]{1,0:T(8,128)(2,1)S(1)} %get-tuple-element.156.after_ref, bf16[1024,5120]{1,0:T(8,128)(2,1)} %bitcast.28, bf16[4,2,4,256,128]{4,3,2,1,0:T(8,128)(2,1)} %bitcast.21), custom_call_target="tpu_custom_call" | custom-call | flops 25165824 | bytes 25165824 | tf_op jit(solution)/shard_map/load/pallas_call | solution.py:137
  43.0 1.9 %project.3 = bf16[8,4,5248]{2,1,0:T(4,128)(2,1)S(1)} custom-call(bf16[32,1024]{1,0:T(8,128)(2,1)S(1)} %collective-permute-done.stream_ref, bf16[1,1024]{1,0:T(2,128)(2,1)S(1)} %copy-done.1, bf16[1024,5120]{1,0:T(8,128)(2,1)S(1)} %get-tuple-element.158.weight_ref), custom_call_target="tpu_custom_call" | custom-call | tf_op jit(solution)/shard_map/project/pallas_call | solution.py:152
  44.9 10.7 %conditional.6 = ((bf16[32,1024]{1,0:T(8,128)(2,1)S(1)}, bf16[8,1,1024]{2,1,0:T(2,128)(2,1)S(1)})) conditional(s32[]{:T(128)} %clamp.14, (bf16[32,1024]{1,0:T(8,128)(2,1)S(1)}, bf16[8,1,1024]{2,1,0:T(2,128)(2,1)S(1)}) %tuple.47, (bf16[8,4,5248]{2,1,0:T(4,128)(2,1)S(1)}, s32[32]{0:T(128)S(1)}, s32[3]{0:T(128)S(1)}, ...), branch_computations={%region_2.3_spmd, %region_3.4_spmd, %region_4.5_spmd} | conditional | flops 4294967296 | bytes 28753992 | solution.py:464
  45.5 0.7 reduce.1
  46.3 9.3 %all_to_all.53 = bf16[8,2,512]{2,1,0:T(2,128)(2,1)S(1)} all-to-all(bf16[8,2,512]{2,1,0:T(2,128)(2,1)S(1)} %reshape.25), channel_id=1, replica_groups=mesh['pipe'=4,'mp'=8] {'mp'}, dimensions={0} | all-to-all | bytes 32768 | tf_op jit(solution)/shard_map/cond/branch_2_fun/all_to_all | solution.py:402
  55.6 0.7 collective-permute-start.1
  56.2 4.6 %load.5 = (bf16[1024,5120]{1,0:T(8,128)(2,1)S(1)}, bf16[4,2,4,256,128]{4,3,2,1,0:T(8,128)(2,1)S(1)}) custom-call(s32[1]{0:T(128)} %constant.38.clone.1.order_ref, bf16[32,1024]{1,0:T(8,128)(2,1)S(1)} %get-tuple-element.160.after_ref, bf16[1024,5120]{1,0:T(8,128)(2,1)} %bitcast.29, bf16[4,2,4,256,128]{4,3,2,1,0:T(8,128)(2,1)} %bitcast.22), custom_call_target="tpu_custom_call" | custom-call | flops 25165824 | bytes 25165824 | tf_op jit(solution)/shard_map/load/pallas_call | solution.py:137
  60.8 1.9 %project.4 = bf16[8,4,5248]{2,1,0:T(4,128)(2,1)S(1)} custom-call(bf16[32,1024]{1,0:T(8,128)(2,1)S(1)} %collective-permute-done.1.stream_ref, bf16[1,1024]{1,0:T(2,128)(2,1)S(1)} %copy-done.1, bf16[1024,5120]{1,0:T(8,128)(2,1)S(1)} %get-tuple-element.161.weight_ref), custom_call_target="tpu_custom_call" | custom-call | tf_op jit(solution)/shard_map/project/pallas_call | solution.py:152
  62.8 0.8 collective-permute-start.2
  63.6 4.6 %load.6 = (bf16[1024,5120]{1,0:T(8,128)(2,1)S(1)}, bf16[4,2,4,256,128]{4,3,2,1,0:T(8,128)(2,1)S(1)}) custom-call(s32[1]{0:T(128)} %constant.39.clone.1.order_ref, bf16[32,1024]{1,0:T(8,128)(2,1)S(1)} %get-tuple-element.181.after_ref, bf16[1024,5120]{1,0:T(8,128)(2,1)} %bitcast.30, bf16[4,2,4,256,128]{4,3,2,1,0:T(8,128)(2,1)} %bitcast.23), custom_call_target="tpu_custom_call" | custom-call | flops 25165824 | bytes 25165824 | tf_op jit(solution)/shard_map/load/pallas_call | solution.py:137
  68.2 1.9 %project.5 = bf16[8,4,5248]{2,1,0:T(4,128)(2,1)S(1)} custom-call(bf16[32,1024]{1,0:T(8,128)(2,1)S(1)} %collective-permute-done.2.stream_ref, bf16[1,1024]{1,0:T(2,128)(2,1)S(1)} %copy-done.1, bf16[1024,5120]{1,0:T(8,128)(2,1)S(1)} %get-tuple-element.163.weight_ref), custom_call_target="tpu_custom_call" | custom-call | tf_op jit(solution)/shard_map/project/pallas_call | solution.py:152
  71.0 1.3 collective-permute-start.4
  72.3 2.3 %load.7.early_ref = bf16[6144,384]{1,0:T(8,128)(2,1)S(1)} custom-call(s32[1]{0:T(128)} %constant.40.clone.1.order_ref, bf16[8,32,1024]{2,1,0:T(8,128)(2,1)S(1)} %get-tuple-element.183.after_ref.rows_ref, bf16[8192,384]{1,0:T(8,128)(2,1)} %source_ref.1), custom_call_target="tpu_custom_call" | custom-call | flops 12582912 | bytes 12582912 | tf_op jit(solution)/shard_map/load/pallas_call | solution.py:137
  74.6 69.1 %collective-permute-done.4.over_ref = bf16[8,32,1024]{2,1,0:T(8,128)(2,1)S(1)} collective-permute-done((bf16[8,32,1024]{2,1,0:T(8,128)(2,1)S(1)}, bf16[8,32,1024]{2,1,0:T(8,128)(2,1)S(1)}, u32[]{:S(2)}, u32[]{:S(2)}) %collective-permute-start.4) | collective-permute-done | bytes 524320 | tf_op jit(solution)/shard_map/ppermute | solution.py:481
  143.7 2.4 %final_logits.1 = (f32[32,384]{1,0:T(8,128)S(1)}, f32[1,128]{1,0:T(1,128)S(1)}) custom-call(s32[32]{0:T(128)S(1)} %copy-done.2, s32[32]{0:T(128)S(1)} %copy-done.3, s32[3]{0:T(128)S(1)} %pad_add_fusion.place_ref, bf16[8,32,1024]{2,1,0:T(8,128)(2,1)S(1)} %get-tuple-element.183.after_ref.rows_ref, bf16[8,32,1024]{2,1,0:T(8,128)(2,1)S(1)} %collective-permute-done.4.over_ref, ...), custom_call_target="tpu_custom_call" | custom-call | tf_op jit(solution)/shard_map/final_logits/pallas_call | solution.py:350
  146.2 10.3 %all_to_all.59 = f32[32,1,128]{2,1,0:T(1,128)S(1)} all-to-all(f32[32,1,128]{2,1,0:T(1,128)S(1)} %broadcast_in_dim.46), channel_id=1, replica_groups=mesh['pipe'=4,'mp'=8] {'pipe','mp'}, dimensions={0} | all-to-all | bytes 32768 | tf_op jit(solution)/shard_map/all_to_all | solution.py:402
  156.4 0.8 finish.1
  (39 shorter events, 1.7 us)
Async XLA Ops:
  0.6 5.2 %copy-start.7 = (f32[1,128]{1,0:T(1,128)S(1)}, f32[1,128]{1,0:T(1,128)}, u32[]{:S(2)}) copy-start(f32[1,128]{1,0:T(1,128)} %constant.41.clone) | copy-start | bytes 1540
  0.6 5.2 %copy-start.4 = (bf16[1024]{0:T(1024)(128)(2,1)S(1)}, bf16[1024]{0:T(1024)(128)(2,1)}, u32[]{:S(2)}) copy-start(bf16[1024]{0:T(1024)(128)(2,1)} %param.32) | copy-start | bytes 6148
  0.7 5.2 %copy-start = (bf16[1,4,2,4,256,128]{5,4,3,2,1,0:T(8,128)(2,1)S(1)}, bf16[1,4,2,4,256,128]{5,4,3,2,1,0:T(8,128)(2,1)}, u32[]{:S(2)}) copy-start(bf16[1,4,2,4,256,128]{5,4,3,2,1,0:T(8,128)(2,1)} %param.31) | copy-start | bytes 6291460
  0.7 5.2 %copy-start.6 = (s32[32]{0:T(128)S(1)}, s32[32]{0:T(128)}, u32[]{:S(2)}) copy-start(s32[32]{0:T(128)} %param.24) | copy-start | bytes 388
  0.7 5.2 %copy-start.5 = (bf16[1,5120]{1,0:T(2,128)(2,1)S(1)}, bf16[1,5120]{1,0:T(2,128)(2,1)}, u32[]{:S(2)}) copy-start(bf16[1,5120]{1,0:T(2,128)(2,1)} %param.29) | copy-start | bytes 30724
  22.2 13.2 %slice-start = ((s8[8388608]{0:T(1024)(128)(4,1)}), s8[4194304]{0:T(1024)(128)(4,1)S(1)}, s32[]{:S(2)}) async-start(s8[8388608]{0:T(1024)(128)(4,1)} %bitcast.13), calls=%async_computation.12 | async-start | bytes 8388608 | tf_op jit(solution)/shard_map/cond
  22.2 13.2 %slice-start.1 = ((s8[8388608]{0:T(1024)(128)(4,1)}), s8[4194304]{0:T(1024)(128)(4,1)S(1)}, s32[]{:S(2)}) async-start(s8[8388608]{0:T(1024)(128)(4,1)} %bitcast.13), calls=%async_computation.13 | async-start | bytes 8388608 | tf_op jit(solution)/shard_map/cond
  37.0 5.9 %collective-permute-start = (bf16[32,1024]{1,0:T(8,128)(2,1)S(1)}, bf16[32,1024]{1,0:T(8,128)(2,1)S(1)}, u32[]{:S(2)}, u32[]{:S(2)}) collective-permute-start(bf16[32,1024]{1,0:T(8,128)(2,1)S(1)} %get-tuple-element.156.after_ref), channel_id=1, source_target_pairs={{0,8},{1,9},{2,10},{3,11},{4,12},{5,13},{6,14},{7,15}} | collective-permute-start | bytes 196616 | tf_op jit(solution)/shard_map/ppermute | solution.py:467
  38.3 4.6 %copy-start.1 = (bf16[1,1024]{1,0:T(2,128)(2,1)S(1)}, bf16[1,1024]{1,0:T(2,128)(2,1)}, u32[]{:S(2)}) copy-start(bf16[1,1024]{1,0:T(2,128)(2,1)} %gain_ref.5) | copy-start | bytes 6148
  55.6 5.3 %collective-permute-start.1 = (bf16[32,1024]{1,0:T(8,128)(2,1)S(1)}, bf16[32,1024]{1,0:T(8,128)(2,1)S(1)}, u32[]{:S(2)}, u32[]{:S(2)}) collective-permute-start(bf16[32,1024]{1,0:T(8,128)(2,1)S(1)} %get-tuple-element.160.after_ref), channel_id=1, source_target_pairs={{8,16},{9,17},{10,18},{11,19},{12,20},{13,21},{14,22},{15,23}} | collective-permute-start | bytes 196616 | tf_op jit(solution)/shard_map/ppermute | solution.py:467
  62.8 5.5 %collective-permute-start.2 = (bf16[32,1024]{1,0:T(8,128)(2,1)S(1)}, bf16[32,1024]{1,0:T(8,128)(2,1)S(1)}, u32[]{:S(2)}, u32[]{:S(2)}) collective-permute-start(bf16[32,1024]{1,0:T(8,128)(2,1)S(1)} %get-tuple-element.181.after_ref), channel_id=1, source_target_pairs={{16,24},{17,25},{18,26},{19,27},{20,28},{21,29},{22,30},{23,31}} | collective-permute-start | bytes 196616 | tf_op jit(solution)/shard_map/ppermute | solution.py:467
  70.2 0.7 collective-permute-start.3
  71.0 72.8 %copy-start.2 = (s32[32]{0:T(128)S(1)}, s32[32]{0:T(128)}, u32[]{:S(2)}) copy-start(s32[32]{0:T(128)} %assign_ref.1) | copy-start | bytes 388
  71.0 72.8 %copy-start.3 = (s32[32]{0:T(128)S(1)}, s32[32]{0:T(128)}, u32[]{:S(2)}) copy-start(s32[32]{0:T(128)} %tokens_ref.1) | copy-start | bytes 388
  71.0 72.7 %collective-permute-start.4 = (bf16[8,32,1024]{2,1,0:T(8,128)(2,1)S(1)}, bf16[8,32,1024]{2,1,0:T(8,128)(2,1)S(1)}, u32[]{:S(2)}, u32[]{:S(2)}) collective-permute-start(bf16[8,32,1024]{2,1,0:T(8,128)(2,1)S(1)} %get-tuple-element.183.after_ref.rows_ref), channel_id=1, source_target_pairs={{8,0},{24,16},{9,1},{25,17},{10,2},{26,18},{11,3},{27,19},{12,4},{... | collective-permute-start | bytes 1572872 | tf_op jit(solution)/shard_map/ppermute | solution.py:481

commit v5 on v4

--- a/solution.py
+++ b/solution.py
@@ -7,6 +7,7 @@
 from jax.experimental import pallas as pl
 from jax.experimental.pallas import tpu as pltpu
 from jax.sharding import PartitionSpec as P
+
 
 HEADS = 32
 KV_HEADS = 4
@@ -17,8 +18,9 @@
 LANES = 128
 CHUNK = 512
 OUT_CHUNK = 256
-COVER = 32
-GRANT = 16 * 1024 * 1024
+COVER = 128
+RELAY_PIECES = 4
+GRANT = 10 * 1024 * 1024
 FULL_GRANT = 60 * 1024 * 1024
 
 VMEM = pl.BlockSpec(memory_space=pltpu.VMEM)
@@ -48,7 +50,7 @@
     peers, count, _ = out_ref.shape
     current = stream_ref[...].astype(jnp.float32)
     squares = jnp.sum(current * current, axis=1, keepdims=True)
-    scaled = (current * gain_ref[...].astype(jnp.float32)).astype(jnp.bfloat16)
+    scaled = (current * gain_ref[:, : stream_ref.shape[1]].astype(jnp.float32)).astype(jnp.bfloat16)
     high = squares.astype(jnp.bfloat16).astype(jnp.float32)
     middle = (squares - high).astype(jnp.bfloat16).astype(jnp.float32)
     low = squares - high - middle
@@ -74,7 +76,8 @@
 
 
 def project_first_kernel(
-    place_ref, stream_hbm, gain_hbm, source_ref, out_ref, stream_ref, gain_ref, weight_ref, sem
+    place_ref, stream_hbm, gain_hbm, source_ref, cache_hbm,
+    out_ref, stream_ref, cache_ref, gain_ref, weight_ref, sem,
 ):
     del place_ref
     columns = weight_ref.shape[1] // CHUNK
@@ -85,34 +88,38 @@
     copy_gain.start()
     for copy in copies:
         copy.start()
+    copy_cache = pltpu.make_async_copy(cache_hbm, cache_ref, sem.at[columns + 2])
+    copy_cache.start()
     copy_stream.wait()
     copy_gain.wait()
     project_body(stream_ref, gain_ref, weight_ref, out_ref, copies)
+    copy_cache.wait()
 
 
 def project_kernel(stream_ref, gain_ref, weight_ref, out_ref):
     project_body(stream_ref, gain_ref, weight_ref, out_ref, None)
 
 
-def project_first(place, stream, gain, weight, peers):
+def project_first(place, stream, gain, weight, cache, peers):
     columns = weight.shape[1]
     count = stream.shape[0] // peers
     return pl.pallas_call(
         project_first_kernel,
-        in_specs=[SMEM, HBM, HBM, HBM],
-        out_specs=[VMEM, VMEM],
+        in_specs=[SMEM] + [HBM] * 4,
+        out_specs=[VMEM] * 3,
         out_shape=[
             jax.ShapeDtypeStruct((peers, count, columns + LANES), jnp.bfloat16),
             pltpu.VMEM(stream.shape, stream.dtype),
+            pltpu.VMEM(cache.shape, cache.dtype),
         ],
         scratch_shapes=[
             pltpu.VMEM(gain.shape, gain.dtype),
             pltpu.VMEM(weight.shape, weight.dtype),
-            pltpu.SemaphoreType.DMA((columns // CHUNK + 2,)),
+            pltpu.SemaphoreType.DMA((columns // CHUNK + 3,)),
         ],
         compiler_params=pltpu.CompilerParams(vmem_limit_bytes=FULL_GRANT),
         name="project_first",
-    )(place, in_hbm(stream), in_hbm(gain), in_hbm(weight))
+    )(place, in_hbm(stream), in_hbm(gain), in_hbm(weight), in_hbm(cache))
 
 
 def load_kernel(order_ref, after_ref, *refs):
@@ -146,6 +153,46 @@
     )(jnp.full((1,), order, jnp.int32), after, *[in_hbm(array) for array in arrays])
 
 
+def relay_kernel(source_ref, out_ref, buffer_ref, sem_in, sem_out):
+    pieces = sem_in.shape[0]
+    size = source_ref.shape[0] // pieces
+    spans = [pl.ds(i * size, size) for i in range(pieces)]
+    arrive = [
+        pltpu.make_async_copy(source_ref.at[span], buffer_ref.at[span], sem_in.at[i])
+        for i, span in enumerate(spans)
+    ]
+    leave = [
+        pltpu.make_async_copy(buffer_ref.at[span], out_ref.at[span], sem_out.at[i])
+        for i, span in enumerate(spans)
+    ]
+    for copy in arrive:
+        copy.start()
+    for i in range(pieces):
+        arrive[i].wait()
+        leave[i].start()
+    for copy in leave:
+        copy.wait()
+
+
+def relay(array):
+    return pl.pallas_call(
+        relay_kernel,
+        in_specs=[HBM],
+        out_specs=pl.BlockSpec(memory_space=pl.ANY),
+        out_shape=jax.ShapeDtypeStruct(array.shape, array.dtype),
+        scratch_shapes=[
+            pltpu.VMEM(array.shape, array.dtype),
+            pltpu.SemaphoreType.DMA((RELAY_PIECES,)),
+            pltpu.SemaphoreType.DMA((RELAY_PIECES,)),
+        ],
+        compiler_params=PARAMS,
+        cost_estimate=pl.CostEstimate(
+            flops=4 * array.size, bytes_accessed=4 * array.size, transcendentals=0
+        ),
+        name="relay",
+    )(in_hbm(array))
+
+
 def project(stream, gain, weight, peers):
     columns = weight.shape[1]
     count = stream.shape[0] // peers
@@ -157,6 +204,30 @@
         compiler_params=PARAMS,
         name="project",
     )(stream, gain, in_vmem(weight))
+
+
+def project_load_kernel(stream_ref, gain_ref, weight_ref, cache_hbm, out_ref, cache_ref, sem):
+    copy = pltpu.make_async_copy(cache_hbm, cache_ref, sem.at[0])
+    copy.start()
+    project_body(stream_ref, gain_ref, weight_ref, out_ref, None)
+    copy.wait()
+
+
+def project_load(stream, gain, weight, cache, peers):
+    columns = weight.shape[1]
+    count = stream.shape[0] // peers
+    return pl.pallas_call(
+        project_load_kernel,
+        in_specs=[VMEM, VMEM, VMEM, HBM],
+        out_specs=[VMEM, VMEM],
+        out_shape=[
+            jax.ShapeDtypeStruct((peers, count, columns + LANES), jnp.bfloat16),
+            pltpu.VMEM(cache.shape, cache.dtype),
+        ],
+        scratch_shapes=[pltpu.SemaphoreType.DMA((1,))],
+        compiler_params=PARAMS,
+        name="project_load",
+    )(stream, gain, in_vmem(weight), in_hbm(cache))
 
 
 def attend_body(lengths_ref, place_ref, parts_ref, bias_ref, frequency_ref, cache, out_ref, width):
@@ -192,7 +263,8 @@
     inverse = lax.rsqrt(squares / width + EPS)
 
     def columns_of(at):
-        bias = bias_ref[:, at : at + HEAD_DIM].astype(jnp.float32)
+        shifted = at + bias_ref.shape[1] - (query_cols + 2 * key_cols)
+        bias = bias_ref[:, shifted : shifted + HEAD_DIM].astype(jnp.float32)
         return total_of(at, HEAD_DIM) * inverse + bias
 
     def rotate(head):
@@ -289,38 +361,52 @@
     )(gathered, in_vmem(weight), stream)
 
 
+def total_square(ref):
+    pieces, requests, _ = ref.shape
+    squares = jnp.zeros((requests, 1), jnp.float32)
+    for m in range(pieces):
+        current = ref[m].astype(jnp.float32)
+        squares = squares + jnp.sum(current * current, axis=1, keepdims=True)
+    return squares
+
+
+def square_kernel(rows_ref, out_ref):
+    out_ref[...] = total_square(rows_ref)
+
+
+def row_squares(rows):
+    return pl.pallas_call(
+        square_kernel,
+        in_specs=[VMEM],
+        out_specs=VMEM,
+        out_shape=jax.ShapeDtypeStruct((rows.shape[1], 1), jnp.float32),
+        compiler_params=PARAMS,
+        cost_estimate=pl.CostEstimate(
+            flops=COVER * rows.size * HEADS * LANES // 8, bytes_accessed=rows.size, transcendentals=0
+        ),
+        name="row_squares",
+    )(rows)
+
+
 def logits_kernel(
-    assign_ref, tokens_ref, place_ref, rows_ref, over_ref, gain_ref, early_ref, source_ref,
-    logits_ref, stats_ref, scratch_ref, late_ref, sem, *, width,
+    assign_ref, tokens_ref, place_ref, rows_ref, over_ref, own_ref, gain_ref, weight_ref,
+    logits_ref, stats_ref, scratch_ref, inverse_ref, *, width,
 ):
     pieces, requests, share = rows_ref.shape
-    vocab = early_ref.shape[1]
-    early = early_ref.shape[0] // share
-    copies = []
-    for i in range(pieces - early):
-        copies.append(
-            pltpu.make_async_copy(
-                source_ref.at[pl.ds((early + i) * share, share)],
-                late_ref.at[pl.ds(i * share, share)],
-                sem.at[i],
-            )
-        )
-        copies[i].start()
+    vocab = weight_ref.shape[1]
     own = place_ref[2] == 1
-    squares = jnp.zeros((requests, 1), jnp.float32)
-    for m in range(pieces):
-        current = jnp.where(own, rows_ref[m], over_ref[m]).astype(jnp.float32)
-        squares = squares + jnp.sum(current * current, axis=1, keepdims=True)
-    inverse = lax.rsqrt(squares / width + EPS)
+    inverse_ref[...] = lax.rsqrt(own_ref[...] / width + EPS)
+
+    @pl.when(place_ref[2] != 1)
+    def _():
+        inverse_ref[...] = lax.rsqrt(total_square(over_ref) / width + EPS)
+
+    inverse = inverse_ref[...]
     logits = jnp.zeros((requests, vocab), jnp.float32)
     for m in range(pieces):
         current = jnp.where(own, rows_ref[m], over_ref[m]).astype(jnp.float32)
         normed = (current * gain_ref[m].astype(jnp.float32) * inverse).astype(jnp.bfloat16)
-        if m < early:
-            weight = early_ref[m * share : (m + 1) * share]
-        else:
-            copies[m - early].wait()
-            weight = late_ref[(m - early) * share : (m - early + 1) * share]
+        weight = weight_ref[m * share : (m + 1) * share]
         logits = logits + jnp.dot(normed, weight, preferred_element_type=jnp.float32)
     scratch_ref[...] = logits
     row = lax.broadcasted_iota(jnp.int32, (requests, vocab), 0)
@@ -342,14 +428,13 @@
     stats_ref[...] = jnp.sum(spread_out, axis=0, keepdims=True)
 
 
-def final_logits(assign, tokens, place, rows, over, gain, early, weight, width):
-    pieces, requests, share = rows.shape
+def final_logits(assign, tokens, place, rows, over, own, gain, weight, width):
+    requests = rows.shape[1]
     vocab = weight.shape[1]
-    late = weight.shape[0] - early.shape[0]
     lanes = -(-3 * requests // LANES) * LANES
     return pl.pallas_call(
         functools.partial(logits_kernel, width=width),
-        in_specs=[SMEM, SMEM, SMEM, VMEM, VMEM, VMEM, VMEM, HBM],
+        in_specs=[SMEM] * 3 + [VMEM] * 5,
         out_specs=[VMEM, VMEM],
         out_shape=[
             jax.ShapeDtypeStruct((requests, vocab), jnp.float32),
@@ -357,12 +442,11 @@
         ],
         scratch_shapes=[
             pltpu.VMEM((requests, vocab), jnp.float32),
-            pltpu.VMEM((late, vocab), weight.dtype),
-            pltpu.SemaphoreType.DMA((late // share,)),
+            pltpu.VMEM((requests, 1), jnp.float32),
         ],
         compiler_params=PARAMS,
         name="final_logits",
-    )(assign, tokens, place, rows, over, gain, in_vmem(early), in_hbm(weight))
+    )(assign, tokens, place, rows, over, own, gain, in_vmem(weight))
 
 
 def finish_kernel(logits_ref, stats_ref, out_ref, chosen_ref):
@@ -436,12 +520,20 @@
     cache = kv_cache[0]
     final_row = final_gain[None]
 
-    def run_layer(payload, current, gains, cache_ready):
+    def layer_step(payload, current, cache_here, weight_here, bias_here):
         parts = exchange(payload, "mp")
         attended, current = attend(
-            lengths, place, parts, qkv_bias, frequency, cache_ready, current, width
-        )
-        return combine(spread(attended, "mp"), weight_out, current), gains
+            lengths, place, parts, bias_here, frequency, cache_here, current, width
+        )
+        return combine(spread(attended, "mp"), weight_here, current)
+
+    def run_one(payload, current, gains, cache_ready):
+        return layer_step(payload, current, cache_ready, weight_out, qkv_bias), gains
+
+    def run_two(payload, current, gains, cache_ready, out_moved, bias_moved):
+        current = layer_step(payload, current, cache_ready, out_moved, bias_moved)
+        payload, cache_own = project_load(current, attn_gain, weight_in, cache, peers)
+        return layer_step(payload, current, cache_own, weight_out, qkv_bias), gains
 
     def share_gains(payload, current, gains, *ready):
         return current, spread(final_row, "mp")
@@ -449,22 +541,37 @@
     def skip(payload, current, gains, *ready):
         return current, gains
 
+    def move(array):
+        return lax.ppermute(array, "pipe", [(i, i + 1) for i in range(2, sections, 2)])
+
     gain_full = jnp.zeros((peers, 1, share), final_gain.dtype)
-    for layer in range(sections):
-        active = section == layer
-        if layer == 0:
-            payload, stream = project_first(place, hidden_in, attn_gain, weight_in, peers)
-            branch = jnp.where(active, 0, 1)
-            branches = (run_layer, share_gains)
-            ready = [cache]
-        else:
-            payload = project(stream, attn_gain, in_ready, peers)
-            branch = jnp.where(active, 1, jnp.where(section == 0, 2, 0) if layer == 1 else 0)
-            branches = (skip, run_layer, share_gains) if layer == 1 else (skip, run_layer)
-        stream, gain_full = lax.switch(branch, branches, payload, stream, gain_full, *ready)
-        if layer + 1 < sections:
-            in_ready, *ready = load(layer, stream, [weight_in, cache])
-            stream = lax.ppermute(stream, "pipe", [(layer, layer + 1)])
+    small = move(jnp.concatenate([attn_gain, qkv_bias], axis=1))
+    in_moved, cache_moved, out_moved = move(weight_in), move(cache), move(weight_out)
+
+    payload, stream, cache_ready = project_first(
+        place, hidden_in, attn_gain, weight_in, cache, peers
+    )
+    stream, gain_full = lax.switch(
+        jnp.where(section == 0, 0, 1), (run_one, share_gains), payload, stream, gain_full,
+        cache_ready,
+    )
+    in_ready, cache_ready = load(0, stream, [weight_in, cache])
+    stream = lax.ppermute(stream, "pipe", [(0, 1)])
+
+    payload = project(stream, attn_gain, in_ready, peers)
+    stream, gain_full = lax.switch(
+        jnp.where(section == 1, 1, jnp.where(section == 0, 2, 0)),
+        (skip, run_one, share_gains), payload, stream, gain_full, cache_ready,
+    )
+    for top in range(3, sections, 2):
+        in_ready, cache_ready = load(top, stream, [in_moved, cache_moved])
+        out_here = relay(out_moved)
+        stream = lax.ppermute(stream, "pipe", [(top - 2, top)])
+        payload = project(stream, small, in_ready, peers)
+        stream, gain_full = lax.switch(
+            (section == top).astype(jnp.int32),
+            (skip, run_two), payload, stream, gain_full, cache_ready, out_here, small,
+        )
 
     last = sections - 1
     arrived = stream
@@ -477,11 +584,10 @@
         lambda b: jnp.broadcast_to(b[None], (peers,) + b.shape),
         arrived,
     )
-    (head_ready,) = load(sections, rows, [head_weight], width * 3 // 4)
     over = lax.ppermute(rows, "pipe", [(i, i - 1) for i in range(1, sections, 2)])
 
     logits, stats = final_logits(
-        assign, token_ids, place, rows, over, gain_full, head_ready, head_weight, width
+        assign, token_ids, place, rows, over, row_squares(rows), gain_full, head_weight, width
     )
     stats = spread(stats, ("pipe", "mp"))
     logprobs, chosen = finish(logits, stats.reshape(stats.shape[0], stats.shape[2]))

time: 158 us -> 163 us (1.032)
  starting transfers between devices: 4.76 us -> 15.7 us
  waiting for transfers between devices: 69.1 us -> 65.8 us
  Pallas kernels: 33.8 us -> 32.1 us
    ppermute x3 -> x6, starting transfers between devices: 2.8 us -> 13.5 us  [the longest x4 11.6 us: move(): lax.ppermute(array, 'pipe', [(i, i + 1) for i in range(2, sections, 2)])]
    pallas_call x1 -> x3, Pallas kernels: 5.06 us -> 12.6 us  [the longest x1 6.95 us: relay(): pl.pallas_call(relay_kernel, in_specs=[HBM], out_specs=pl.BlockSpec(memor...]
    pallas_call x4 -> x2, Pallas kernels: 16.1 us -> 9.19 us  [load(): pl.pallas_call(load_kernel, in_specs=[SMEM, VMEM] + [HBM] * len(arrays),...]
    ppermute x1, waiting for transfers between devices: 69.1 us -> 65.8 us  [local(): lax.ppermute(rows, 'pipe', [(i, i - 1) for i in range(1, sections, 2)])]
    pallas_call x3 -> x2, Pallas kernels: 5.73 us -> 3.82 us  [project(): pl.pallas_call(project_kernel, in_specs=[VMEM, VMEM, VMEM], out_specs=VME...]
  transfers between devices with their start and end apart: 5 -> 8, of which waited for: 1 -> 1; matrix products, arithmetic and copies ran while one was open for 0% -> 1% of each run, Pallas kernels for 10% -> 17%
where the time goes in v5:
time: 163 us
  waiting for transfers between devices  65.8 us (40%)
  blocking collectives  46.3 us (28%)
  Pallas kernels  32.1 us (20%)
  starting transfers between devices  15.7 us (10%)
    ppermute x1, waiting for transfers between devices, local(): lax.ppermute(rows, 'pipe', [(i, i - 1) for i in range(1, sections, 2)])  65.8 us
    all_to_all x4, blocking collectives, exchange(): return lax.all_to_all(blocks, axis, 0, 0, tiled=True)  46.3 us
    ppermute x4, starting transfers between devices, move(): lax.ppermute(array, 'pipe', [(i, i + 1) for i in range(2, sections, 2)])  11.6 us
    pallas_call x2, Pallas kernels, load(): pl.pallas_call(load_kernel, in_specs=[SMEM, VMEM] + [HBM] * len(arrays),...  9.19 us
    pallas_call x1, Pallas kernels, relay(): pl.pallas_call(relay_kernel, in_specs=[HBM], out_specs=pl.BlockSpec(memor...  6.95 us
    pallas_call x1, Pallas kernels, project_first(): pl.pallas_call(project_first_kernel, in_specs=[SMEM] + [HBM] * 4, out_spe...  5.46 us
    pallas_call x2, Pallas kernels, project(): pl.pallas_call(project_kernel, in_specs=[VMEM, VMEM, VMEM], out_specs=VME...  3.82 us
  transfers between devices with their start and end apart: 8, of which 1 were waited for; matrix products, arithmetic and copies ran while one was open for 1% of the time, Pallas kernels for 17%

profile of v5, /device:TPU:0, one launch (start us, length us, event | category | flops | bytes accessed | tf_op | source)
XLA Modules:
  0.0 163.0 jit_solution(2622406102864412659)
XLA Ops:
  0.7 4.8 %collective-permute-start.3 = (bf16[1024,5120]{1,0:T(8,128)(2,1)}, bf16[1024,5120]{1,0:T(8,128)(2,1)}, u32[]{:S(2)}, u32[]{:S(2)}) collective-permute-start(bf16[1024,5120]{1,0:T(8,128)(2,1)} %bitcast.9), channel_id=1, source_target_pairs={{16,24},{17,25},{18,26},{19,27},{20,28},{21,29},{22,30},{23,31}} | collective-permute-start | bytes 31457288 | tf_op jit(solution)/shard_map/ppermute | solution.py:545
  5.5 4.0 %collective-permute-start.5 = (bf16[4096,1024]{1,0:T(8,128)(2,1)}, bf16[4096,1024]{1,0:T(8,128)(2,1)}, u32[]{:S(2)}, u32[]{:S(2)}) collective-permute-start(bf16[4096,1024]{1,0:T(8,128)(2,1)} %bitcast.15), channel_id=1, source_target_pairs={{16,24},{17,25},{18,26},{19,27},{20,28},{21,29},{22,30},{23,31}} | collective-permute-start | bytes 25165832 | tf_op jit(solution)/shard_map/ppermute | solution.py:545
  9.5 2.1 %collective-permute-start.4 = (bf16[4,2,4,256,128]{4,3,2,1,0:T(8,128)(2,1)}, bf16[4,2,4,256,128]{4,3,2,1,0:T(8,128)(2,1)}, u32[]{:S(2)}, u32[]{:S(2)}) collective-permute-start(bf16[4,2,4,256,128]{4,3,2,1,0:T(8,128)(2,1)} %bitcast.31), channel_id=1, source_target_pairs={{16,24},{17,25},{18,26},{19,27},{20,28},{21,29},{22,30},{23,31}} | collective-permute-start | bytes 6291464 | tf_op jit(solution)/shard_map/ppermute | solution.py:545
  11.6 5.5 %project_first.1 = (bf16[8,4,5248]{2,1,0:T(4,128)(2,1)S(1)}, bf16[32,1024]{1,0:T(8,128)(2,1)S(1)}, bf16[4,2,4,256,128]{4,3,2,1,0:T(8,128)(2,1)S(1)}) custom-call(s32[3]{0:T(128)S(1)} %pad_add_fusion.place_ref, bf16[32,1024]{1,0:T(8,128)(2,1)} %stream_hbm.1, bf16[1,1024]{1,0:T(2,128)(2,1)} %gain_ref.1, bf16[1024,5120]{1,0:T(8,128)(2,1)} %bitcast.10, ...), custom_call_target="tpu_custom_call" | custom-call | tf_op jit(solution)/shard_map/project_first/pallas_call | solution.py:106
  17.2 31.3 %conditional.4 = (bf16[32,1024]{1,0:T(8,128)(2,1)S(1)}, bf16[8,1,1024]{2,1,0:T(2,128)(2,1)S(1)}) conditional(s32[]{:T(128)} %clamp.11, (bf16[8,4,5248]{2,1,0:T(4,128)(2,1)S(1)}, s32[32]{0:T(128)S(1)}, s32[3]{0:T(128)S(1)}, bf16[1,5120]{1,0:T(2,128)(2,1)S(1)}, f32[1,128]{1,0:T(1,128)S(1)}, /*index=5*/bf16[4,2,4,256,128]{4,3,2,1,0:T(8,128)(2,1)S(1)}, ...), branch_computations={%region_0.1_spmd, %region_1.2_spmd} | conditional | flops 17179869184 | bytes 28770370 | solution.py:554
  17.2 16.6 %all_to_all.49.parts_ref = bf16[8,4,5248]{2,1,0:T(4,128)(2,1)S(1)} all-to-all(bf16[8,4,5248]{2,1,0:T(4,128)(2,1)S(1)} %get-tuple-element.83), channel_id=1, replica_groups=mesh['pipe'=4,'mp'=8] {'mp'}, dimensions={0} | all-to-all | bytes 671744 | tf_op jit(solution)/shard_map/cond/branch_0_fun/all_to_all | solution.py:486
  33.8 2.1 %attend.4 = (bf16[4,4096]{1,0:T(4,128)(2,1)S(1)}, bf16[32,1024]{1,0:T(8,128)(2,1)S(1)}) custom-call(s32[32]{0:T(128)S(1)} %get-tuple-element.81.lengths_ref, s32[3]{0:T(128)S(1)} %get-tuple-element.82.place_ref, bf16[8,4,5248]{2,1,0:T(4,128)(2,1)S(1)} %all_to_all.49.parts_ref, bf16[1,5120]{1,0:T(2,128)(2,1)S(1)} %get-tuple-element.84.bias_ref, ...), custom_call_target="tpu_custom_call" | custom-call | flops 17179869184 | bytes 2097152 | tf_op jit(solution)/shard_map/cond/branch_0_fun/attend/pallas_call | solution.py:325
  35.9 10.9 %all_to_all.50.gathered_ref = bf16[8,4,4096]{2,1,0:T(4,128)(2,1)S(1)} all-to-all(bf16[8,4,4096]{2,1,0:T(4,128)(2,1)S(1)} %broadcast_in_dim.19), channel_id=1, replica_groups=mesh['pipe'=4,'mp'=8] {'mp'}, dimensions={0} | all-to-all | bytes 524288 | tf_op jit(solution)/shard_map/cond/branch_0_fun/all_to_all | solution.py:486
  46.8 1.5 combine.4
  48.4 1.3 collective-permute-start
  49.8 4.6 %load.2 = (bf16[1024,5120]{1,0:T(8,128)(2,1)S(1)}, bf16[4,2,4,256,128]{4,3,2,1,0:T(8,128)(2,1)S(1)}) custom-call(s32[1]{0:T(128)} %constant.35.clone.1.order_ref, bf16[32,1024]{1,0:T(8,128)(2,1)S(1)} %get-tuple-element.145.after_ref, bf16[1024,5120]{1,0:T(8,128)(2,1)} %bitcast.11, bf16[4,2,4,256,128]{4,3,2,1,0:T(8,128)(2,1)} %bitcast.33), custom_call_target="tpu_custom_call" | custom-call | flops 25165824 | bytes 25165824 | tf_op jit(solution)/shard_map/load/pallas_call | solution.py:144
  54.4 1.9 %project.2 = bf16[8,4,5248]{2,1,0:T(4,128)(2,1)S(1)} custom-call(bf16[32,1024]{1,0:T(8,128)(2,1)S(1)} %collective-permute-done.stream_ref, bf16[1,1024]{1,0:T(2,128)(2,1)S(1)} %copy-done.2, bf16[1024,5120]{1,0:T(8,128)(2,1)S(1)} %get-tuple-element.147.weight_ref), custom_call_target="tpu_custom_call" | custom-call | tf_op jit(solution)/shard_map/project/pallas_call | solution.py:199
  56.3 10.7 %conditional.5 = ((bf16[32,1024]{1,0:T(8,128)(2,1)S(1)}, bf16[8,1,1024]{2,1,0:T(2,128)(2,1)S(1)})) conditional(s32[]{:T(128)} %clamp.10, (bf16[32,1024]{1,0:T(8,128)(2,1)S(1)}, bf16[8,1,1024]{2,1,0:T(2,128)(2,1)S(1)}) %tuple.41, (bf16[8,4,5248]{2,1,0:T(4,128)(2,1)S(1)}, s32[32]{0:T(128)S(1)}, s32[3]{0:T(128)S(1)}, ...), branch_computations={%region_2.3_spmd, %region_3.4_spmd, %region_4.5_spmd} | conditional | flops 17179869184 | bytes 28753992 | solution.py:562
  56.9 0.8 reduce.1
  57.7 9.3 %all_to_all.53 = bf16[8,2,512]{2,1,0:T(2,128)(2,1)S(1)} all-to-all(bf16[8,2,512]{2,1,0:T(2,128)(2,1)S(1)} %reshape.25), channel_id=1, replica_groups=mesh['pipe'=4,'mp'=8] {'mp'}, dimensions={0} | all-to-all | bytes 32768 | tf_op jit(solution)/shard_map/cond/branch_2_fun/all_to_all | solution.py:486
  68.4 7.0 %relay.1 = bf16[4096,1024]{1,0:T(8,128)(2,1)} custom-call(bf16[4096,1024]{1,0:T(8,128)(2,1)} %collective-permute-done.5.source_ref), custom_call_target="tpu_custom_call" | custom-call | flops 16777216 | bytes 16777216 | tf_op jit(solution)/shard_map/relay/pallas_call | solution.py:178
  75.4 4.6 %load.3 = (bf16[1024,5120]{1,0:T(8,128)(2,1)S(1)}, bf16[4,2,4,256,128]{4,3,2,1,0:T(8,128)(2,1)S(1)}) custom-call(s32[1]{0:T(128)} %constant.36.clone.1.order_ref, bf16[32,1024]{1,0:T(8,128)(2,1)S(1)} %get-tuple-element.149.after_ref, bf16[1024,5120]{1,0:T(8,128)(2,1)} %collective-permute-done.3.refs_0_, ...), custom_call_target="tpu_custom_call" | custom-call | flops 25165824 | bytes 25165824 | tf_op jit(solution)/shard_map/load/pallas_call | solution.py:144
  80.0 1.9 %project.3 = bf16[8,4,5248]{2,1,0:T(4,128)(2,1)S(1)} custom-call(bf16[32,1024]{1,0:T(8,128)(2,1)S(1)} %collective-permute-done.1.stream_ref, bf16[1,6144]{1,0:T(2,128)(2,1)S(1)} %collective-permute-done.2.gain_ref, bf16[1024,5120]{1,0:T(8,128)(2,1)S(1)} %get-tuple-element.150.weight_ref), custom_call_target="tpu_custom_call" | custom-call | tf_op jit(solution)/shard_map/project/pallas_call | solution.py:199
  82.2 0.7 collective-permute-start.6
  83.0 1.6 collective-permute-start.7
  84.7 65.8 %collective-permute-done.7.over_ref = bf16[8,32,1024]{2,1,0:T(8,128)(2,1)S(1)} collective-permute-done((bf16[8,32,1024]{2,1,0:T(8,128)(2,1)S(1)}, bf16[8,32,1024]{2,1,0:T(8,128)(2,1)S(1)}, u32[]{:S(2)}, u32[]{:S(2)}) %collective-permute-start.7) | collective-permute-done | bytes 524320 | tf_op jit(solution)/shard_map/ppermute | solution.py:587
  150.5 2.0 %final_logits.1 = (f32[32,384]{1,0:T(8,128)S(1)}, f32[1,128]{1,0:T(1,128)S(1)}) custom-call(s32[32]{0:T(128)S(1)} %copy-done, s32[32]{0:T(128)S(1)} %copy-done.1, s32[3]{0:T(128)S(1)} %pad_add_fusion.place_ref, bf16[8,32,1024]{2,1,0:T(8,128)(2,1)S(1)} %get-tuple-element.169.rows_ref, bf16[8,32,1024]{2,1,0:T(8,128)(2,1)S(1)} %collective-permute-done.7.over_ref, ...), custom_call_target="tpu_custom_call" | custom-call | tf_op jit(solution)/shard_map/final_logits/pallas_call | solution.py:435
  152.6 9.6 %all_to_all.59 = f32[32,1,128]{2,1,0:T(1,128)S(1)} all-to-all(f32[32,1,128]{2,1,0:T(1,128)S(1)} %broadcast_in_dim.46), channel_id=1, replica_groups=mesh['pipe'=4,'mp'=8] {'pipe','mp'}, dimensions={0} | all-to-all | bytes 32768 | tf_op jit(solution)/shard_map/all_to_all | solution.py:486
  162.2 0.8 finish.1
  (47 shorter events, 2.8 us)
Async XLA Ops:
  0.6 16.5 %copy-start.6 = (f32[1,128]{1,0:T(1,128)S(1)}, f32[1,128]{1,0:T(1,128)}, u32[]{:S(2)}) copy-start(f32[1,128]{1,0:T(1,128)} %constant.37.clone) | copy-start | bytes 1540
  0.6 16.5 %copy-start.4 = (bf16[1024]{0:T(1024)(128)(2,1)S(1)}, bf16[1024]{0:T(1024)(128)(2,1)}, u32[]{:S(2)}) copy-start(bf16[1024]{0:T(1024)(128)(2,1)} %param.30) | copy-start | bytes 6148
  0.7 16.5 %copy-start.5 = (s32[32]{0:T(128)S(1)}, s32[32]{0:T(128)}, u32[]{:S(2)}) copy-start(s32[32]{0:T(128)} %param.22) | copy-start | bytes 388
  0.7 16.5 %copy-start.3 = (bf16[1,5120]{1,0:T(2,128)(2,1)S(1)}, bf16[1,5120]{1,0:T(2,128)(2,1)}, u32[]{:S(2)}) copy-start(bf16[1,5120]{1,0:T(2,128)(2,1)} %param.27) | copy-start | bytes 30724
  0.7 74.7 %collective-permute-start.3 = (bf16[1024,5120]{1,0:T(8,128)(2,1)}, bf16[1024,5120]{1,0:T(8,128)(2,1)}, u32[]{:S(2)}, u32[]{:S(2)}) collective-permute-start(bf16[1024,5120]{1,0:T(8,128)(2,1)} %bitcast.9), channel_id=1, source_target_pairs={{16,24},{17,25},{18,26},{19,27},{20,28},{21,29},{22,30},{23,31}} | collective-permute-start | bytes 31457288 | tf_op jit(solution)/shard_map/ppermute | solution.py:545
  5.5 62.9 %collective-permute-start.5 = (bf16[4096,1024]{1,0:T(8,128)(2,1)}, bf16[4096,1024]{1,0:T(8,128)(2,1)}, u32[]{:S(2)}, u32[]{:S(2)}) collective-permute-start(bf16[4096,1024]{1,0:T(8,128)(2,1)} %bitcast.15), channel_id=1, source_target_pairs={{16,24},{17,25},{18,26},{19,27},{20,28},{21,29},{22,30},{23,31}} | collective-permute-start | bytes 25165832 | tf_op jit(solution)/shard_map/ppermute | solution.py:545
  9.5 65.9 %collective-permute-start.4 = (bf16[4,2,4,256,128]{4,3,2,1,0:T(8,128)(2,1)}, bf16[4,2,4,256,128]{4,3,2,1,0:T(8,128)(2,1)}, u32[]{:S(2)}, u32[]{:S(2)}) collective-permute-start(bf16[4,2,4,256,128]{4,3,2,1,0:T(8,128)(2,1)} %bitcast.31), channel_id=1, source_target_pairs={{16,24},{17,25},{18,26},{19,27},{20,28},{21,29},{22,30},{23,31}} | collective-permute-start | bytes 6291464 | tf_op jit(solution)/shard_map/ppermute | solution.py:545
  17.2 29.7 %slice-start.3 = ((s8[8388608]{0:T(1024)(128)(4,1)}), s8[4194304]{0:T(1024)(128)(4,1)S(1)}, s32[]{:S(2)}) async-start(s8[8388608]{0:T(1024)(128)(4,1)} %bitcast.19), calls=%async_computation.15 | async-start | bytes 8388608 | tf_op jit(solution)/shard_map/cond
  33.8 13.1 %slice-start.4 = ((s8[8388608]{0:T(1024)(128)(4,1)}), s8[4194304]{0:T(1024)(128)(4,1)S(1)}, s32[]{:S(2)}) async-start(s8[8388608]{0:T(1024)(128)(4,1)} %bitcast.19), calls=%async_computation.16 | async-start | bytes 8388608 | tf_op jit(solution)/shard_map/cond
  48.4 5.9 %copy-start.2 = (bf16[1,1024]{1,0:T(2,128)(2,1)S(1)}, bf16[1,1024]{1,0:T(2,128)(2,1)}, u32[]{:S(2)}) copy-start(bf16[1,1024]{1,0:T(2,128)(2,1)} %gain_ref.1) | copy-start | bytes 6148
  48.4 5.9 %collective-permute-start = (bf16[32,1024]{1,0:T(8,128)(2,1)S(1)}, bf16[32,1024]{1,0:T(8,128)(2,1)S(1)}, u32[]{:S(2)}, u32[]{:S(2)}) collective-permute-start(bf16[32,1024]{1,0:T(8,128)(2,1)S(1)} %get-tuple-element.145.after_ref), channel_id=1, source_target_pairs={{0,8},{1,9},{2,10},{3,11},{4,12},{5,13},{6,14},{7,15}} | collective-permute-start | bytes 196616 | tf_op jit(solution)/shard_map/ppermute | solution.py:559
  67.0 13.0 %collective-permute-start.1 = (bf16[32,1024]{1,0:T(8,128)(2,1)S(1)}, bf16[32,1024]{1,0:T(8,128)(2,1)S(1)}, u32[]{:S(2)}, u32[]{:S(2)}) collective-permute-start(bf16[32,1024]{1,0:T(8,128)(2,1)S(1)} %get-tuple-element.149.after_ref), channel_id=1, source_target_pairs={{8,24},{9,25},{10,26},{11,27},{12,28},{13,29},{14,30},{15,31}} | collective-permute-start | bytes 196616 | tf_op jit(solution)/shard_map/ppermute | solution.py:569
  67.7 12.3 %collective-permute-start.2 = (bf16[1,6144]{1,0:T(2,128)(2,1)S(1)}, bf16[1,6144]{1,0:T(2,128)(2,1)S(1)}, u32[]{:S(2)}, u32[]{:S(2)}) collective-permute-start(bf16[1,6144]{1,0:T(2,128)(2,1)S(1)} %pad_maximum_fusion), channel_id=1, source_target_pairs={{16,24},{17,25},{18,26},{19,27},{20,28},{21,29},{22,30},{23,31}} | collective-permute-start | bytes 36872 | tf_op jit(solution)/shard_map/ppermute | solution.py:545
  82.2 0.7 collective-permute-start.6
  82.9 67.6 %slice-start.11 = ((s8[6291456]{0:T(1024)(128)(4,1)}), s8[2097152]{0:T(1024)(128)(4,1)S(1)}, s32[]{:S(2)}) async-start(s8[6291456]{0:T(1024)(128)(4,1)} %bitcast.27), calls=%async_computation.23 | async-start | bytes 4194304
  83.0 67.5 %slice-start.12 = ((s8[6291456]{0:T(1024)(128)(4,1)}), s8[4194304]{0:T(1024)(128)(4,1)S(1)}, s32[]{:S(2)}) async-start(s8[6291456]{0:T(1024)(128)(4,1)} %bitcast.27), calls=%async_computation.24 | async-start | bytes 8388608
  83.0 67.5 %copy-start = (s32[32]{0:T(128)S(1)}, s32[32]{0:T(128)}, u32[]{:S(2)}) copy-start(s32[32]{0:T(128)} %assign_ref.1) | copy-start | bytes 388
  83.0 67.5 %copy-start.1 = (s32[32]{0:T(128)S(1)}, s32[32]{0:T(128)}, u32[]{:S(2)}) copy-start(s32[32]{0:T(128)} %tokens_ref.1) | copy-start | bytes 388
  83.0 67.5 %collective-permute-start.7 = (bf16[8,32,1024]{2,1,0:T(8,128)(2,1)S(1)}, bf16[8,32,1024]{2,1,0:T(8,128)(2,1)S(1)}, u32[]{:S(2)}, u32[]{:S(2)}) collective-permute-start(bf16[8,32,1024]{2,1,0:T(8,128)(2,1)S(1)} %get-tuple-element.169.rows_ref), channel_id=1, source_target_pairs={{8,0},{24,16},{9,1},{25,17},{10,2},{26,18},{11,3},{27,19},{12,4},{... | collective-permute-start | bytes 1572872 | tf_op jit(solution)/shard_map/ppermute | solution.py:587

commit v6 on v5

--- a/solution.py
+++ b/solution.py
@@ -239,14 +239,14 @@
     at_row = lax.broadcasted_iota(jnp.int32, (count, HEAD_DIM), 0)
     positions = jnp.zeros((count, HEAD_DIM), jnp.int32)
     wide = (GROUP * count, count * length)
-    rows = lax.broadcasted_iota(jnp.int32, wide, 0) % count
-    columns = lax.broadcasted_iota(jnp.int32, wide, 1)
-    visible = columns < 0
+    at_wide = lax.broadcasted_iota(jnp.int32, (GROUP * count, 1), 0) % count
+    limit = jnp.zeros((GROUP * count, 1), jnp.int32)
     for r in range(count):
         position = lengths_ref[first + r]
         positions = jnp.where(at_row == r, position, positions)
-        mine = (rows == r) & (columns >= r * length) & (columns < r * length + position)
-        visible = visible | mine
+        limit = jnp.where(at_wide == r, position, limit)
+    offset = lax.broadcasted_iota(jnp.int32, wide, 1) - at_wide * length
+    visible = (offset >= 0) & (offset < limit)
     angles = positions.astype(jnp.float32) * frequency_ref[...]
     lane = lax.broadcasted_iota(jnp.int32, (count, HEAD_DIM), 1)
     cosine = jnp.cos(angles)
@@ -280,27 +280,32 @@
         value_new = columns_of(query_cols + key_cols + k * HEAD_DIM)
         value_new = value_new.astype(jnp.bfloat16).astype(jnp.float32)
         heads.append((queries, key_new, value_new))
+    raw = []
+    for k in range(KV_HEADS):
+        keys = cache[:, 0, k].reshape(count * length, HEAD_DIM)
+        raw.append(
+            lax.dot_general(
+                heads[k][0], keys, (((1,), (1,)), ((), ())), preferred_element_type=jnp.float32
+            )
+        )
+    mixed = []
     for k in range(KV_HEADS):
         queries, key_new, value_new = heads[k]
-        keys = cache[:, 0, k].reshape(count * length, HEAD_DIM)
-        values = cache[:, 1, k].reshape(count * length, HEAD_DIM)
-        scores = (
-            lax.dot_general(
-                queries, keys, (((1,), (1,)), ((), ())), preferred_element_type=jnp.float32
-            )
-            * scale
-        )
         tiled_key = jnp.concatenate([key_new] * GROUP, axis=0)
-        tiled_value = jnp.concatenate([value_new] * GROUP, axis=0)
         self_score = (
             jnp.sum(queries.astype(jnp.float32) * tiled_key, axis=1, keepdims=True) * scale
         )
-        top = jnp.max(jnp.where(visible, scores, -1e30), axis=1, keepdims=True)
-        top = jnp.maximum(top, self_score)
-        weights = jnp.where(visible, jnp.exp(scores - top), 0.0)
+        scores = jnp.where(visible, raw[k] * scale, -1e30)
+        top = jnp.maximum(jnp.max(scores, axis=1, keepdims=True), self_score)
+        weights = jnp.exp(scores - top)
         self_weight = jnp.exp(self_score - top)
         total = jnp.sum(weights, axis=1, keepdims=True) + self_weight
-        summed = jnp.dot(weights.astype(jnp.bfloat16), values, preferred_element_type=jnp.float32)
+        mixed.append((weights.astype(jnp.bfloat16), self_weight, total))
+    for k in range(KV_HEADS):
+        weights, self_weight, total = mixed[k]
+        values = cache[:, 1, k].reshape(count * length, HEAD_DIM)
+        tiled_value = jnp.concatenate([heads[k][2]] * GROUP, axis=0)
+        summed = jnp.dot(weights, values, preferred_element_type=jnp.float32)
         summed = summed + self_weight.astype(jnp.bfloat16).astype(jnp.float32) * tiled_value
         attended = summed / total
         for g in range(GROUP):

time: 163 us -> 161 us (0.988)
  waiting for transfers between devices: 65.8 us -> 63.8 us
    ppermute x1, waiting for transfers between devices: 65.8 us -> 63.8 us  [local(): lax.ppermute(rows, 'pipe', [(i, i - 1) for i in range(1, sections, 2)])]
where the time goes in v6:
time: 161 us; the launch traced here: 160 us
  waiting for transfers between devices  63.8 us (40%)
  blocking collectives  46.3 us (29%)
  Pallas kernels  31.4 us (20%)
  starting transfers between devices  15.7 us (10%)
    ppermute x1, waiting for transfers between devices, local(): lax.ppermute(rows, 'pipe', [(i, i - 1) for i in range(1, sections, 2)])  63.8 us
    all_to_all x4, blocking collectives, exchange(): return lax.all_to_all(blocks, axis, 0, 0, tiled=True)  46.3 us
    ppermute x4, starting transfers between devices, move(): lax.ppermute(array, 'pipe', [(i, i + 1) for i in range(2, sections, 2)])  11.6 us
    pallas_call x2, Pallas kernels, load(): pl.pallas_call(load_kernel, in_specs=[SMEM, VMEM] + [HBM] * len(arrays),...  9.19 us
    pallas_call x1, Pallas kernels, relay(): pl.pallas_call(relay_kernel, in_specs=[HBM], out_specs=pl.BlockSpec(memor...  6.95 us
    pallas_call x1, Pallas kernels, project_first(): pl.pallas_call(project_first_kernel, in_specs=[SMEM] + [HBM] * 4, out_spe...  5.46 us
    pallas_call x2, Pallas kernels, project(): pl.pallas_call(project_kernel, in_specs=[VMEM, VMEM, VMEM], out_specs=VME...  3.82 us
  transfers between devices with their start and end apart: 8, of which 1 were waited for; matrix products, arithmetic and copies ran while one was open for 1% of the time, Pallas kernels for 17%

profile of v6, /device:TPU:0, one launch (start us, length us, event | category | flops | bytes accessed | tf_op | source)
XLA Modules:
  0.0 160.3 jit_solution(13582095935041296776)
XLA Ops:
  0.7 4.8 %collective-permute-start.3 = (bf16[1024,5120]{1,0:T(8,128)(2,1)}, bf16[1024,5120]{1,0:T(8,128)(2,1)}, u32[]{:S(2)}, u32[]{:S(2)}) collective-permute-start(bf16[1024,5120]{1,0:T(8,128)(2,1)} %bitcast.9), channel_id=1, source_target_pairs={{16,24},{17,25},{18,26},{19,27},{20,28},{21,29},{22,30},{23,31}} | collective-permute-start | bytes 31457288 | tf_op jit(solution)/shard_map/ppermute | solution.py:550
  5.5 4.0 %collective-permute-start.5 = (bf16[4096,1024]{1,0:T(8,128)(2,1)}, bf16[4096,1024]{1,0:T(8,128)(2,1)}, u32[]{:S(2)}, u32[]{:S(2)}) collective-permute-start(bf16[4096,1024]{1,0:T(8,128)(2,1)} %bitcast.15), channel_id=1, source_target_pairs={{16,24},{17,25},{18,26},{19,27},{20,28},{21,29},{22,30},{23,31}} | collective-permute-start | bytes 25165832 | tf_op jit(solution)/shard_map/ppermute | solution.py:550
  9.5 2.1 %collective-permute-start.4 = (bf16[4,2,4,256,128]{4,3,2,1,0:T(8,128)(2,1)}, bf16[4,2,4,256,128]{4,3,2,1,0:T(8,128)(2,1)}, u32[]{:S(2)}, u32[]{:S(2)}) collective-permute-start(bf16[4,2,4,256,128]{4,3,2,1,0:T(8,128)(2,1)} %bitcast.31), channel_id=1, source_target_pairs={{16,24},{17,25},{18,26},{19,27},{20,28},{21,29},{22,30},{23,31}} | collective-permute-start | bytes 6291464 | tf_op jit(solution)/shard_map/ppermute | solution.py:550
  11.6 5.5 %project_first.1 = (bf16[8,4,5248]{2,1,0:T(4,128)(2,1)S(1)}, bf16[32,1024]{1,0:T(8,128)(2,1)S(1)}, bf16[4,2,4,256,128]{4,3,2,1,0:T(8,128)(2,1)S(1)}) custom-call(s32[3]{0:T(128)S(1)} %pad_add_fusion.place_ref, bf16[32,1024]{1,0:T(8,128)(2,1)} %stream_hbm.1, bf16[1,1024]{1,0:T(2,128)(2,1)} %gain_ref.1, bf16[1024,5120]{1,0:T(8,128)(2,1)} %bitcast.10, ...), custom_call_target="tpu_custom_call" | custom-call | tf_op jit(solution)/shard_map/project_first/pallas_call | solution.py:106
  17.2 30.6 %conditional.4 = (bf16[32,1024]{1,0:T(8,128)(2,1)S(1)}, bf16[8,1,1024]{2,1,0:T(2,128)(2,1)S(1)}) conditional(s32[]{:T(128)} %clamp.11, (bf16[8,4,5248]{2,1,0:T(4,128)(2,1)S(1)}, s32[32]{0:T(128)S(1)}, s32[3]{0:T(128)S(1)}, bf16[1,5120]{1,0:T(2,128)(2,1)S(1)}, f32[1,128]{1,0:T(1,128)S(1)}, /*index=5*/bf16[4,2,4,256,128]{4,3,2,1,0:T(8,128)(2,1)S(1)}, ...), branch_computations={%region_0.1_spmd, %region_1.2_spmd} | conditional | flops 17179869184 | bytes 28770370 | solution.py:559
  17.2 16.6 %all_to_all.49.parts_ref = bf16[8,4,5248]{2,1,0:T(4,128)(2,1)S(1)} all-to-all(bf16[8,4,5248]{2,1,0:T(4,128)(2,1)S(1)} %get-tuple-element.83), channel_id=1, replica_groups=mesh['pipe'=4,'mp'=8] {'mp'}, dimensions={0} | all-to-all | bytes 671744 | tf_op jit(solution)/shard_map/cond/branch_0_fun/all_to_all | solution.py:491
  33.8 1.4 attend.4
  35.2 10.9 %all_to_all.50.gathered_ref = bf16[8,4,4096]{2,1,0:T(4,128)(2,1)S(1)} all-to-all(bf16[8,4,4096]{2,1,0:T(4,128)(2,1)S(1)} %broadcast_in_dim.19), channel_id=1, replica_groups=mesh['pipe'=4,'mp'=8] {'mp'}, dimensions={0} | all-to-all | bytes 524288 | tf_op jit(solution)/shard_map/cond/branch_0_fun/all_to_all | solution.py:491
  46.1 1.5 combine.4
  47.7 1.3 collective-permute-start
  49.1 4.6 %load.2 = (bf16[1024,5120]{1,0:T(8,128)(2,1)S(1)}, bf16[4,2,4,256,128]{4,3,2,1,0:T(8,128)(2,1)S(1)}) custom-call(s32[1]{0:T(128)} %constant.35.clone.1.order_ref, bf16[32,1024]{1,0:T(8,128)(2,1)S(1)} %get-tuple-element.145.after_ref, bf16[1024,5120]{1,0:T(8,128)(2,1)} %bitcast.11, bf16[4,2,4,256,128]{4,3,2,1,0:T(8,128)(2,1)} %bitcast.33), custom_call_target="tpu_custom_call" | custom-call | flops 25165824 | bytes 25165824 | tf_op jit(solution)/shard_map/load/pallas_call | solution.py:144
  53.7 1.9 %project.2 = bf16[8,4,5248]{2,1,0:T(4,128)(2,1)S(1)} custom-call(bf16[32,1024]{1,0:T(8,128)(2,1)S(1)} %collective-permute-done.stream_ref, bf16[1,1024]{1,0:T(2,128)(2,1)S(1)} %copy-done.2, bf16[1024,5120]{1,0:T(8,128)(2,1)S(1)} %get-tuple-element.147.weight_ref), custom_call_target="tpu_custom_call" | custom-call | tf_op jit(solution)/shard_map/project/pallas_call | solution.py:199
  55.6 10.7 %conditional.5 = ((bf16[32,1024]{1,0:T(8,128)(2,1)S(1)}, bf16[8,1,1024]{2,1,0:T(2,128)(2,1)S(1)})) conditional(s32[]{:T(128)} %clamp.10, (bf16[32,1024]{1,0:T(8,128)(2,1)S(1)}, bf16[8,1,1024]{2,1,0:T(2,128)(2,1)S(1)}) %tuple.41, (bf16[8,4,5248]{2,1,0:T(4,128)(2,1)S(1)}, s32[32]{0:T(128)S(1)}, s32[3]{0:T(128)S(1)}, ...), branch_computations={%region_2.3_spmd, %region_3.4_spmd, %region_4.5_spmd} | conditional | flops 17179869184 | bytes 28753992 | solution.py:567
  56.2 0.8 reduce.1
  57.0 9.3 %all_to_all.53 = bf16[8,2,512]{2,1,0:T(2,128)(2,1)S(1)} all-to-all(bf16[8,2,512]{2,1,0:T(2,128)(2,1)S(1)} %reshape.25), channel_id=1, replica_groups=mesh['pipe'=4,'mp'=8] {'mp'}, dimensions={0} | all-to-all | bytes 32768 | tf_op jit(solution)/shard_map/cond/branch_2_fun/all_to_all | solution.py:491
  66.3 0.7 collective-permute-start.1
  67.7 7.0 %relay.1 = bf16[4096,1024]{1,0:T(8,128)(2,1)} custom-call(bf16[4096,1024]{1,0:T(8,128)(2,1)} %collective-permute-done.5.source_ref), custom_call_target="tpu_custom_call" | custom-call | flops 16777216 | bytes 16777216 | tf_op jit(solution)/shard_map/relay/pallas_call | solution.py:178
  74.7 4.6 %load.3 = (bf16[1024,5120]{1,0:T(8,128)(2,1)S(1)}, bf16[4,2,4,256,128]{4,3,2,1,0:T(8,128)(2,1)S(1)}) custom-call(s32[1]{0:T(128)} %constant.36.clone.1.order_ref, bf16[32,1024]{1,0:T(8,128)(2,1)S(1)} %get-tuple-element.149.after_ref, bf16[1024,5120]{1,0:T(8,128)(2,1)} %collective-permute-done.3.refs_0_, ...), custom_call_target="tpu_custom_call" | custom-call | flops 25165824 | bytes 25165824 | tf_op jit(solution)/shard_map/load/pallas_call | solution.py:144
  79.3 1.9 %project.3 = bf16[8,4,5248]{2,1,0:T(4,128)(2,1)S(1)} custom-call(bf16[32,1024]{1,0:T(8,128)(2,1)S(1)} %collective-permute-done.1.stream_ref, bf16[1,6144]{1,0:T(2,128)(2,1)S(1)} %collective-permute-done.2.gain_ref, bf16[1024,5120]{1,0:T(8,128)(2,1)S(1)} %get-tuple-element.150.weight_ref), custom_call_target="tpu_custom_call" | custom-call | tf_op jit(solution)/shard_map/project/pallas_call | solution.py:199
  82.3 1.6 collective-permute-start.7
  84.0 63.8 %collective-permute-done.7.over_ref = bf16[8,32,1024]{2,1,0:T(8,128)(2,1)S(1)} collective-permute-done((bf16[8,32,1024]{2,1,0:T(8,128)(2,1)S(1)}, bf16[8,32,1024]{2,1,0:T(8,128)(2,1)S(1)}, u32[]{:S(2)}, u32[]{:S(2)}) %collective-permute-start.7) | collective-permute-done | bytes 524320 | tf_op jit(solution)/shard_map/ppermute | solution.py:592
  147.9 2.0 %final_logits.1 = (f32[32,384]{1,0:T(8,128)S(1)}, f32[1,128]{1,0:T(1,128)S(1)}) custom-call(s32[32]{0:T(128)S(1)} %copy-done, s32[32]{0:T(128)S(1)} %copy-done.1, s32[3]{0:T(128)S(1)} %pad_add_fusion.place_ref, bf16[8,32,1024]{2,1,0:T(8,128)(2,1)S(1)} %get-tuple-element.169.rows_ref, bf16[8,32,1024]{2,1,0:T(8,128)(2,1)S(1)} %collective-permute-done.7.over_ref, ...), custom_call_target="tpu_custom_call" | custom-call | tf_op jit(solution)/shard_map/final_logits/pallas_call | solution.py:440
  149.9 9.6 %all_to_all.59 = f32[32,1,128]{2,1,0:T(1,128)S(1)} all-to-all(f32[32,1,128]{2,1,0:T(1,128)S(1)} %broadcast_in_dim.46), channel_id=1, replica_groups=mesh['pipe'=4,'mp'=8] {'pipe','mp'}, dimensions={0} | all-to-all | bytes 32768 | tf_op jit(solution)/shard_map/all_to_all | solution.py:491
  159.6 0.8 finish.1
  (47 shorter events, 2.8 us)
Async XLA Ops:
  0.6 16.5 %copy-start.6 = (f32[1,128]{1,0:T(1,128)S(1)}, f32[1,128]{1,0:T(1,128)}, u32[]{:S(2)}) copy-start(f32[1,128]{1,0:T(1,128)} %constant.37.clone) | copy-start | bytes 1540
  0.6 16.5 %copy-start.4 = (bf16[1024]{0:T(1024)(128)(2,1)S(1)}, bf16[1024]{0:T(1024)(128)(2,1)}, u32[]{:S(2)}) copy-start(bf16[1024]{0:T(1024)(128)(2,1)} %param.30) | copy-start | bytes 6148
  0.7 16.5 %copy-start.5 = (s32[32]{0:T(128)S(1)}, s32[32]{0:T(128)}, u32[]{:S(2)}) copy-start(s32[32]{0:T(128)} %param.22) | copy-start | bytes 388
  0.7 16.5 %copy-start.3 = (bf16[1,5120]{1,0:T(2,128)(2,1)S(1)}, bf16[1,5120]{1,0:T(2,128)(2,1)}, u32[]{:S(2)}) copy-start(bf16[1,5120]{1,0:T(2,128)(2,1)} %param.27) | copy-start | bytes 30724
  0.7 74.0 %collective-permute-start.3 = (bf16[1024,5120]{1,0:T(8,128)(2,1)}, bf16[1024,5120]{1,0:T(8,128)(2,1)}, u32[]{:S(2)}, u32[]{:S(2)}) collective-permute-start(bf16[1024,5120]{1,0:T(8,128)(2,1)} %bitcast.9), channel_id=1, source_target_pairs={{16,24},{17,25},{18,26},{19,27},{20,28},{21,29},{22,30},{23,31}} | collective-permute-start | bytes 31457288 | tf_op jit(solution)/shard_map/ppermute | solution.py:550
  5.5 62.2 %collective-permute-start.5 = (bf16[4096,1024]{1,0:T(8,128)(2,1)}, bf16[4096,1024]{1,0:T(8,128)(2,1)}, u32[]{:S(2)}, u32[]{:S(2)}) collective-permute-start(bf16[4096,1024]{1,0:T(8,128)(2,1)} %bitcast.15), channel_id=1, source_target_pairs={{16,24},{17,25},{18,26},{19,27},{20,28},{21,29},{22,30},{23,31}} | collective-permute-start | bytes 25165832 | tf_op jit(solution)/shard_map/ppermute | solution.py:550
  9.5 65.2 %collective-permute-start.4 = (bf16[4,2,4,256,128]{4,3,2,1,0:T(8,128)(2,1)}, bf16[4,2,4,256,128]{4,3,2,1,0:T(8,128)(2,1)}, u32[]{:S(2)}, u32[]{:S(2)}) collective-permute-start(bf16[4,2,4,256,128]{4,3,2,1,0:T(8,128)(2,1)} %bitcast.31), channel_id=1, source_target_pairs={{16,24},{17,25},{18,26},{19,27},{20,28},{21,29},{22,30},{23,31}} | collective-permute-start | bytes 6291464 | tf_op jit(solution)/shard_map/ppermute | solution.py:550
  17.2 29.0 %slice-start.3 = ((s8[8388608]{0:T(1024)(128)(4,1)}), s8[4194304]{0:T(1024)(128)(4,1)S(1)}, s32[]{:S(2)}) async-start(s8[8388608]{0:T(1024)(128)(4,1)} %bitcast.19), calls=%async_computation.15 | async-start | bytes 8388608 | tf_op jit(solution)/shard_map/cond
  33.8 12.4 %slice-start.4 = ((s8[8388608]{0:T(1024)(128)(4,1)}), s8[4194304]{0:T(1024)(128)(4,1)S(1)}, s32[]{:S(2)}) async-start(s8[8388608]{0:T(1024)(128)(4,1)} %bitcast.19), calls=%async_computation.16 | async-start | bytes 8388608 | tf_op jit(solution)/shard_map/cond
  47.7 5.9 %copy-start.2 = (bf16[1,1024]{1,0:T(2,128)(2,1)S(1)}, bf16[1,1024]{1,0:T(2,128)(2,1)}, u32[]{:S(2)}) copy-start(bf16[1,1024]{1,0:T(2,128)(2,1)} %gain_ref.1) | copy-start | bytes 6148
  47.7 5.9 %collective-permute-start = (bf16[32,1024]{1,0:T(8,128)(2,1)S(1)}, bf16[32,1024]{1,0:T(8,128)(2,1)S(1)}, u32[]{:S(2)}, u32[]{:S(2)}) collective-permute-start(bf16[32,1024]{1,0:T(8,128)(2,1)S(1)} %get-tuple-element.145.after_ref), channel_id=1, source_target_pairs={{0,8},{1,9},{2,10},{3,11},{4,12},{5,13},{6,14},{7,15}} | collective-permute-start | bytes 196616 | tf_op jit(solution)/shard_map/ppermute | solution.py:564
  66.3 13.0 %collective-permute-start.1 = (bf16[32,1024]{1,0:T(8,128)(2,1)S(1)}, bf16[32,1024]{1,0:T(8,128)(2,1)S(1)}, u32[]{:S(2)}, u32[]{:S(2)}) collective-permute-start(bf16[32,1024]{1,0:T(8,128)(2,1)S(1)} %get-tuple-element.149.after_ref), channel_id=1, source_target_pairs={{8,24},{9,25},{10,26},{11,27},{12,28},{13,29},{14,30},{15,31}} | collective-permute-start | bytes 196616 | tf_op jit(solution)/shard_map/ppermute | solution.py:574
  67.0 12.3 %collective-permute-start.2 = (bf16[1,6144]{1,0:T(2,128)(2,1)S(1)}, bf16[1,6144]{1,0:T(2,128)(2,1)S(1)}, u32[]{:S(2)}, u32[]{:S(2)}) collective-permute-start(bf16[1,6144]{1,0:T(2,128)(2,1)S(1)} %pad_maximum_fusion), channel_id=1, source_target_pairs={{16,24},{17,25},{18,26},{19,27},{20,28},{21,29},{22,30},{23,31}} | collective-permute-start | bytes 36872 | tf_op jit(solution)/shard_map/ppermute | solution.py:550
  81.5 0.7 collective-permute-start.6
  82.3 65.6 %slice-start.11 = ((s8[6291456]{0:T(1024)(128)(4,1)}), s8[2097152]{0:T(1024)(128)(4,1)S(1)}, s32[]{:S(2)}) async-start(s8[6291456]{0:T(1024)(128)(4,1)} %bitcast.27), calls=%async_computation.23 | async-start | bytes 4194304
  82.3 65.6 %slice-start.12 = ((s8[6291456]{0:T(1024)(128)(4,1)}), s8[4194304]{0:T(1024)(128)(4,1)S(1)}, s32[]{:S(2)}) async-start(s8[6291456]{0:T(1024)(128)(4,1)} %bitcast.27), calls=%async_computation.24 | async-start | bytes 8388608
  82.3 65.6 %copy-start = (s32[32]{0:T(128)S(1)}, s32[32]{0:T(128)}, u32[]{:S(2)}) copy-start(s32[32]{0:T(128)} %assign_ref.1) | copy-start | bytes 388
  82.3 65.6 %copy-start.1 = (s32[32]{0:T(128)S(1)}, s32[32]{0:T(128)}, u32[]{:S(2)}) copy-start(s32[32]{0:T(128)} %tokens_ref.1) | copy-start | bytes 388
  82.3 65.6 %collective-permute-start.7 = (bf16[8,32,1024]{2,1,0:T(8,128)(2,1)S(1)}, bf16[8,32,1024]{2,1,0:T(8,128)(2,1)S(1)}, u32[]{:S(2)}, u32[]{:S(2)}) collective-permute-start(bf16[8,32,1024]{2,1,0:T(8,128)(2,1)S(1)} %get-tuple-element.169.rows_ref), channel_id=1, source_target_pairs={{8,0},{24,16},{9,1},{25,17},{10,2},{26,18},{11,3},{27,19},{12,4},{... | collective-permute-start | bytes 1572872 | tf_op jit(solution)/shard_map/ppermute | solution.py:592
